TPU v7x, 512 devices: a 4x2x32 block of a 4x8x32 slice. The times are simulated.
512 devices in a mesh: pert: 2 (over y), ga: 32 (over z), band: 8 (over x, core).
Axes of the slice: x: 4, y: 2, z: 32, core: 2. Of those that a mesh axis runs over, the one named last changes fastest.
The devices are a block of a 4x8x32 slice.
Arguments:
- psi: float32 [2, 8, 131072], P(None, 'band', 'ga'), may hold values from -6 to 6
- potential: float32 [256, 128, 128], P('pert', 'ga'), parts along dimension 0, may hold values from 1 to 3
- miller: int32 [131072], replicated, may hold values from 0 to 2097151, as said below
- occupied: int32 [8], replicated, may hold values 0 or 1
Outputs:
- projected: float32 [2, 16, 131072], P(None, ('pert', 'band'), 'ga'), parts along dimension 1
There are 2 independent parts, one for each index of `pert`. A program takes and returns all parts, laid end to end along the dimension named above; an argument that names none is the same for every part. Nothing has to cross between parts.
Inputs may be any that keep to these rules, and one draw needn't show every extreme that they name: `miller`: entry k is the flat index a 128^2 + b * 128 + c of coefficient k, with Fourier indices a, b, c in 0..127 taken modulo 128; the entries are distinct; each of a, b, c, read as a signed index in -64..128/2-1, lies in -32..128/4-1; the j-th block of 4096 entries holds only points whose signed a plus 128/4 is congruent to j modulo 131072/4096.
All inputs are finite; a program needn't handle non-finite values.
Results may differ from a plain program's by a relative error of at most 0.00013.
Values sent between devices are 32-bit elements; how exact they have to be, the bound alone decides.
No kernel may reach another device: no remote copies, remote signals or barrier semaphores. Data moves between devices by JAX's collectives and lax.ppermute only.
A program may use at most 64 MiB of HBM per device.

v0:
```python
import jax
import jax.numpy as jnp
from jax import lax
from jax.sharding import PartitionSpec as P

NPW = 131072


highest = lax.Precision.HIGHEST


def sent_to_all(x, axis):
    copies = jnp.broadcast_to(x, (lax.axis_size(axis), *x.shape))
    return lax.all_to_all(copies, axis, split_axis=0, concat_axis=0, tiled=True)


def in_order(blocks, dim):
    blocks = jnp.moveaxis(blocks, 0, dim)
    lengths = blocks.shape
    return blocks.reshape(*lengths[:dim], lengths[dim] * lengths[dim + 1], *lengths[dim + 2 :])


def gathered_copies(x, axis, dim):
    blocks = sent_to_all(x, axis)
    return in_order(blocks, dim)


def taken_together(x, axis):
    return sent_to_all(x, axis).sum(axis=0)


def in_one(arrays, axis):
    line, at, done = (jnp.concatenate([a.reshape(-1) for a in arrays]), 0, [])
    subtotal = taken_together(line, axis)
    for a in arrays:
        done.append(subtotal[at : at + a.size].reshape(a.shape))
        at += a.size
    return tuple(done)


def phases(first_index, second_index, direction, length):
    turns = first_index[:, None] * second_index[None, :] % length
    angle = direction * 2.0 * jnp.pi / length * turns.astype(jnp.float32)
    return (jnp.cos(angle), jnp.sin(angle))


def contract(pattern, real_part, imag_part, twiddle):
    cosine, sine_part = twiddle
    out_real = jnp.einsum(pattern, real_part, cosine, precision=highest) - jnp.einsum(
        pattern, imag_part, sine_part, precision=highest
    )
    out_imag = jnp.einsum(pattern, real_part, sine_part, precision=highest) + jnp.einsum(
        pattern, imag_part, cosine, precision=highest
    )
    return (out_real, out_imag)


def inner_products(left_real, left_imag, right_real, right_imag):
    over_real = jnp.einsum("mk,nk->mn", left_real, right_real, precision=highest) + jnp.einsum(
        "mk,nk->mn", left_imag, right_imag, precision=highest
    )
    over_imag = jnp.einsum("mk,nk->mn", left_real, right_imag, precision=highest) - jnp.einsum(
        "mk,nk->mn", left_imag, right_real, precision=highest
    )
    return (over_real, over_imag)


def subtract(applied_real, applied_imag, basis_real, basis_imag, weight_real, weight_imag):
    proj_real = jnp.einsum("mn,mk->nk", weight_real, basis_real, precision=highest) - jnp.einsum(
        "mn,mk->nk", weight_imag, basis_imag, precision=highest
    )
    proj_imag = jnp.einsum("mn,mk->nk", weight_imag, basis_real, precision=highest) + jnp.einsum(
        "mn,mk->nk", weight_real, basis_imag, precision=highest
    )
    return (applied_real - proj_real, applied_imag - proj_imag)


def shards(psi, potential, miller, occupied):
    grid_size = potential.shape[0]
    owners = lax.axis_size("ga")
    quarter = grid_size // 4
    per_shard = psi.shape[2]
    band_count = psi.shape[1]
    owner_index = lax.axis_index("ga")
    kept_rows = grid_size // 2
    kept_planes = grid_size // (2 * owners)
    full_index = jnp.arange(grid_size, dtype=jnp.int32)
    kept_index = (jnp.arange(kept_rows, dtype=jnp.int32) + grid_size - quarter) % grid_size
    inverse_rows = phases(kept_index, full_index, 1.0, grid_size)
    forward_rows = phases(full_index, kept_index, -1.0, grid_size)
    slot_index = jnp.arange(owners * kept_planes, dtype=jnp.int32)
    plane_index = (
        slot_index // kept_planes + owners * (slot_index % kept_planes) + grid_size - quarter
    ) % grid_size
    inverse_planes = phases(plane_index, full_index, 1.0, grid_size)
    forward_planes = phases(full_index, plane_index, -1.0, grid_size)
    local_points = lax.dynamic_slice_in_dim(miller, owner_index * per_shard, per_shard)
    index_a = local_points // (grid_size * grid_size)
    index_b = local_points // grid_size % grid_size
    index_c = local_points % grid_size
    plane_pos = (index_a + quarter) % grid_size
    position = (plane_pos // owners * kept_rows + (index_b + quarter) % grid_size) * kept_rows + (
        index_c + quarter
    ) % grid_size
    slab_size = kept_planes * kept_rows * kept_rows
    real_part = jnp.zeros((band_count, slab_size), jnp.float32).at[:, position].set(psi[0])
    imag_part = jnp.zeros((band_count, slab_size), jnp.float32).at[:, position].set(psi[1])
    real_part = real_part.reshape(band_count, kept_planes, kept_rows, kept_rows)
    imag_part = imag_part.reshape(band_count, kept_planes, kept_rows, kept_rows)
    real_part, imag_part = contract("ntbc,by->ntyc", real_part, imag_part, inverse_rows)
    pieces = (
        lax.all_to_all(real_part, "ga", split_axis=2, concat_axis=1, tiled=True),
        lax.all_to_all(imag_part, "ga", split_axis=2, concat_axis=1, tiled=True),
    )
    wide_real, wide_imag = contract("nsyc,cz->nsyz", pieces[0], pieces[1], inverse_rows)
    pieces = (wide_real, wide_imag)
    wave_real, wave_imag = contract("nsyz,sx->nxyz", pieces[0], pieces[1], inverse_planes)
    wave_real = wave_real * potential
    wave_imag = wave_imag * potential
    wide_real, wide_imag = contract("nxyz,xs->nsyz", wave_real, wave_imag, forward_planes)
    narrow = contract("nsyz,zc->nsyc", wide_real, wide_imag, forward_rows)
    real_part = lax.all_to_all(narrow[0], "ga", split_axis=1, concat_axis=2, tiled=True)
    imag_part = lax.all_to_all(narrow[1], "ga", split_axis=1, concat_axis=2, tiled=True)
    real_part, imag_part = contract("ntyc,yb->ntbc", real_part, imag_part, forward_rows)
    inverse_volume = 1.0 / grid_size**3
    applied_real = real_part.reshape(band_count, slab_size)[:, position] * inverse_volume
    applied_imag = imag_part.reshape(band_count, slab_size)[:, position] * inverse_volume
    weights = occupied.astype(jnp.float32)[:, None]
    all_psi = gathered_copies(psi, "band", 1)
    basis_real = all_psi[0]
    basis_imag = all_psi[1]
    over_real, over_imag = inner_products(basis_real, basis_imag, applied_real, applied_imag)
    over_real, over_imag = in_one((over_real, over_imag), "ga")
    weight_real = weights * (over_real / NPW)
    weight_imag = weights * (over_imag / NPW)
    left_real, left_imag = subtract(
        applied_real, applied_imag, basis_real, basis_imag, weight_real, weight_imag
    )
    return jnp.stack([left_real, left_imag])


def solution(mesh):
    in_specs = (P(None, "band", "ga"), P("pert", "ga", None), P(), P())
    out_specs = P(None, ("pert", "band"), "ga")
    return jax.shard_map(shards, mesh=mesh, in_specs=in_specs, out_specs=out_specs, check_vma=False)
```

profile of v0, /device:TPU:40, one launch (start us, length us, event | category | flops | bytes accessed | tf_op | source)
XLA Modules:
  0.0 286.4 jit_solution(11097856054643396616)
XLA Ops:
  0.0 0.7 fusion.243
  0.7 0.8 broadcast_clamp_fusion
  1.5 15.5 %scatter_custom_fusion.1 = f32[8192]{0:T(1024)S(1)} fusion(s32[4096]{0:T(1024)S(1)} %get-tuple-element.6, f32[4096]{0:T(1024)S(1)} %bitcast.239, f32[]{:T(128)} %constant.167.clone.1), kind=kCustom, calls=%fused_computation.154 | custom fusion | bytes 32772 | tf_op jit(solution)/shard_map/scatter | solution.py:107
  17.3 15.5 %scatter_custom_fusion = f32[8192]{0:T(1024)S(1)} fusion(s32[4096]{0:T(1024)S(1)} %get-tuple-element.6, f32[4096]{0:T(1024)S(1)} %bitcast.238, f32[]{:T(128)} %constant.167.clone.1), kind=kCustom, calls=%fused_computation.156 | custom fusion | bytes 32772 | tf_op jit(solution)/shard_map/scatter | solution.py:106
  33.0 0.4 fusion.111
  33.4 0.4 fusion.105
  33.9 0.8 reshape.406
  34.7 45.8 %all-to-all-start = ((f32[32,1,512]{2,1,0:T(1,128)}), f32[32,1,512]{2,1,0:T(1,128)S(1)}, u32[]{:S(2)}, u32[]{:S(2)}) async-start(f32[32,1,512]{2,1,0:T(1,128)} %reshape.406), calls=%async_computation | async-start | bytes 131072 | tf_op jit(solution)/shard_map/all_to_all | solution.py:112
  80.5 0.4 fusion.109
  80.9 0.4 fusion.102
  81.4 0.8 reshape.408
  82.2 23.5 %all-to-all-done = f32[32,1,512]{2,1,0:T(1,128)S(1)} async-done(((f32[32,1,512]{2,1,0:T(1,128)}), f32[32,1,512]{2,1,0:T(1,128)S(1)}, u32[]{:S(2)}, u32[]{:S(2)}) %all-to-all-start) | async-done | bytes 65568 | tf_op jit(solution)/shard_map/all_to_all | solution.py:112
  105.7 4.7 %all-to-all-start.1 = ((f32[32,1,512]{2,1,0:T(1,128)}), f32[32,1,512]{2,1,0:T(1,128)S(1)}, u32[]{:S(2)}, u32[]{:S(2)}) async-start(f32[32,1,512]{2,1,0:T(1,128)} %reshape.408), calls=%async_computation.1 | async-start | bytes 131072 | tf_op jit(solution)/shard_map/all_to_all | solution.py:113
  110.5 0.5 broadcast.581
  111.0 0.8 reduce.1
  111.8 0.1 reshape.407
  112.1 0.4 fusion.56
  112.5 0.4 fusion.52
  113.0 21.2 %all-to-all-done.1 = f32[32,1,512]{2,1,0:T(1,128)S(1)} async-done(((f32[32,1,512]{2,1,0:T(1,128)}), f32[32,1,512]{2,1,0:T(1,128)S(1)}, u32[]{:S(2)}, u32[]{:S(2)}) %all-to-all-start.1) | async-done | bytes 65568 | tf_op jit(solution)/shard_map/all_to_all | solution.py:113
  134.2 0.9 broadcast_in_dim.7
  135.1 4.6 %all-to-all-start.4 = ((f32[8,2,1,4096]{3,2,1,0:T(1,128)}), f32[8,2,1,4096]{3,2,1,0:T(1,128)S(1)}, u32[]{:S(2)}, u32[]{:S(2)}) async-start(f32[8,2,1,4096]{3,2,1,0:T(1,128)} %broadcast_in_dim.7), calls=%async_computation.4 | async-start | bytes 524288 | tf_op jit(solution)/shard_map/all_to_all | solution.py:14
  139.7 0.8 reduce.2
  140.5 0.1 reshape.409
  140.7 0.5 convolution_subtract_fusion.2
  141.2 0.6 fusion.49
  141.8 0.6 fusion.59
  142.4 0.4 convolution_add_fusion.2
  142.9 0.5 copy-done
  143.4 0.6 fusion.1
  144.0 0.5 fusion.46
  144.5 0.5 fusion.62
  144.9 0.6 fusion
  145.6 0.5 convolution_add_fusion.3
  146.0 0.5 convolution_subtract_fusion.3
  146.5 0.4 fusion.68
  147.0 0.5 fusion.3
  147.5 0.8 reshape.410
  148.3 4.8 %all-to-all-start.2 = ((f32[32,1,512]{2,1,0:T(1,128)}), f32[32,1,512]{2,1,0:T(1,128)S(1)}, u32[]{:S(2)}, u32[]{:S(2)}) async-start(f32[32,1,512]{2,1,0:T(1,128)} %reshape.410), calls=%async_computation.2 | async-start | bytes 131072 | tf_op jit(solution)/shard_map/all_to_all | solution.py:122
  153.0 0.5 fusion.43
  153.5 0.5 fusion.2
  154.1 0.8 reshape.412
  154.8 24.3 %all-to-all-done.2 = f32[32,1,512]{2,1,0:T(1,128)S(1)} async-done(((f32[32,1,512]{2,1,0:T(1,128)}), f32[32,1,512]{2,1,0:T(1,128)S(1)}, u32[]{:S(2)}, u32[]{:S(2)}) %all-to-all-start.2) | async-done | bytes 65568 | tf_op jit(solution)/shard_map/all_to_all | solution.py:122
  179.1 4.8 %all-to-all-start.3 = ((f32[32,1,512]{2,1,0:T(1,128)}), f32[32,1,512]{2,1,0:T(1,128)S(1)}, u32[]{:S(2)}, u32[]{:S(2)}) async-start(f32[32,1,512]{2,1,0:T(1,128)} %reshape.412), calls=%async_computation.3 | async-start | bytes 131072 | tf_op jit(solution)/shard_map/all_to_all | solution.py:123
  183.9 0.8 reduce.3
  184.8 0.1 reshape.411
  184.9 0.4 fusion.40
  185.3 0.4 fusion.66
  185.7 23.0 %all-to-all-done.3 = f32[32,1,512]{2,1,0:T(1,128)S(1)} async-done(((f32[32,1,512]{2,1,0:T(1,128)}), f32[32,1,512]{2,1,0:T(1,128)S(1)}, u32[]{:S(2)}, u32[]{:S(2)}) %all-to-all-start.3) | async-done | bytes 65568 | tf_op jit(solution)/shard_map/all_to_all | solution.py:123
  208.7 0.8 reduce.4
  209.6 0.4 fusion.4
  210.1 23.0 %gather_fusion.1 = f32[4096]{0:T(1024)S(1)} fusion(f32[8192]{0:T(1024)S(1)} %reshape.324, s32[4096]{0:T(1024)S(1)} %get-tuple-element.5), kind=kCustom, calls=%fused_computation.1 | custom fusion | bytes 49152 | tf_op jit(solution)/shard_map/gather | solution.py:127
  233.1 0.4 fusion.5
  233.6 23.0 %gather_fusion = f32[4096]{0:T(1024)S(1)} fusion(f32[8192]{0:T(1024)S(1)} %reshape.314, s32[4096]{0:T(1024)S(1)} %get-tuple-element.5), kind=kCustom, calls=%fused_computation | custom fusion | bytes 49152 | tf_op jit(solution)/shard_map/gather | solution.py:126
  256.6 0.4 convolution_bitcast_fusion.2
  257.0 0.4 convolution_bitcast_fusion
  257.5 0.5 fusion.6
  257.9 0.4 fusion.7
  258.5 25.3 %all_to_all.71 = f32[32,1,16]{2,1,0:T(1,128)S(1)} all-to-all(f32[32,1,16]{2,1,0:T(1,128)S(1)} %broadcast_in_dim.8), channel_id=1, replica_groups=mesh['pert'=2,'ga'=32,'band'=8] {'ga'}, dimensions={0} | all-to-all | bytes 4096 | tf_op jit(solution)/shard_map/all_to_all | solution.py:14
  283.8 0.6 copy-done.2
  284.4 0.3 fusion.10
  284.8 0.3 fusion.16
  285.1 0.3 fusion.8
  285.4 0.3 fusion.14
  285.8 0.6 pad_maximum_fusion
  (35 shorter events, 1.6 us)
Async XLA Ops:
  34.7 71.0 %all-to-all-start = ((f32[32,1,512]{2,1,0:T(1,128)}), f32[32,1,512]{2,1,0:T(1,128)S(1)}, u32[]{:S(2)}, u32[]{:S(2)}) async-start(f32[32,1,512]{2,1,0:T(1,128)} %reshape.406), calls=%async_computation | async-start | bytes 131072 | tf_op jit(solution)/shard_map/all_to_all | solution.py:112
  82.2 28.3 %copy-start.1 = (f32[2,1,4096]{2,1,0:T(1,128)S(1)}, f32[2,1,4096]{2,1,0:T(1,128)}, u32[]{:S(2)}) copy-start(f32[2,1,4096]{2,1,0:T(1,128)} %param.4) | copy-start | bytes 98308
  105.7 28.5 %all-to-all-start.1 = ((f32[32,1,512]{2,1,0:T(1,128)}), f32[32,1,512]{2,1,0:T(1,128)S(1)}, u32[]{:S(2)}, u32[]{:S(2)}) async-start(f32[32,1,512]{2,1,0:T(1,128)} %reshape.408), calls=%async_computation.1 | async-start | bytes 131072 | tf_op jit(solution)/shard_map/all_to_all | solution.py:113
  135.1 13.2 %all-to-all-start.4 = ((f32[8,2,1,4096]{3,2,1,0:T(1,128)}), f32[8,2,1,4096]{3,2,1,0:T(1,128)S(1)}, u32[]{:S(2)}, u32[]{:S(2)}) async-start(f32[8,2,1,4096]{3,2,1,0:T(1,128)} %broadcast_in_dim.7), calls=%async_computation.4 | async-start | bytes 524288 | tf_op jit(solution)/shard_map/all_to_all | solution.py:14
  142.4 1.0 copy-start
  148.3 30.9 %all-to-all-start.2 = ((f32[32,1,512]{2,1,0:T(1,128)}), f32[32,1,512]{2,1,0:T(1,128)S(1)}, u32[]{:S(2)}, u32[]{:S(2)}) async-start(f32[32,1,512]{2,1,0:T(1,128)} %reshape.410), calls=%async_computation.2 | async-start | bytes 131072 | tf_op jit(solution)/shard_map/all_to_all | solution.py:122
  179.1 29.5 %all-to-all-start.3 = ((f32[32,1,512]{2,1,0:T(1,128)}), f32[32,1,512]{2,1,0:T(1,128)S(1)}, u32[]{:S(2)}, u32[]{:S(2)}) async-start(f32[32,1,512]{2,1,0:T(1,128)} %reshape.412), calls=%async_computation.3 | async-start | bytes 131072 | tf_op jit(solution)/shard_map/all_to_all | solution.py:123
  283.8 0.7 copy-start.2
where the time goes:
time: 287 us; the launch traced here: 286 us
  waiting for transfers between devices  92 us (32%)
  local copies, waits for them, and re-layouts  85.1 us (30%)
  starting transfers between devices  64.6 us (23%)
  blocking collectives  25.3 us (9%)
  matrix products  14 us (5%)
  other arithmetic  4.85 us (2%)
    all_to_all x1, starting transfers between devices, shards(): lax.all_to_all(real_part, 'ga', split_axis=2, concat_axis=1, tiled=True)  45.8 us
    all_to_all x1, blocking collectives, sent_to_all(): return lax.all_to_all(copies, axis, split_axis=0, concat_axis=0, tiled=True)  25.3 us
    all_to_all x1, waiting for transfers between devices, shards(): lax.all_to_all(narrow[0], 'ga', split_axis=1, concat_axis=2, tiled=True)  24.3 us
    all_to_all x1, waiting for transfers between devices, shards(): lax.all_to_all(real_part, 'ga', split_axis=2, concat_axis=1, tiled=True)  23.5 us
    gather x1, local copies, waits for them, and re-layouts, shards(): imag_part.reshape(band_count, slab_size)[:, position] * inverse_volume  23 us
    gather x1, local copies, waits for them, and re-layouts, shards(): real_part.reshape(band_count, slab_size)[:, position] * inverse_volume  23 us
    all_to_all x1, waiting for transfers between devices, shards(): lax.all_to_all(narrow[1], 'ga', split_axis=1, concat_axis=2, tiled=True)  23 us
    all_to_all x1, waiting for transfers between devices, shards(): lax.all_to_all(imag_part, 'ga', split_axis=2, concat_axis=1, tiled=True)  21.2 us
  transfers between devices with their start and end apart: 5, of which 4 were waited for; matrix products, arithmetic and copies ran while one was open for 5% of the time, Pallas kernels for 0%

commit v1 on v0

v1 whole, which is shorter than its diff:
```python
import functools

import jax
import jax.numpy as jnp
import numpy as np
from jax import lax
from jax.experimental import pallas as pl
from jax.experimental.pallas import tpu as pltpu
from jax.sharding import PartitionSpec as P

highest = lax.Precision.HIGHEST
INTERPRET = False


def dot(a, b):
    return jnp.dot(a, b, precision=highest, preferred_element_type=jnp.float32)


def thirds(x):
    high = x.astype(jnp.bfloat16)
    rest = x - high.astype(jnp.float32)
    mid = rest.astype(jnp.bfloat16)
    low = (rest - mid.astype(jnp.float32)).astype(jnp.bfloat16)
    return high, mid, low


def turned(x):
    half = x.shape[1] // 2
    return jnp.concatenate([-x[:, half:], x[:, :half]], axis=1)


def tables(size, owners):
    kept, per = size // 2, size // (2 * owners)
    signed = np.arange(kept) - size // 4
    full = np.arange(size)
    angle = 2.0 * np.pi / size * (full[:, None] * signed[None, :] % size)
    cosine, sine = np.cos(angle), np.sin(angle)
    rows = [np.einsum("yb,tu->ytub", part, np.eye(per)).reshape(size * per, per * kept) for part in (cosine, sine)]
    along_y = np.concatenate(rows, axis=1)
    along_z = np.block([[cosine.T, sine.T], [-sine.T, cosine.T]])
    along_x = np.block([[cosine, -sine], [sine, cosine]])
    own = size // owners
    back = [part.reshape(owners, own * per, per * kept).transpose(2, 1, 0).reshape(per * kept, size * per) for part in rows]
    back_y = np.concatenate([back[0], -back[1]], axis=1)
    as32 = lambda x: np.asarray(x, np.float32)
    return as32(along_y), as32(along_z), as32(along_x), as32(along_x.T), as32(along_z.T / size**3), as32(back_y)


def places(points, size, owners):
    quarter = size // 4
    plane = (points // (size * size) + quarter) % size
    row = (points // size + quarter) % size
    column = (points + quarter) % size
    return plane // owners * (size // 2) + row, column


def picks(index, count):
    return lax.broadcasted_iota(jnp.int32, (count, index.shape[1]), 0) == index


def spread_kernel(owner_ref, psi_ref, points_ref, along_ref, out_ref, *, size, owners):
    del owner_ref
    line, column = places(points_ref[0], size, owners)
    lines = along_ref.shape[1] // 2
    at_line = picks(line, lines).astype(jnp.bfloat16)
    at_column = picks(column, size // 2)
    zero = jnp.zeros((), jnp.bfloat16)
    total = None
    for real, imag in zip(thirds(psi_ref[0]), thirds(psi_ref[1])):
        spread = jnp.concatenate([jnp.where(at_column, real, zero), jnp.where(at_column, imag, zero)], axis=0)
        term = lax.dot_general(at_line, spread, (((1,), (1,)), ((), ())), preferred_element_type=jnp.float32)
        total = term if total is None else total + term
    out_ref[...] = dot(along_ref[...], jnp.concatenate([total, turned(total)], axis=0))


def apply_kernel(field_ref, potential_ref, z_ref, x_ref, back_x_ref, back_z_ref, out_ref, wide_ref, *, size, owners):
    per, own = size // (2 * owners), size // owners
    group = per * own
    wide = dot(field_ref[...], z_ref[...])
    for part in range(2):
        wide_ref[part] = wide[:, part * size : (part + 1) * size]

    def planes(y, part):
        return [wide_ref[part, pl.ds(y * per + t, owners, stride=group), :] for t in range(per)]

    columns = [jnp.concatenate(planes(y, 0) + planes(y, 1), axis=0) for y in range(own)]
    wave = dot(x_ref[...], jnp.concatenate(columns, axis=1))
    scale = jnp.concatenate([potential_ref[:, y, :] for y in range(own)], axis=1)
    product = jnp.concatenate([wave[:size] * scale, wave[size:] * scale], axis=0)
    back = dot(back_x_ref[...], product)
    for y in range(own):
        for t in range(per):
            for part in range(2):
                first = (part * per + t) * owners
                wide_ref[part, pl.ds(y * per + t, owners, stride=group), :] = back[first : first + owners, y * size : (y + 1) * size]
    out_ref[...] = dot(wide_ref[0], back_z_ref[:size]) + dot(wide_ref[1], back_z_ref[size:])


def pair_kernel(fields_ref, product_ref, out_ref, *, owners):
    bands = fields_ref.shape[0]
    lanes = product_ref.shape[1]
    group = product_ref.shape[0] // owners
    product = product_ref[...]
    half = lanes // 2
    crossed = jnp.concatenate([product[:, half:], -product[:, :half]], axis=1)
    sums = []
    for other in (product, crossed):
        for m in range(bands):
            sums.append(jnp.sum(fields_ref[m].reshape(product.shape) * other, axis=0, keepdims=True))
    sums = jnp.concatenate(sums, axis=0)
    sums = dot(sums, jnp.ones((lanes, lanes), jnp.float32))
    on_diagonal = lax.broadcasted_iota(jnp.int32, sums.shape, 0) == lax.broadcasted_iota(jnp.int32, sums.shape, 1)
    row = jnp.sum(jnp.where(on_diagonal, sums, 0.0), axis=0, keepdims=True)
    for r in range(group):
        out_ref[pl.ds(r, owners, stride=group + 1), :] = product_ref[pl.ds(r, owners, stride=group), :]
    out_ref[pl.ds(group, owners, stride=group + 1), :] = jnp.broadcast_to(row, (owners, lanes))


def project_kernel(owner_ref, occupied_ref, rows_ref, basis_ref, points_ref, along_ref, out_ref, *, size, owners, coefs):
    del owner_ref
    bands = occupied_ref.shape[0]
    group = rows_ref.shape[0] // owners
    sums = jnp.sum(rows_ref[pl.ds(group - 1, owners, stride=group), :], axis=0, keepdims=True)
    rows = jnp.concatenate([rows_ref[pl.ds(r, owners, stride=group), :] for r in range(group - 1)], axis=0)
    lines = dot(along_ref[...], jnp.concatenate([rows, turned(rows)], axis=0))
    line, column = places(points_ref[0], size, owners)
    at_line = picks(line, lines.shape[0]).astype(jnp.bfloat16)
    at_column = picks(column, size // 2)
    found = None
    for part in thirds(lines.T):
        term = jnp.dot(part, at_line, preferred_element_type=jnp.float32)
        found = term if found is None else found + term
    half = size // 2
    applied = [jnp.sum(jnp.where(at_column, found[p * half : (p + 1) * half], 0.0), axis=0, keepdims=True) for p in range(2)]
    tall, lanes = out_ref.shape[1:]
    taken = [jnp.zeros((tall, lanes), jnp.float32) for _ in range(2)]
    for m in range(bands):
        share = occupied_ref[m].astype(jnp.float32)
        weight_real = sums[:, m : m + 1] * (1.0 / coefs) * share
        weight_imag = sums[:, bands + m : bands + m + 1] * (1.0 / coefs) * share
        basis = basis_ref[m].reshape(2, tall, lanes)
        taken[0] = taken[0] + weight_real * basis[0] - weight_imag * basis[1]
        taken[1] = taken[1] + weight_imag * basis[0] + weight_real * basis[1]
    for p in range(2):
        for r in range(tall):
            out_ref[p, r : r + 1, :] = applied[p][:, r * lanes : (r + 1) * lanes] - taken[p][r : r + 1]


def whole(shape):
    return pl.BlockSpec(shape, lambda *_: (0,) * len(shape))


def spread(owner, psi, points, table, size, owners):
    block = points.shape[2]
    return pl.pallas_call(
        functools.partial(spread_kernel, size=size, owners=owners),
        out_shape=jax.ShapeDtypeStruct((table.shape[0], size), jnp.float32),
        grid_spec=pltpu.PrefetchScalarGridSpec(
            num_scalar_prefetch=1,
            grid=(1,),
            in_specs=[whole(psi.shape), pl.BlockSpec((1, 1, block), lambda i, at: (at[0], 0, 0)), whole(table.shape)],
            out_specs=whole((table.shape[0], size)),
        ),
        interpret=INTERPRET,
        name="spread",
    )(owner, psi, points, table)


def apply(field, potential, along_z, along_x, back_x, back_z, size, owners):
    return pl.pallas_call(
        functools.partial(apply_kernel, size=size, owners=owners),
        out_shape=jax.ShapeDtypeStruct(field.shape, jnp.float32),
        scratch_shapes=[pltpu.VMEM((2, *field.shape), jnp.float32)],
        interpret=INTERPRET,
        name="apply",
    )(field, potential, along_z, along_x, back_x, back_z)


def pair(gathered, product, owners):
    bands, tall = gathered.shape[0], product.shape[0] // gathered.shape[2]
    return pl.pallas_call(
        functools.partial(pair_kernel, owners=owners),
        out_shape=jax.ShapeDtypeStruct((product.shape[0] + owners, product.shape[1]), jnp.float32),
        grid=(1,),
        in_specs=[whole((bands, tall, *gathered.shape[2:])), whole(product.shape)],
        out_specs=whole((product.shape[0] + owners, product.shape[1])),
        interpret=INTERPRET,
        name="pair",
    )(gathered, product)


def project(owner, occupied, rows, gathered, points, table, size, owners, block, coefs):
    bands = gathered.shape[0]
    lanes = gathered.shape[3]
    tall = 2 * block // (gathered.shape[2] * lanes)
    last = gathered.shape[1] // tall - 1
    out_shape = (2, block // lanes, lanes)
    return pl.pallas_call(
        functools.partial(project_kernel, size=size, owners=owners, coefs=coefs),
        out_shape=jax.ShapeDtypeStruct(out_shape, jnp.float32),
        grid_spec=pltpu.PrefetchScalarGridSpec(
            num_scalar_prefetch=2,
            grid=(1,),
            in_specs=[
                whole(rows.shape),
                pl.BlockSpec((bands, tall, *gathered.shape[2:]), lambda i, at, occ: (0, last, 0, 0)),
                pl.BlockSpec((1, 1, block), lambda i, at, occ: (at[0], 0, 0)),
                whole(table.shape),
            ],
            out_specs=whole(out_shape),
        ),
        interpret=INTERPRET,
        name="project",
    )(owner, occupied, rows, gathered, points, table)


def shards(psi, potential, miller, occupied):
    size = potential.shape[0]
    owners = lax.axis_size("ga")
    bands = lax.axis_size("band")
    block = psi.shape[2]
    along_y, along_z, along_x, back_x, back_z, back_y = tables(size, owners)
    owner = lax.axis_index("ga").reshape(1)
    points = miller.reshape(-1, 1, block)
    rows = spread(owner, psi, points, along_y, size, owners)
    group = rows.shape[0] // owners
    rows = lax.all_to_all(rows.reshape(owners, group, size), "ga", split_axis=0, concat_axis=0, tiled=True)
    sent = jnp.concatenate([rows, psi.reshape(-1, group, size)], axis=0)
    gathered = lax.all_to_all(jnp.broadcast_to(sent, (bands, *sent.shape)), "band", split_axis=0, concat_axis=0, tiled=True)
    product = apply(rows.reshape(-1, size), potential, along_z, along_x, back_x, back_z, size, owners)
    rows = pair(gathered, product, owners)
    rows = lax.all_to_all(rows.reshape(owners, 1, -1), "ga", split_axis=0, concat_axis=0, tiled=True).reshape(rows.shape)
    out = project(owner, occupied, rows, gathered, points, back_y, size, owners, block, miller.shape[0])
    return out.reshape(2, 1, block)


def solution(mesh):
    in_specs = (P(None, "band", "ga"), P("pert", "ga", None), P(), P())
    out_specs = P(None, ("pert", "band"), "ga")
    return jax.shard_map(shards, mesh=mesh, in_specs=in_specs, out_specs=out_specs, check_vma=False)
```

time: 287 us -> 151 us (0.53)
  blocking collectives: 25.3 us -> 114 us
  local copies, waits for them, and re-layouts: 85.1 us -> 2.21 us
  waiting for transfers between devices: 92 us -> 14.8 us
  starting transfers between devices: 64.6 us -> 4.59 us
  matrix products: 14 us -> 0 us
  Pallas kernels: 0 us -> 13.5 us
  other arithmetic: 4.85 us -> 0.77 us
    all_to_all x1 -> x2, blocking collectives: 25.3 us -> 114 us  [the longest x1 76.7 us: shards(): lax.all_to_all(rows.reshape(owners, group, size), 'ga', split_axis=0, con...]
    all_to_all x5 -> x1, waiting for transfers between devices: 92 us -> 14.8 us  [shards(): lax.all_to_all(jnp.broadcast_to(sent, (bands, *sent.shape)), 'band', spli...]
    all_to_all x5 -> x1, starting transfers between devices: 64.6 us -> 4.59 us  [shards(): lax.all_to_all(jnp.broadcast_to(sent, (bands, *sent.shape)), 'band', spli...]
    gather x2 -> x0, local copies, waits for them, and re-layouts: 46.1 us -> none  [the longest x1 23 us: shards(): imag_part.reshape(band_count, slab_size)[:, position] * inverse_volume]
    scatter x2 -> x0, local copies, waits for them, and re-layouts: 31.1 us -> none  [the longest x1 15.5 us: shards(): jnp.zeros((band_count, slab_size), jnp.float32).at[:, position].set(psi[0])]
    pallas_call x0 -> x4, Pallas kernels: none -> 13.5 us  [the longest x1 3.96 us: apply(): pl.pallas_call(functools.partial(apply_kernel, size=size, owners=owners),...]
    dot_general x28 -> x0, matrix products: 12.4 us -> none  [the longest x5 2.37 us: contract(): jnp.einsum(pattern, imag_part, cosine, precision=highest)]
    unnamed x15 -> x4, local copies, waits for them, and re-layouts: 4.64 us -> 1.06 us
  transfers between devices with their start and end apart: 5 -> 1, of which waited for: 4 -> 1; matrix products, arithmetic and copies ran while one was open for 5% -> 0% of each run, Pallas kernels for 0% -> 3%
where the time goes in v1:
time: 151 us; the launch traced here: 150 us
  blocking collectives  114 us (75%)
  waiting for transfers between devices  14.8 us (10%)
  Pallas kernels  13.5 us (9%)
  starting transfers between devices  4.59 us (3%)
  local copies, waits for them, and re-layouts  2.21 us (1%)
    all_to_all x1, blocking collectives, shards(): lax.all_to_all(rows.reshape(owners, group, size), 'ga', split_axis=0, con...  76.7 us
    all_to_all x1, blocking collectives, shards(): lax.all_to_all(rows.reshape(owners, 1, -1), 'ga', split_axis=0, concat_ax...  37.6 us
    all_to_all x1, waiting for transfers between devices, shards(): lax.all_to_all(jnp.broadcast_to(sent, (bands, *sent.shape)), 'band', spli...  14.8 us
    all_to_all x1, starting transfers between devices, shards(): lax.all_to_all(jnp.broadcast_to(sent, (bands, *sent.shape)), 'band', spli...  4.59 us
    pallas_call x1, Pallas kernels, apply(): pl.pallas_call(functools.partial(apply_kernel, size=size, owners=owners),...  3.96 us
    pallas_call x1, Pallas kernels, project(): pl.pallas_call(functools.partial(project_kernel, size=size, owners=owners...  3.92 us
    pallas_call x1, Pallas kernels, spread(): pl.pallas_call(functools.partial(spread_kernel, size=size, owners=owners)...  3.48 us
  transfers between devices with their start and end apart: 1, of which 1 were waited for; matrix products, arithmetic and copies ran while one was open for 0% of the time, Pallas kernels for 3%

profile of v1, /device:TPU:40, one launch (start us, length us, event | category | flops | bytes accessed | tf_op | source)
XLA Modules:
  0.0 150.2 jit_solution(1666896981771819147)
XLA Ops:
  0.0 3.5 %spread.1 = f32[256,128]{1,0:T(8,128)} custom-call(s32[1]{0:T(128)} %bitcast.owner_ref, f32[2,1,4096]{2,1,0:T(1,128)} %psi_ref.1, s32[32,1,4096]{2,1,0:T(1,128)} %bitcast.8, f32[256,256]{1,0:T(8,128)} %constant.16.clone.along_ref), custom_call_target="tpu_custom_call" | custom-call | tf_op jit(solution)/shard_map/spread/pallas_call | solution.py:155
  3.5 76.7 %all_to_all.15 = f32[32,8,128]{2,1,0:T(8,128)S(1)} all-to-all(f32[32,8,128]{2,1,0:T(8,128)} %bitcast.13), channel_id=1, replica_groups=mesh['pert'=2,'ga'=32,'band'=8] {'ga'}, dimensions={0} | all-to-all | bytes 262144 | tf_op jit(solution)/shard_map/all_to_all | solution.py:227
  80.2 0.0 copy-start.1
  80.2 0.8 pad_maximum_fusion
  80.9 1.1 broadcast_in_dim.3
  82.1 0.0 copy-done.1
  82.1 4.6 %all-to-all-start.1 = ((f32[8,40,8,128]{3,2,1,0:T(8,128)}), f32[8,40,8,128]{3,2,1,0:T(8,128)S(1)}, u32[]{:S(2)}, u32[]{:S(2)}) async-start(f32[8,40,8,128]{3,2,1,0:T(8,128)} %broadcast_in_dim.3), calls=%async_computation.1 | async-start | bytes 2621440 | tf_op jit(solution)/shard_map/all_to_all | solution.py:229
  86.7 4.0 %apply.1.product_ref = f32[256,128]{1,0:T(8,128)} custom-call(f32[256,128]{1,0:T(8,128)} %bitcast.10, f32[128,4,128]{2,1,0:T(4,128)} %potential_ref.1, f32[128,256]{1,0:T(8,128)} %constant.17.clone.z_ref.back_x_ref, f32[256,128]{1,0:T(8,128)} %constant.18.clone.x_ref, f32[128,256]{1,0:T(8,128)} %constant.17.clone.z_ref.back_x_ref, ...), custom_call_target="tpu_custom_call" | custom-call | tf_op jit(solution)/shard_map/apply/pallas_call | solution.py:170
  90.6 14.8 %all-to-all-done.1.fields_ref.basis_ref = f32[8,40,8,128]{3,2,1,0:T(8,128)S(1)} async-done(((f32[8,40,8,128]{3,2,1,0:T(8,128)}), f32[8,40,8,128]{3,2,1,0:T(8,128)S(1)}, u32[]{:S(2)}, u32[]{:S(2)}) %all-to-all-start.1) | async-done | bytes 1310752 | tf_op jit(solution)/shard_map/all_to_all | solution.py:229
  105.4 0.0 copy-start
  105.4 1.1 copy-done
  106.5 2.2 %pair.1 = f32[288,128]{1,0:T(8,128)} custom-call(f32[8,40,8,128]{3,2,1,0:T(8,128)} %copy-done, f32[256,128]{1,0:T(8,128)} %apply.1.product_ref), custom_call_target="tpu_custom_call" | custom-call | tf_op jit(solution)/shard_map/pair/pallas_call | solution.py:181
  108.6 37.6 %all_to_all.16 = f32[32,1,1152]{2,1,0:T(1,128)} all-to-all(f32[32,1,1152]{2,1,0:T(1,128)} %bitcast.12), channel_id=1, replica_groups=mesh['pert'=2,'ga'=32,'band'=8] {'ga'}, dimensions={0} | all-to-all | bytes 294912 | tf_op jit(solution)/shard_map/all_to_all | solution.py:232
  146.3 3.9 %project.1 = f32[2,32,128]{2,1,0:T(8,128)} custom-call(s32[1]{0:T(128)} %bitcast.owner_ref, s32[8]{0:T(128)} %occupied_ref.1, f32[288,128]{1,0:T(8,128)} %bitcast.11, f32[8,40,8,128]{3,2,1,0:T(8,128)} %copy-done, s32[32,1,4096]{2,1,0:T(1,128)} %bitcast.9, f32[128,512]{1,0:T(8,128)} %constant.20.clone.along_ref), custom_call_target="tpu_custom_call" | custom-call | tf_op jit(solution)/shard_map/project/pallas_call | solution.py:198
Async XLA Ops:
  80.2 1.9 %copy-start.1 = (f32[32,8,128]{2,1,0:T(8,128)}, f32[32,8,128]{2,1,0:T(8,128)S(1)}, u32[]{:S(2)}) copy-start(f32[32,8,128]{2,1,0:T(8,128)S(1)} %all_to_all.15) | copy-start | bytes 393220
  82.1 23.3 %all-to-all-start.1 = ((f32[8,40,8,128]{3,2,1,0:T(8,128)}), f32[8,40,8,128]{3,2,1,0:T(8,128)S(1)}, u32[]{:S(2)}, u32[]{:S(2)}) async-start(f32[8,40,8,128]{3,2,1,0:T(8,128)} %broadcast_in_dim.3), calls=%async_computation.1 | async-start | bytes 2621440 | tf_op jit(solution)/shard_map/all_to_all | solution.py:229
  105.4 1.1 copy-start

commit v2 on v1

v2 whole, which is shorter than its diff:
```python
import functools

import jax
import jax.numpy as jnp
import numpy as np
from jax import lax
from jax.experimental import pallas as pl
from jax.experimental.pallas import tpu as pltpu
from jax.sharding import Mesh
from jax.sharding import PartitionSpec as P

highest = lax.Precision.HIGHEST
INTERPRET = False


def near(x):
    return x if INTERPRET else pltpu.with_memory_space_constraint(x, pltpu.VMEM)


def made(shape):
    return jax.ShapeDtypeStruct(shape, jnp.float32) if INTERPRET else pltpu.VMEM(shape, jnp.float32)


def dot(a, b):
    return jnp.dot(a, b, precision=highest, preferred_element_type=jnp.float32)


def thirds(x):
    high = x.astype(jnp.bfloat16)
    rest = x - high.astype(jnp.float32)
    mid = rest.astype(jnp.bfloat16)
    low = (rest - mid.astype(jnp.float32)).astype(jnp.bfloat16)
    return high, mid, low


def turned(x):
    half = x.shape[1] // 2
    return jnp.concatenate([-x[:, half:], x[:, :half]], axis=1)


def tables(size, owners):
    kept, per = size // 2, size // (2 * owners)
    signed = np.arange(kept) - size // 4
    full = np.arange(size)
    angle = 2.0 * np.pi / size * (full[:, None] * signed[None, :] % size)
    cosine, sine = np.cos(angle), np.sin(angle)
    rows = [np.einsum("yb,tu->ytub", part, np.eye(per)).reshape(size * per, per * kept) for part in (cosine, sine)]
    along_y = np.concatenate(rows, axis=1)
    along_z = np.block([[cosine.T, sine.T], [-sine.T, cosine.T]])
    along_x = np.block([[cosine, -sine], [sine, cosine]])
    own = size // owners
    back = [part.reshape(owners, own * per, per * kept).transpose(2, 1, 0).reshape(per * kept, size * per) for part in rows]
    back_y = np.concatenate([back[0], -back[1]], axis=1)
    as32 = lambda x: np.asarray(x, np.float32)
    return as32(along_y), as32(along_z), as32(along_x), as32(along_x.T), as32(along_z.T / size**3), as32(back_y)


def places(points, size, owners):
    quarter = size // 4
    plane = (points // (size * size) + quarter) % size
    row = (points // size + quarter) % size
    column = (points + quarter) % size
    return plane // owners * (size // 2) + row, column


def picks(index, count):
    return lax.broadcasted_iota(jnp.int32, (count, index.shape[1]), 0) == index


def own_points(owner_ref, points_ref, held_ref, sem):
    copy = pltpu.make_async_copy(points_ref.at[owner_ref[0]], held_ref, sem)
    copy.start()
    copy.wait()
    return held_ref[...]


def spread_kernel(owner_ref, psi_ref, points_ref, along_ref, out_ref, held_ref, sem, *, size, owners):
    line, column = places(own_points(owner_ref, points_ref, held_ref, sem), size, owners)
    at_line = picks(line, along_ref.shape[1] // 2).astype(jnp.bfloat16)
    at_column = picks(column, size // 2)
    zero = jnp.zeros((), jnp.bfloat16)
    total = None
    for real, imag in zip(thirds(psi_ref[0]), thirds(psi_ref[1])):
        spread = jnp.concatenate([jnp.where(at_column, real, zero), jnp.where(at_column, imag, zero)], axis=0)
        term = lax.dot_general(at_line, spread, (((1,), (1,)), ((), ())), preferred_element_type=jnp.float32)
        total = term if total is None else total + term
    out_ref[...] = dot(along_ref[...], jnp.concatenate([total, turned(total)], axis=0))


def fan_kernel(rows_ref, psi_ref, out_ref):
    for i in range(out_ref.shape[0]):
        out_ref[i, : rows_ref.shape[0]] = rows_ref[...]
        out_ref[i, rows_ref.shape[0] :] = psi_ref[...]


def apply_kernel(field_ref, potential_ref, z_ref, x_ref, back_x_ref, back_z_ref, out_ref, wide_ref, *, size, owners):
    per, own = size // (2 * owners), size // owners
    group = per * own
    wide = dot(field_ref[...], z_ref[...])
    for part in range(2):
        wide_ref[part] = wide[:, part * size : (part + 1) * size]

    def planes(y, part):
        return [wide_ref[part, pl.ds(y * per + t, owners, stride=group), :] for t in range(per)]

    columns = [jnp.concatenate(planes(y, 0) + planes(y, 1), axis=0) for y in range(own)]
    wave = dot(x_ref[...], jnp.concatenate(columns, axis=1))
    scale = jnp.concatenate([potential_ref[:, y, :] for y in range(own)], axis=1)
    product = jnp.concatenate([wave[:size] * scale, wave[size:] * scale], axis=0)
    back = dot(back_x_ref[...], product)
    for y in range(own):
        for t in range(per):
            for part in range(2):
                first = (part * per + t) * owners
                wide_ref[part, pl.ds(y * per + t, owners, stride=group), :] = back[first : first + owners, y * size : (y + 1) * size]
    out_ref[...] = dot(wide_ref[0], back_z_ref[:size]) + dot(wide_ref[1], back_z_ref[size:])


def pair_kernel(mine_ref, theirs_ref, product_ref, out_ref, *, owners):
    lanes = product_ref.shape[1]
    group = product_ref.shape[0] // owners
    product = product_ref[...]
    half = lanes // 2
    crossed = jnp.concatenate([product[:, half:], -product[:, :half]], axis=1)
    sums = []
    for other in (product, crossed):
        for fields_ref in (mine_ref, theirs_ref):
            for m in range(fields_ref.shape[0]):
                fields = fields_ref[m, :owners].reshape(product.shape)
                sums.append(jnp.sum(fields * other, axis=0, keepdims=True))
    sums = jnp.concatenate(sums, axis=0)
    sums = dot(sums, jnp.ones((lanes, lanes), jnp.float32))
    on_diagonal = lax.broadcasted_iota(jnp.int32, sums.shape, 0) == lax.broadcasted_iota(jnp.int32, sums.shape, 1)
    row = jnp.sum(jnp.where(on_diagonal, sums, 0.0), axis=0, keepdims=True)
    for r in range(group):
        out_ref[pl.ds(r, owners, stride=group + 1), :] = product_ref[pl.ds(r, owners, stride=group), :]
    out_ref[pl.ds(group, owners, stride=group + 1), :] = jnp.broadcast_to(row, (owners, lanes))


def project_kernel(owner_ref, core_ref, occupied_ref, rows_ref, mine_ref, theirs_ref, points_ref, along_ref, out_ref, held_ref, sem, *, size, owners, coefs):
    chips = mine_ref.shape[0]
    bands = 2 * chips
    group = rows_ref.shape[0] // owners
    sums = jnp.sum(rows_ref[pl.ds(group - 1, owners, stride=group), :], axis=0, keepdims=True)
    rows = jnp.concatenate([rows_ref[pl.ds(r, owners, stride=group), :] for r in range(group - 1)], axis=0)
    lines = dot(along_ref[...], jnp.concatenate([rows, turned(rows)], axis=0))
    line, column = places(own_points(owner_ref, points_ref, held_ref, sem), size, owners)
    at_line = picks(line, lines.shape[0]).astype(jnp.bfloat16)
    at_column = picks(column, size // 2)
    found = None
    for part in thirds(lines.T):
        term = jnp.dot(part, at_line, preferred_element_type=jnp.float32)
        found = term if found is None else found + term
    half = size // 2
    applied = [jnp.sum(jnp.where(at_column, found[p * half : (p + 1) * half], 0.0), axis=0, keepdims=True) for p in range(2)]
    tall, lanes = out_ref.shape[1:]
    taken = [jnp.zeros((tall, lanes), jnp.float32) for _ in range(2)]
    core = core_ref[0]
    for m in range(bands):
        held, chip = (mine_ref, m) if m < chips else (theirs_ref, m - chips)
        share = occupied_ref[2 * chip + (core if m < chips else 1 - core)].astype(jnp.float32)
        weight_real = sums[:, m : m + 1] * (1.0 / coefs) * share
        weight_imag = sums[:, bands + m : bands + m + 1] * (1.0 / coefs) * share
        basis = held[chip, owners:].reshape(2, tall, lanes)
        taken[0] = taken[0] + weight_real * basis[0] - weight_imag * basis[1]
        taken[1] = taken[1] + weight_imag * basis[0] + weight_real * basis[1]
    for p in range(2):
        for r in range(tall):
            out_ref[p, r : r + 1, :] = applied[p][:, r * lanes : (r + 1) * lanes] - taken[p][r : r + 1]


SCALARS = pl.BlockSpec(memory_space=pltpu.SMEM)
FAR = pl.BlockSpec(memory_space=pl.ANY)
WHOLE = pl.BlockSpec(memory_space=pltpu.VMEM)


def spread(owner, psi, points, table, size, owners):
    return pl.pallas_call(
        functools.partial(spread_kernel, size=size, owners=owners),
        out_shape=made((table.shape[0], size)),
        in_specs=[SCALARS, WHOLE, FAR, WHOLE],
        scratch_shapes=[pltpu.VMEM(points.shape[1:], points.dtype), pltpu.SemaphoreType.DMA],
        interpret=INTERPRET,
        name="spread",
    )(owner, near(psi), points, near(table))


def fan(rows, psi, copies):
    return pl.pallas_call(
        fan_kernel,
        out_shape=made((copies, rows.shape[0] + psi.shape[0], *rows.shape[1:])),
        interpret=INTERPRET,
        name="fan",
    )(near(rows), near(psi))


def apply(field, potential, along_z, along_x, back_x, back_z, size, owners):
    return pl.pallas_call(
        functools.partial(apply_kernel, size=size, owners=owners),
        out_shape=made(field.shape),
        scratch_shapes=[pltpu.VMEM((2, *field.shape), jnp.float32)],
        interpret=INTERPRET,
        name="apply",
    )(*map(near, (field, potential, along_z, along_x, back_x, back_z)))


def pair(mine, theirs, product, owners):
    return pl.pallas_call(
        functools.partial(pair_kernel, owners=owners),
        out_shape=made((product.shape[0] + owners, product.shape[1])),
        interpret=INTERPRET,
        name="pair",
    )(*map(near, (mine, theirs, product)))


def project(at, occupied, rows, mine, theirs, points, table, size, owners, coefs):
    block = points.shape[2]
    return pl.pallas_call(
        functools.partial(project_kernel, size=size, owners=owners, coefs=coefs),
        out_shape=jax.ShapeDtypeStruct((2, block // size, size), jnp.float32),
        in_specs=[SCALARS, SCALARS, SCALARS, WHOLE, WHOLE, WHOLE, FAR, WHOLE],
        scratch_shapes=[pltpu.VMEM(points.shape[1:], points.dtype), pltpu.SemaphoreType.DMA],
        interpret=INTERPRET,
        name="project",
    )(*at, occupied, near(rows), near(mine), near(theirs), points, near(table))


def shards(psi, potential, miller, occupied):
    size = potential.shape[0]
    owners = lax.axis_size("ga")
    block = psi.shape[2]
    along_y, along_z, along_x, back_x, back_z, back_y = tables(size, owners)
    at = tuple(lax.axis_index(axis).reshape(1) for axis in ("ga", "core"))
    points = miller.reshape(-1, 1, block)
    rows = spread(at[0], psi, points, along_y, size, owners)
    group = rows.shape[0] // owners
    rows = lax.all_to_all(rows.reshape(owners, group, size), "ga", split_axis=0, concat_axis=0, tiled=True)
    sent = fan(rows, psi.reshape(-1, group, size), lax.axis_size("chip"))
    mine = lax.all_to_all(sent, "chip", split_axis=0, concat_axis=0, tiled=True)
    theirs = lax.ppermute(mine, "core", [(0, 1), (1, 0)])
    product = apply(rows.reshape(-1, size), potential, along_z, along_x, back_x, back_z, size, owners)
    rows = pair(mine, theirs, product, owners)
    rows = lax.all_to_all(rows.reshape(owners, 1, -1), "ga", split_axis=0, concat_axis=0, tiled=True).reshape(rows.shape)
    out = project(at, occupied, rows, mine, theirs, points, back_y, size, owners, miller.shape[0])
    return out.reshape(2, 1, block)


def solution(mesh):
    groups, owners, bands = (mesh.shape[axis] for axis in ("pert", "ga", "band"))
    mesh = Mesh(mesh.devices.reshape(groups, owners, bands // 2, 2), ("pert", "ga", "chip", "core"))
    in_specs = (P(None, ("chip", "core"), "ga"), P("pert", "ga", None), P(), P())
    out_specs = P(None, ("pert", "chip", "core"), "ga")
    return jax.shard_map(shards, mesh=mesh, in_specs=in_specs, out_specs=out_specs, check_vma=False)
```

time: 151 us -> 141 us (0.934)
  blocking collectives: 114 us -> 89.8 us
  waiting for transfers between devices: 14.8 us -> 33 us
  Pallas kernels: 13.5 us -> 8.82 us
  starting transfers between devices: 4.59 us -> 6.88 us
    all_to_all x1, blocking collectives: 37.6 us -> 13.3 us  [shards(): mine = lax.all_to_all(sent, 'chip', split_axis=0, concat_axis=0, tiled=True)]
    all_to_all x1, waiting for transfers between devices: 14.8 us -> 33 us  [shards(): lax.all_to_all(rows.reshape(owners, 1, -1), 'ga', split_axis=0, concat_ax...]
    ppermute x0 -> x1, starting transfers between devices: none -> 1.94 us  [shards(): theirs = lax.ppermute(mine, 'core', [(0, 1), (1, 0)])]
    pallas_call x1, Pallas kernels: 3.96 us -> 2.11 us  [apply(): pl.pallas_call(functools.partial(apply_kernel, size=size, owners=owners),...]
  transfers between devices with their start and end apart: 1 -> 2, of which waited for: 1 -> 1; matrix products, arithmetic and copies ran while one was open for 0% -> 0% of each run, Pallas kernels for 3% -> 2%
where the time goes in v2:
time: 141 us; the launch traced here: 140 us
  blocking collectives  89.8 us (64%)
  waiting for transfers between devices  33 us (23%)
  Pallas kernels  8.82 us (6%)
  starting transfers between devices  6.88 us (5%)
  local copies, waits for them, and re-layouts  1.74 us (1%)
    all_to_all x1, blocking collectives, shards(): lax.all_to_all(rows.reshape(owners, group, size), 'ga', split_axis=0, con...  76.5 us
    all_to_all x1, waiting for transfers between devices, shards(): lax.all_to_all(rows.reshape(owners, 1, -1), 'ga', split_axis=0, concat_ax...  33 us
    all_to_all x1, blocking collectives, shards(): mine = lax.all_to_all(sent, 'chip', split_axis=0, concat_axis=0, tiled=True)  13.3 us
    all_to_all x1, starting transfers between devices, shards(): lax.all_to_all(rows.reshape(owners, 1, -1), 'ga', split_axis=0, concat_ax...  4.94 us
    pallas_call x1, Pallas kernels, project(): pl.pallas_call(functools.partial(project_kernel, size=size, owners=owners...  3.13 us
  transfers between devices with their start and end apart: 2, of which 1 were waited for; matrix products, arithmetic and copies ran while one was open for 0% of the time, Pallas kernels for 2%

profile of v2, /device:TPU:40, one launch (start us, length us, event | category | flops | bytes accessed | tf_op | source)
XLA Modules:
  0.0 140.4 jit_solution(6385382411607495627)
XLA Ops:
  0.0 0.0 copy-start.2
  0.0 0.9 copy-done.2
  1.0 0.0 copy-start.4
  1.0 0.8 copy-done.4
  1.7 2.6 %spread.1 = f32[256,128]{1,0:T(8,128)S(1)} custom-call(s32[1]{0:T(128)} %bitcast.owner_ref, f32[2,1,4096]{2,1,0:T(1,128)S(1)} %copy-done.4, s32[32,1,4096]{2,1,0:T(1,128)} %bitcast.13, f32[256,256]{1,0:T(8,128)S(1)} %copy-done.2), custom_call_target="tpu_custom_call" | custom-call | tf_op jit(solution)/shard_map/spread/pallas_call | solution.py:178
  4.3 76.5 %all_to_all.15.rows_ref = f32[32,8,128]{2,1,0:T(8,128)S(1)} all-to-all(f32[32,8,128]{2,1,0:T(8,128)S(1)} %bitcast.11), channel_id=1, replica_groups=mesh['pert'=2,'ga'=32,'chip'=4,'core'=2] {'ga'}, dimensions={0} | all-to-all | bytes 262144 | tf_op jit(solution)/shard_map/all_to_all | solution.py:237
  80.8 0.0 copy-start
  80.8 0.0 copy-start.3
  80.8 0.0 copy-start.5
  80.8 0.0 copy-start.6
  80.9 13.3 %all_to_all.16.mine_ref = f32[4,40,8,128]{3,2,1,0:T(8,128)S(1)} all-to-all(f32[4,40,8,128]{3,2,1,0:T(8,128)S(1)} %fan.1), channel_id=1, replica_groups=mesh['pert'=2,'ga'=32,'chip'=4,'core'=2] {'chip'}, dimensions={0} | all-to-all | bytes 1310720 | tf_op jit(solution)/shard_map/all_to_all | solution.py:239
  94.2 1.9 %collective-permute-start = (f32[4,40,8,128]{3,2,1,0:T(8,128)S(1)}, f32[4,40,8,128]{3,2,1,0:T(8,128)S(1)}, u32[]{:S(2)}, u32[]{:S(2)}) collective-permute-start(f32[4,40,8,128]{3,2,1,0:T(8,128)S(1)} %all_to_all.16.mine_ref), channel_id=1, source_target_pairs={{0,1},{1,0},{2,3},{3,2},{4,5},{5,4},{6,7},{7,6},{8,9},{9,8},{10,11... | collective-permute-start | bytes 1966088 | tf_op jit(solution)/shard_map/ppermute | solution.py:240
  96.1 0.0 copy-done
  96.1 0.0 copy-done.3
  96.1 0.0 copy-done.5
  96.1 0.0 copy-done.6
  96.1 2.1 %apply.1.product_ref = f32[256,128]{1,0:T(8,128)S(1)} custom-call(f32[256,128]{1,0:T(8,128)S(1)} %bitcast.9, f32[128,4,128]{2,1,0:T(4,128)S(1)} %copy-done.3, f32[128,256]{1,0:T(8,128)S(1)} %copy-done, f32[256,128]{1,0:T(8,128)S(1)} %copy-done.6, f32[128,256]{1,0:T(8,128)S(1)} %copy-done, f32[256,128]{1,0:T(8,128)S(1)} %copy-done.5), custom_call_target="tpu_custom_call" | custom-call | tf_op jit(solution)/shard_map/apply/pallas_call | solution.py:198
  98.3 0.0 collective-permute-done.theirs_ref
  98.3 1.0 pair.1
  99.2 0.0 copy-start.1
  99.2 4.9 %all-to-all-start.2 = ((f32[32,1,1152]{2,1,0:T(1,128)}), f32[32,1,1152]{2,1,0:T(1,128)S(1)}, u32[]{:S(2)}, u32[]{:S(2)}) async-start(f32[32,1,1152]{2,1,0:T(1,128)} %bitcast.6), calls=%async_computation.2 | async-start | bytes 294912 | tf_op jit(solution)/shard_map/all_to_all | solution.py:243
  104.2 33.0 %all-to-all-done.2 = f32[32,1,1152]{2,1,0:T(1,128)S(1)} async-done(((f32[32,1,1152]{2,1,0:T(1,128)}), f32[32,1,1152]{2,1,0:T(1,128)S(1)}, u32[]{:S(2)}, u32[]{:S(2)}) %all-to-all-start.2) | async-done | bytes 147488 | tf_op jit(solution)/shard_map/all_to_all | solution.py:243
  137.2 0.0 copy-done.1
  137.2 3.1 %project.1 = f32[2,32,128]{2,1,0:T(8,128)} custom-call(s32[1]{0:T(128)} %bitcast.owner_ref, s32[1]{0:T(128)} %bitcast.1.core_ref, s32[8]{0:T(128)} %occupied_ref.1, f32[288,128]{1,0:T(8,128)S(1)} %bitcast.10, f32[4,40,8,128]{3,2,1,0:T(8,128)S(1)} %all_to_all.16.mine_ref, f32[4,40,8,128]{3,2,1,0:T(8,128)S(1)} %collective-permute-done.theirs_ref, ...), custom_call_target="tpu_custom_call" | custom-call | tf_op jit(solution)/shard_map/project/pallas_call | solution.py:218
  (1 shorter events, 0.0 us)
Async XLA Ops:
  0.0 0.9 copy-start.2
  1.0 0.8 copy-start.4
  80.8 15.3 %copy-start = (f32[128,256]{1,0:T(8,128)S(1)}, f32[128,256]{1,0:T(8,128)}, u32[]{:S(2)}) copy-start(f32[128,256]{1,0:T(8,128)} %constant.21.clone.z_ref.back_x_ref) | copy-start | bytes 393220
  80.8 15.3 %copy-start.3 = (f32[128,4,128]{2,1,0:T(4,128)S(1)}, f32[128,4,128]{2,1,0:T(4,128)}, u32[]{:S(2)}) copy-start(f32[128,4,128]{2,1,0:T(4,128)} %potential_ref.1) | copy-start | bytes 786436
  80.8 15.3 %copy-start.5 = (f32[256,128]{1,0:T(8,128)S(1)}, f32[256,128]{1,0:T(8,128)}, u32[]{:S(2)}) copy-start(f32[256,128]{1,0:T(8,128)} %constant.23.clone.back_z_ref) | copy-start | bytes 393220
  80.8 15.3 %copy-start.6 = (f32[256,128]{1,0:T(8,128)S(1)}, f32[256,128]{1,0:T(8,128)}, u32[]{:S(2)}) copy-start(f32[256,128]{1,0:T(8,128)} %constant.22.clone.x_ref) | copy-start | bytes 393220
  94.2 4.1 %collective-permute-start = (f32[4,40,8,128]{3,2,1,0:T(8,128)S(1)}, f32[4,40,8,128]{3,2,1,0:T(8,128)S(1)}, u32[]{:S(2)}, u32[]{:S(2)}) collective-permute-start(f32[4,40,8,128]{3,2,1,0:T(8,128)S(1)} %all_to_all.16.mine_ref), channel_id=1, source_target_pairs={{0,1},{1,0},{2,3},{3,2},{4,5},{5,4},{6,7},{7,6},{8,9},{9,8},{10,11... | collective-permute-start | bytes 1966088 | tf_op jit(solution)/shard_map/ppermute | solution.py:240
  99.2 38.0 %copy-start.1 = (f32[128,512]{1,0:T(8,128)S(1)}, f32[128,512]{1,0:T(8,128)}, u32[]{:S(2)}) copy-start(f32[128,512]{1,0:T(8,128)} %constant.24.clone.along_ref) | copy-start | bytes 786436
  99.2 38.0 %all-to-all-start.2 = ((f32[32,1,1152]{2,1,0:T(1,128)}), f32[32,1,1152]{2,1,0:T(1,128)S(1)}, u32[]{:S(2)}, u32[]{:S(2)}) async-start(f32[32,1,1152]{2,1,0:T(1,128)} %bitcast.6), calls=%async_computation.2 | async-start | bytes 294912 | tf_op jit(solution)/shard_map/all_to_all | solution.py:243

commit v3 on v2

v3 whole, which is shorter than its diff:
```python
import functools

import jax
import jax.numpy as jnp
import numpy as np
from jax import lax
from jax.experimental import pallas as pl
from jax.experimental.pallas import tpu as pltpu
from jax.sharding import Mesh
from jax.sharding import PartitionSpec as P

highest = lax.Precision.HIGHEST
INTERPRET = False


def near(x):
    return x if INTERPRET else pltpu.with_memory_space_constraint(x, pltpu.VMEM)


def made(shape, dtype=jnp.float32):
    return jax.ShapeDtypeStruct(shape, dtype) if INTERPRET else pltpu.VMEM(shape, dtype)


def halves(x):
    high = x.astype(jnp.bfloat16)
    return high, (x - high.astype(jnp.float32)).astype(jnp.bfloat16)


def dot(a, b):
    part = functools.partial(jnp.dot, preferred_element_type=jnp.float32)
    return part(a[0], b[0]) + (part(a[0], b[1]) + part(a[1], b[0]))


def turned(x):
    half = x.shape[1] // 2
    return jnp.concatenate([-x[:, half:], x[:, :half]], axis=1)


def tables(size, owners):
    signed = np.arange(size // 2) - size // 4
    angle = 2.0 * np.pi / size * (np.arange(size)[:, None] * signed[None, :] % size)
    cosine, sine = np.cos(angle), np.sin(angle)
    along_y = np.concatenate([cosine, sine], axis=1)
    along_z = np.block([[cosine.T, sine.T], [-sine.T, cosine.T]])
    along_x = np.block([[cosine, -sine], [sine, cosine]])
    back = [part.reshape(owners, size // owners, -1).transpose(2, 1, 0).reshape(size // 2, size) for part in (cosine, -sine)]
    back_y = np.concatenate(back, axis=1)

    def both(table):
        table = np.asarray(table, np.float32)
        high = table.astype(jnp.bfloat16)
        return np.stack([high, (table - high.astype(np.float32)).astype(jnp.bfloat16)])

    return tuple(map(both, (along_y, along_z, along_x, along_x.T, along_z.T / size**3, back_y)))


def places(points, size, owners):
    quarter = size // 4
    plane = (points // (size * size) + quarter) % size
    row = (points // size + quarter) % size
    column = (points + quarter) % size
    return plane // owners * (size // 2) + row, column


def picks(index, count):
    return lax.broadcasted_iota(jnp.int32, (count, index.shape[1]), 0) == index


def own_points(owner_ref, points_ref, held_ref, sem):
    return pltpu.make_async_copy(points_ref.at[owner_ref[0]], held_ref, sem)


def spread_kernel(owner_ref, psi_ref, points_ref, along_ref, out_ref, psi_held, points_held, along_held, sems, *, size, owners):
    copies = [
        own_points(owner_ref, points_ref, points_held, sems.at[0]),
        pltpu.make_async_copy(psi_ref, psi_held, sems.at[1]),
        pltpu.make_async_copy(along_ref, along_held, sems.at[2]),
    ]
    for copy in copies:
        copy.start()
    copies[0].wait()
    line, column = places(points_held[...], size, owners)
    half = size // 2
    lines = half * half // owners
    at_line = picks(line, lines).astype(jnp.bfloat16)
    at_column = picks(column, half)
    zero = jnp.zeros((), jnp.bfloat16)
    copies[1].wait()
    parts = [part for pair in zip(halves(psi_held[0]), halves(psi_held[1])) for part in pair]
    values = jnp.concatenate([jnp.where(at_column, part, zero) for part in parts], axis=0)
    total = lax.dot_general(at_line, values, (((1,), (1,)), ((), ())), preferred_element_type=jnp.float32)
    total = total[:, :size] + total[:, size:]
    around = turned(total)
    planes = lines // half
    fields = [jnp.concatenate([x[t * half : (t + 1) * half] for x in (total, around)], axis=0) for t in range(planes)]
    copies[2].wait()
    rows = dot(along_held[...], halves(jnp.concatenate(fields, axis=1)))
    for t in range(planes):
        out_ref[pl.ds(t, size, stride=planes), :] = rows[:, t * size : (t + 1) * size]


def fan_kernel(rows_ref, out_ref):
    for i in range(out_ref.shape[0]):
        out_ref[i] = rows_ref[...]


def apply_kernel(field_ref, potential_ref, z_ref, x_ref, back_x_ref, back_z_ref, out_ref, wide_ref, *, size, owners):
    per, own = size // (2 * owners), size // owners
    group = per * own
    wide = dot(halves(field_ref[...]), z_ref[...])
    for part in range(2):
        wide_ref[part] = wide[:, part * size : (part + 1) * size]

    def planes(y, part):
        return [wide_ref[part, pl.ds(y * per + t, owners, stride=group), :] for t in range(per)]

    columns = [jnp.concatenate(planes(y, 0) + planes(y, 1), axis=0) for y in range(own)]
    wave = dot(x_ref[...], halves(jnp.concatenate(columns, axis=1)))
    scale = jnp.concatenate([potential_ref[:, y, :] for y in range(own)], axis=1)
    product = jnp.concatenate([wave[:size] * scale, wave[size:] * scale], axis=0)
    back = dot(back_x_ref[...], halves(product))
    for y in range(own):
        for t in range(per):
            for part in range(2):
                first = (part * per + t) * owners
                wide_ref[part, pl.ds(y * per + t, owners, stride=group), :] = back[first : first + owners, y * size : (y + 1) * size]
    out_ref[...] = dot(halves(jnp.concatenate([wide_ref[0], wide_ref[1]], axis=1)), back_z_ref[...])


def pair_kernel(mine_ref, theirs_ref, product_ref, out_ref, *, owners):
    lanes = product_ref.shape[1]
    group = product_ref.shape[0] // owners
    product = product_ref[...]
    half = lanes // 2
    crossed = jnp.concatenate([product[:, half:], -product[:, :half]], axis=1)
    sums = []
    for other in (product, crossed):
        for fields_ref in (mine_ref, theirs_ref):
            for m in range(fields_ref.shape[0]):
                sums.append(jnp.sum(fields_ref[m].reshape(product.shape) * other, axis=0, keepdims=True))
    sums = jnp.concatenate(sums, axis=0)
    sums = jnp.dot(sums, jnp.ones((lanes, lanes), jnp.float32), precision=highest, preferred_element_type=jnp.float32)
    on_diagonal = lax.broadcasted_iota(jnp.int32, sums.shape, 0) == lax.broadcasted_iota(jnp.int32, sums.shape, 1)
    row = jnp.sum(jnp.where(on_diagonal, sums, 0.0), axis=0, keepdims=True)
    for r in range(group):
        out_ref[pl.ds(r, owners, stride=group + 1), :] = product_ref[pl.ds(r, owners, stride=group), :]
    out_ref[pl.ds(group, owners, stride=group + 1), :] = jnp.broadcast_to(row, (owners, lanes))


def sift_kernel(owner_ref, points_ref, after_ref, line_ref, column_ref, held_ref, sem, *, size, owners):
    del after_ref
    copy = own_points(owner_ref, points_ref, held_ref, sem)
    copy.start()
    copy.wait()
    line, column = places(held_ref[...], size, owners)
    line_ref[...] = picks(line, line_ref.shape[0]).astype(jnp.bfloat16)
    column_ref[...] = jnp.broadcast_to(column, column_ref.shape)


def project_kernel(chip_ref, core_ref, occupied_ref, rows_ref, line_ref, column_ref, along_ref, mine_ref, theirs_ref, out_ref, *, size, owners, coefs):
    chips = mine_ref.shape[0]
    bands = 2 * chips
    half = size // 2
    group = rows_ref.shape[0] // owners
    planes = line_ref.shape[0] // half
    sums = jnp.sum(rows_ref[pl.ds(group - 1, owners, stride=group), :], axis=0, keepdims=True)
    fields = []
    for t in range(planes):
        rows = [rows_ref[pl.ds(r, owners, stride=group), :] for r in range(t, group - 1, planes)]
        rows = jnp.concatenate(rows, axis=0)
        fields.append(jnp.concatenate([rows, turned(rows)], axis=0))
    lines = dot(along_ref[...], halves(jnp.concatenate(fields, axis=1)))
    lines = jnp.concatenate([lines[:, t * size : (t + 1) * size].T for t in range(planes)], axis=1)
    at_line = line_ref[...]
    found = jnp.dot(jnp.concatenate(halves(lines), axis=1), jnp.concatenate([at_line, at_line], axis=0), preferred_element_type=jnp.float32)
    at_column = picks(column_ref[:1], half)
    applied = [jnp.sum(jnp.where(at_column, found[p * half : (p + 1) * half], 0.0), axis=0, keepdims=True) for p in range(2)]
    tall, lanes = out_ref.shape[1:]
    taken = [jnp.zeros((tall, lanes), jnp.float32) for _ in range(2)]
    chip, core = chip_ref[0], core_ref[0]
    for m in range(bands):
        held, source, from_core = (mine_ref, m, core) if m < chips else (theirs_ref, m - chips, 1 - core)
        share = occupied_ref[2 * source + from_core].astype(jnp.float32) * (1.0 / coefs)
        weight_real = sums[:, m : m + 1] * share
        weight_imag = sums[:, bands + m : bands + m + 1] * share
        basis = held[lax.rem(chip + chips - source, chips)].reshape(2, tall, lanes)
        taken[0] = taken[0] + weight_real * basis[0] - weight_imag * basis[1]
        taken[1] = taken[1] + weight_imag * basis[0] + weight_real * basis[1]
    for p in range(2):
        for r in range(tall):
            out_ref[p, r : r + 1, :] = applied[p][:, r * lanes : (r + 1) * lanes] - taken[p][r : r + 1]


def carry_kernel(x_ref, after_ref, out_ref):
    del after_ref
    out_ref[...] = x_ref[...]


def join_kernel(*refs):
    for i, ref in enumerate(refs[:-1]):
        refs[-1][i] = ref[...]


SCALARS = pl.BlockSpec(memory_space=pltpu.SMEM)
FAR = pl.BlockSpec(memory_space=pl.ANY)
WHOLE = pl.BlockSpec(memory_space=pltpu.VMEM)


def spread(owner, psi, points, table, size, owners):
    return pl.pallas_call(
        functools.partial(spread_kernel, size=size, owners=owners),
        out_shape=made((size * (size // (2 * owners)), size)),
        in_specs=[SCALARS, FAR, FAR, FAR],
        scratch_shapes=[
            pltpu.VMEM(psi.shape, psi.dtype),
            pltpu.VMEM(points.shape[1:], points.dtype),
            pltpu.VMEM(table.shape, table.dtype),
            pltpu.SemaphoreType.DMA((3,)),
        ],
        interpret=INTERPRET,
        name="spread",
    )(owner, psi, points, table)


def fan(rows, copies):
    return pl.pallas_call(fan_kernel, out_shape=made((copies, *rows.shape)), interpret=INTERPRET, name="fan")(near(rows))


def carry(x, after):
    return pl.pallas_call(carry_kernel, out_shape=made(x.shape), in_specs=[WHOLE, FAR], interpret=INTERPRET, name="carry")(near(x), after)


def join(parts):
    return pl.pallas_call(join_kernel, out_shape=made((len(parts), *parts[0].shape)), interpret=INTERPRET, name="join")(*map(near, parts))


def sift(owner, points, after, size, owners):
    block = points.shape[2]
    lines = size // 2 * (size // (2 * owners))
    return pl.pallas_call(
        functools.partial(sift_kernel, size=size, owners=owners),
        out_shape=(made((lines, block), jnp.bfloat16), made((8, block), jnp.int32)),
        in_specs=[SCALARS, FAR, FAR],
        scratch_shapes=[pltpu.VMEM(points.shape[1:], points.dtype), pltpu.SemaphoreType.DMA],
        interpret=INTERPRET,
        name="sift",
    )(owner, points, after)


def apply(field, potential, along_z, along_x, back_x, back_z, size, owners):
    return pl.pallas_call(
        functools.partial(apply_kernel, size=size, owners=owners),
        out_shape=made(field.shape),
        scratch_shapes=[pltpu.VMEM((2, *field.shape), jnp.float32)],
        interpret=INTERPRET,
        name="apply",
    )(*map(near, (field, potential, along_z, along_x, back_x, back_z)))


def pair(mine, theirs, product, owners):
    return pl.pallas_call(
        functools.partial(pair_kernel, owners=owners),
        out_shape=made((product.shape[0] + owners, product.shape[1])),
        interpret=INTERPRET,
        name="pair",
    )(*map(near, (mine, theirs, product)))


def project(place, occupied, rows, picked, table, mine, theirs, size, owners, coefs):
    lanes = size
    tall = mine.shape[1] // 2
    return pl.pallas_call(
        functools.partial(project_kernel, size=size, owners=owners, coefs=coefs),
        out_shape=jax.ShapeDtypeStruct((2, tall, lanes), jnp.float32),
        in_specs=[SCALARS, SCALARS, SCALARS] + [WHOLE] * 6,
        interpret=INTERPRET,
        name="project",
    )(*place, occupied, *map(near, (rows, *picked, table, mine, theirs)))


def along_ring(x, axis, step):
    count = lax.axis_size(axis)
    return lax.ppermute(x, axis, [(i, (i + step) % count) for i in range(count)])


def shards(psi, potential, miller, occupied):
    size = potential.shape[0]
    owners, chips = lax.axis_size("ga"), lax.axis_size("chip")
    block = psi.shape[2]
    along_y, along_z, along_x, back_x, back_z, back_y = tables(size, owners)
    owner = lax.axis_index("ga").reshape(1)
    place = tuple(lax.axis_index(axis).reshape(1) for axis in ("chip", "core"))
    points = miller.reshape(-1, 1, block)
    rows = spread(owner, psi, points, along_y, size, owners)
    group = rows.shape[0] // owners
    rows = lax.all_to_all(rows.reshape(owners, group, size), "ga", split_axis=0, concat_axis=0, tiled=True)
    mine = lax.all_to_all(fan(rows, chips), "chip", split_axis=0, concat_axis=0, tiled=True)
    theirs = along_ring(mine, "core", 1)
    product = apply(rows.reshape(-1, size), potential, along_z, along_x, back_x, back_z, size, owners)
    sent = pair(mine, theirs, product, owners)
    rows = lax.all_to_all(sent.reshape(owners, 1, -1), "ga", split_axis=0, concat_axis=0, tiled=True).reshape(sent.shape)
    picked = sift(owner, points, sent, size, owners)
    own = carry(psi.reshape(-1, size), sent)
    basis = join([own] + [along_ring(own, "chip", step) for step in range(1, chips)])
    other_basis = along_ring(basis, "core", 1)
    out = project(place, occupied, rows, picked, back_y, basis, other_basis, size, owners, miller.shape[0])
    return out.reshape(2, 1, block)


def solution(mesh):
    groups, owners, bands = (mesh.shape[axis] for axis in ("pert", "ga", "band"))
    mesh = Mesh(mesh.devices.reshape(groups, owners, bands // 2, 2), ("pert", "ga", "chip", "core"))
    in_specs = (P(None, ("chip", "core"), "ga"), P("pert", "ga", None), P(), P())
    out_specs = P(None, ("pert", "chip", "core"), "ga")
    return jax.shard_map(shards, mesh=mesh, in_specs=in_specs, out_specs=out_specs, check_vma=False)
```

time: 141 us -> 137 us (0.972)
  waiting for transfers between devices: 33 us -> 20.9 us
  starting transfers between devices: 6.88 us -> 18.1 us
  local copies, waits for them, and re-layouts: 1.74 us -> 0.04 us
    all_to_all x1, waiting for transfers between devices: 33 us -> 17.1 us  [shards(): lax.all_to_all(sent.reshape(owners, 1, -1), 'ga', split_axis=0, concat_ax...]
    ppermute x1 -> x5, starting transfers between devices: 1.94 us -> 13.2 us  [along_ring(): lax.ppermute(x, axis, [(i, (i + step) % count) for i in range(count)])]
    ppermute x1 -> x5, waiting for transfers between devices: 0.01 us -> 3.77 us  [along_ring(): lax.ppermute(x, axis, [(i, (i + step) % count) for i in range(count)])]
    unnamed x14 -> x12, local copies, waits for them, and re-layouts: 1.74 us -> 0.04 us
  transfers between devices with their start and end apart: 2 -> 6, of which waited for: 1 -> 5; matrix products, arithmetic and copies ran while one was open for 0% -> 0% of each run, Pallas kernels for 2% -> 2%
where the time goes in v3:
time: 137 us; the launch traced here: 136 us
  blocking collectives  89.1 us (65%)
  waiting for transfers between devices  20.9 us (15%)
  starting transfers between devices  18.1 us (13%)
  Pallas kernels  8.12 us (6%)
    all_to_all x1, blocking collectives, shards(): lax.all_to_all(rows.reshape(owners, group, size), 'ga', split_axis=0, con...  76.5 us
    all_to_all x1, waiting for transfers between devices, shards(): lax.all_to_all(sent.reshape(owners, 1, -1), 'ga', split_axis=0, concat_ax...  17.1 us
    ppermute x5, starting transfers between devices, along_ring(): lax.ppermute(x, axis, [(i, (i + step) % count) for i in range(count)])  13.2 us
    all_to_all x1, blocking collectives, shards(): lax.all_to_all(fan(rows, chips), 'chip', split_axis=0, concat_axis=0, til...  12.6 us
    all_to_all x1, starting transfers between devices, shards(): lax.all_to_all(sent.reshape(owners, 1, -1), 'ga', split_axis=0, concat_ax...  4.91 us
    ppermute x5, waiting for transfers between devices, along_ring(): lax.ppermute(x, axis, [(i, (i + step) % count) for i in range(count)])  3.77 us
  transfers between devices with their start and end apart: 6, of which 5 were waited for; matrix products, arithmetic and copies ran while one was open for 0% of the time, Pallas kernels for 2%

profile of v3, /device:TPU:40, one launch (start us, length us, event | category | flops | bytes accessed | tf_op | source)
XLA Modules:
  0.0 136.3 jit_solution(267876065085440118)
XLA Ops:
  0.0 2.3 %spread.1 = f32[256,128]{1,0:T(8,128)S(1)} custom-call(s32[1]{0:T(128)} %bitcast.2.owner_ref, f32[2,1,4096]{2,1,0:T(1,128)} %psi_ref.1, s32[32,1,4096]{2,1,0:T(1,128)} %bitcast.14, bf16[2,128,128]{2,1,0:T(8,128)(2,1)} %constant.23.clone.along_ref), custom_call_target="tpu_custom_call" | custom-call | tf_op jit(solution)/shard_map/spread/pallas_call | solution.py:210
  2.3 76.5 %all_to_all.15.rows_ref = f32[32,8,128]{2,1,0:T(8,128)S(1)} all-to-all(f32[32,8,128]{2,1,0:T(8,128)S(1)} %bitcast.12), channel_id=1, replica_groups=mesh['pert'=2,'ga'=32,'chip'=4,'core'=2] {'ga'}, dimensions={0} | all-to-all | bytes 262144 | tf_op jit(solution)/shard_map/all_to_all | solution.py:296
  78.9 0.0 copy-start
  78.9 0.0 copy-start.1
  78.9 0.0 copy-start.3
  78.9 0.0 copy-start.4
  78.9 12.6 %all_to_all.16.mine_ref = f32[4,32,8,128]{3,2,1,0:T(8,128)S(1)} all-to-all(f32[4,32,8,128]{3,2,1,0:T(8,128)S(1)} %fan.1), channel_id=1, replica_groups=mesh['pert'=2,'ga'=32,'chip'=4,'core'=2] {'chip'}, dimensions={0} | all-to-all | bytes 1048576 | tf_op jit(solution)/shard_map/all_to_all | solution.py:297
  91.5 1.9 %collective-permute-start = (f32[4,32,8,128]{3,2,1,0:T(8,128)S(1)}, f32[4,32,8,128]{3,2,1,0:T(8,128)S(1)}, u32[]{:S(2)}, u32[]{:S(2)}) collective-permute-start(f32[4,32,8,128]{3,2,1,0:T(8,128)S(1)} %all_to_all.16.mine_ref), channel_id=1, source_target_pairs={{0,1},{1,0},{2,3},{3,2},{4,5},{5,4},{6,7},{7,6},{8,9},{9,8},{10,11... | collective-permute-start | bytes 1572872 | tf_op jit(solution)/shard_map/ppermute | solution.py:283
  93.4 0.0 copy-done
  93.5 0.0 copy-done.1
  93.5 0.0 copy-done.3
  93.5 0.0 copy-done.4
  93.5 1.4 %apply.1.product_ref = f32[256,128]{1,0:T(8,128)S(1)} custom-call(f32[256,128]{1,0:T(8,128)S(1)} %bitcast.10, f32[128,4,128]{2,1,0:T(4,128)S(1)} %copy-done.1, bf16[2,128,256]{2,1,0:T(8,128)(2,1)S(1)} %copy-done, bf16[2,256,128]{2,1,0:T(8,128)(2,1)S(1)} %copy-done.3, bf16[2,128,256]{2,1,0:T(8,128)(2,1)S(1)} %copy-done, bf16[2,256,128]{2,1,0:T(8,128)(2,1)S(1)} %copy-done.4), custom_call_target="tpu_custom_call" | custom-call | tf_op jit(solution)/shard_map/apply/pallas_call | solution.py:251
  94.9 0.4 collective-permute-done.theirs_ref
  95.3 1.0 pair.1.after_ref
  96.3 0.0 copy-start.2
  96.3 4.9 %all-to-all-start.2 = ((f32[32,1,1152]{2,1,0:T(1,128)}), f32[32,1,1152]{2,1,0:T(1,128)S(1)}, u32[]{:S(2)}, u32[]{:S(2)}) async-start(f32[32,1,1152]{2,1,0:T(1,128)} %bitcast.6), calls=%async_computation.2 | async-start | bytes 294912 | tf_op jit(solution)/shard_map/all_to_all | solution.py:301
  101.2 0.0 copy-done.2
  101.2 2.5 %collective-permute-start.1 = (f32[64,128]{1,0:T(8,128)S(1)}, f32[64,128]{1,0:T(8,128)S(1)}, u32[]{:S(2)}, u32[]{:S(2)}) collective-permute-start(f32[64,128]{1,0:T(8,128)S(1)} %carry.1.refs_0_), channel_id=1, source_target_pairs={{0,2},{2,4},{4,6},{6,0},{1,3},{3,5},{5,7},{7,1},{8,10},{10,12},{12... | collective-permute-start | bytes 98312 | tf_op jit(solution)/shard_map/ppermute | solution.py:283
  103.8 4.0 %collective-permute-start.2 = (f32[64,128]{1,0:T(8,128)S(1)}, f32[64,128]{1,0:T(8,128)S(1)}, u32[]{:S(2)}, u32[]{:S(2)}) collective-permute-start(f32[64,128]{1,0:T(8,128)S(1)} %carry.1.refs_0_), channel_id=1, source_target_pairs={{0,4},{2,6},{4,0},{6,2},{1,5},{3,7},{5,1},{7,3},{8,12},{10,14},{12... | collective-permute-start | bytes 98312 | tf_op jit(solution)/shard_map/ppermute | solution.py:283
  107.8 2.8 %collective-permute-start.3 = (f32[64,128]{1,0:T(8,128)S(1)}, f32[64,128]{1,0:T(8,128)S(1)}, u32[]{:S(2)}, u32[]{:S(2)}) collective-permute-start(f32[64,128]{1,0:T(8,128)S(1)} %carry.1.refs_0_), channel_id=1, source_target_pairs={{0,6},{2,0},{4,2},{6,4},{1,7},{3,1},{5,3},{7,5},{8,14},{10,8},{12,... | collective-permute-start | bytes 98312 | tf_op jit(solution)/shard_map/ppermute | solution.py:283
  110.5 0.0 collective-permute-done.1.refs_1_
  110.5 0.6 collective-permute-done.2.refs_2_
  111.1 2.5 %collective-permute-done.3.refs_3_ = f32[64,128]{1,0:T(8,128)S(1)} collective-permute-done((f32[64,128]{1,0:T(8,128)S(1)}, f32[64,128]{1,0:T(8,128)S(1)}, u32[]{:S(2)}, u32[]{:S(2)}) %collective-permute-start.3) | collective-permute-done | bytes 32800 | tf_op jit(solution)/shard_map/ppermute | solution.py:283
  113.6 2.0 %collective-permute-start.4 = (f32[4,64,128]{2,1,0:T(8,128)S(1)}, f32[4,64,128]{2,1,0:T(8,128)S(1)}, u32[]{:S(2)}, u32[]{:S(2)}) collective-permute-start(f32[4,64,128]{2,1,0:T(8,128)S(1)} %join.1.mine_ref), channel_id=1, source_target_pairs={{0,1},{1,0},{2,3},{3,2},{4,5},{5,4},{6,7},{7,6},{8,9},{9,8},{10,11... | collective-permute-start | bytes 393224 | tf_op jit(solution)/shard_map/ppermute | solution.py:283
  115.6 0.0 copy-start.5
  115.6 1.0 sift.1
  116.6 0.3 collective-permute-done.4.theirs_ref
  116.9 17.1 %all-to-all-done.2 = f32[32,1,1152]{2,1,0:T(1,128)S(1)} async-done(((f32[32,1,1152]{2,1,0:T(1,128)}), f32[32,1,1152]{2,1,0:T(1,128)S(1)}, u32[]{:S(2)}, u32[]{:S(2)}) %all-to-all-start.2) | async-done | bytes 147488 | tf_op jit(solution)/shard_map/all_to_all | solution.py:301
  134.0 0.0 copy-done.5
  134.0 2.3 %project.1 = f32[2,32,128]{2,1,0:T(8,128)} custom-call(s32[1]{0:T(128)} %bitcast.chip_ref, s32[1]{0:T(128)} %bitcast.1.core_ref, s32[8]{0:T(128)} %occupied_ref.1, f32[288,128]{1,0:T(8,128)S(1)} %bitcast.11, bf16[128,4096]{1,0:T(8,128)(2,1)S(1)} %get-tuple-element.7.line_ref, s32[8,4096]{1,0:T(8,128)S(1)} %get-tuple-element.8.column_ref, ...), custom_call_target="tpu_custom_call" | custom-call | tf_op jit(solution)/shard_map/project/pallas_call | solution.py:272
  (3 shorter events, 0.0 us)
Async XLA Ops:
  78.9 14.6 %copy-start = (bf16[2,128,256]{2,1,0:T(8,128)(2,1)S(1)}, bf16[2,128,256]{2,1,0:T(8,128)(2,1)}, u32[]{:S(2)}) copy-start(bf16[2,128,256]{2,1,0:T(8,128)(2,1)} %constant.24.clone.z_ref.back_x_ref) | copy-start | bytes 393220
  78.9 14.6 %copy-start.1 = (f32[128,4,128]{2,1,0:T(4,128)S(1)}, f32[128,4,128]{2,1,0:T(4,128)}, u32[]{:S(2)}) copy-start(f32[128,4,128]{2,1,0:T(4,128)} %potential_ref.1) | copy-start | bytes 786436
  78.9 14.6 %copy-start.3 = (bf16[2,256,128]{2,1,0:T(8,128)(2,1)S(1)}, bf16[2,256,128]{2,1,0:T(8,128)(2,1)}, u32[]{:S(2)}) copy-start(bf16[2,256,128]{2,1,0:T(8,128)(2,1)} %constant.25.clone.x_ref) | copy-start | bytes 393220
  78.9 14.6 %copy-start.4 = (bf16[2,256,128]{2,1,0:T(8,128)(2,1)S(1)}, bf16[2,256,128]{2,1,0:T(8,128)(2,1)}, u32[]{:S(2)}) copy-start(bf16[2,256,128]{2,1,0:T(8,128)(2,1)} %constant.26.clone.back_z_ref) | copy-start | bytes 393220
  91.5 3.8 %collective-permute-start = (f32[4,32,8,128]{3,2,1,0:T(8,128)S(1)}, f32[4,32,8,128]{3,2,1,0:T(8,128)S(1)}, u32[]{:S(2)}, u32[]{:S(2)}) collective-permute-start(f32[4,32,8,128]{3,2,1,0:T(8,128)S(1)} %all_to_all.16.mine_ref), channel_id=1, source_target_pairs={{0,1},{1,0},{2,3},{3,2},{4,5},{5,4},{6,7},{7,6},{8,9},{9,8},{10,11... | collective-permute-start | bytes 1572872 | tf_op jit(solution)/shard_map/ppermute | solution.py:283
  96.3 4.9 %copy-start.2 = (f32[2,1,4096]{2,1,0:T(1,128)S(1)}, f32[2,1,4096]{2,1,0:T(1,128)}, u32[]{:S(2)}) copy-start(f32[2,1,4096]{2,1,0:T(1,128)} %psi_ref.1) | copy-start | bytes 98308
  96.3 37.7 %all-to-all-start.2 = ((f32[32,1,1152]{2,1,0:T(1,128)}), f32[32,1,1152]{2,1,0:T(1,128)S(1)}, u32[]{:S(2)}, u32[]{:S(2)}) async-start(f32[32,1,1152]{2,1,0:T(1,128)} %bitcast.6), calls=%async_computation.2 | async-start | bytes 294912 | tf_op jit(solution)/shard_map/all_to_all | solution.py:301
  101.2 9.3 %collective-permute-start.1 = (f32[64,128]{1,0:T(8,128)S(1)}, f32[64,128]{1,0:T(8,128)S(1)}, u32[]{:S(2)}, u32[]{:S(2)}) collective-permute-start(f32[64,128]{1,0:T(8,128)S(1)} %carry.1.refs_0_), channel_id=1, source_target_pairs={{0,2},{2,4},{4,6},{6,0},{1,3},{3,5},{5,7},{7,1},{8,10},{10,12},{12... | collective-permute-start | bytes 98312 | tf_op jit(solution)/shard_map/ppermute | solution.py:283
  103.8 7.3 %collective-permute-start.2 = (f32[64,128]{1,0:T(8,128)S(1)}, f32[64,128]{1,0:T(8,128)S(1)}, u32[]{:S(2)}, u32[]{:S(2)}) collective-permute-start(f32[64,128]{1,0:T(8,128)S(1)} %carry.1.refs_0_), channel_id=1, source_target_pairs={{0,4},{2,6},{4,0},{6,2},{1,5},{3,7},{5,1},{7,3},{8,12},{10,14},{12... | collective-permute-start | bytes 98312 | tf_op jit(solution)/shard_map/ppermute | solution.py:283
  107.8 5.8 %collective-permute-start.3 = (f32[64,128]{1,0:T(8,128)S(1)}, f32[64,128]{1,0:T(8,128)S(1)}, u32[]{:S(2)}, u32[]{:S(2)}) collective-permute-start(f32[64,128]{1,0:T(8,128)S(1)} %carry.1.refs_0_), channel_id=1, source_target_pairs={{0,6},{2,0},{4,2},{6,4},{1,7},{3,1},{5,3},{7,5},{8,14},{10,8},{12,... | collective-permute-start | bytes 98312 | tf_op jit(solution)/shard_map/ppermute | solution.py:283
  113.6 3.3 %collective-permute-start.4 = (f32[4,64,128]{2,1,0:T(8,128)S(1)}, f32[4,64,128]{2,1,0:T(8,128)S(1)}, u32[]{:S(2)}, u32[]{:S(2)}) collective-permute-start(f32[4,64,128]{2,1,0:T(8,128)S(1)} %join.1.mine_ref), channel_id=1, source_target_pairs={{0,1},{1,0},{2,3},{3,2},{4,5},{5,4},{6,7},{7,6},{8,9},{9,8},{10,11... | collective-permute-start | bytes 393224 | tf_op jit(solution)/shard_map/ppermute | solution.py:283
  115.6 18.4 %copy-start.5 = (bf16[2,64,256]{2,1,0:T(8,128)(2,1)S(1)}, bf16[2,64,256]{2,1,0:T(8,128)(2,1)}, u32[]{:S(2)}) copy-start(bf16[2,64,256]{2,1,0:T(8,128)(2,1)} %constant.27.clone.along_ref) | copy-start | bytes 196612

commit v4 on v3

v4 whole, which is shorter than its diff:
```python
import functools

import jax
import jax.numpy as jnp
import numpy as np
from jax import lax
from jax.experimental import pallas as pl
from jax.experimental.pallas import tpu as pltpu
from jax.sharding import Mesh
from jax.sharding import PartitionSpec as P

highest = lax.Precision.HIGHEST
INTERPRET = False


def near(x):
    return x if INTERPRET else pltpu.with_memory_space_constraint(x, pltpu.VMEM)


def made(shape, dtype=jnp.float32):
    return jax.ShapeDtypeStruct(shape, dtype) if INTERPRET else pltpu.VMEM(shape, dtype)


def halves(x):
    high = x.astype(jnp.bfloat16)
    return high, (x - high.astype(jnp.float32)).astype(jnp.bfloat16)


def dot(a, b):
    part = functools.partial(jnp.dot, preferred_element_type=jnp.float32)
    return part(a[0], b[0]) + (part(a[0], b[1]) + part(a[1], b[0]))


def turned(x):
    half = x.shape[1] // 2
    return jnp.concatenate([-x[:, half:], x[:, :half]], axis=1)


def tables(size, owners):
    signed = np.arange(size // 2) - size // 4
    angle = 2.0 * np.pi / size * (np.arange(size)[:, None] * signed[None, :] % size)
    cosine, sine = np.cos(angle), np.sin(angle)
    along_y = np.concatenate([cosine, sine], axis=1)
    along_z = np.block([[cosine.T, sine.T], [-sine.T, cosine.T]])
    along_x = np.block([[cosine, -sine], [sine, cosine]])
    back = [part.reshape(owners, size // owners, -1).transpose(2, 1, 0).reshape(size // 2, size) for part in (cosine, -sine)]
    back_y = np.concatenate(back, axis=1)

    def both(table):
        table = np.asarray(table, np.float32)
        high = table.astype(jnp.bfloat16)
        return np.stack([high, (table - high.astype(np.float32)).astype(jnp.bfloat16)])

    return tuple(map(both, (along_y, along_z, along_x, along_x.T, along_z.T / size**3, back_y)))


def places(points, size, owners):
    quarter = size // 4
    plane = (points // (size * size) + quarter) % size
    row = (points // size + quarter) % size
    column = (points + quarter) % size
    return plane // owners * (size // 2) + row, column


def picks(index, count):
    return lax.broadcasted_iota(jnp.int32, (count, index.shape[1]), 0) == index


def own_points(owner_ref, points_ref, held_ref, sem):
    return pltpu.make_async_copy(points_ref.at[owner_ref[0]], held_ref, sem)


def spread_kernel(owner_ref, core_ref, psi_ref, points_ref, along_ref, out_ref, psi_held, points_held, along_held, sems, *, size, owners):
    del core_ref
    copies = [
        own_points(owner_ref, points_ref, points_held, sems.at[0]),
        pltpu.make_async_copy(psi_ref, psi_held, sems.at[1]),
        pltpu.make_async_copy(along_ref, along_held, sems.at[2]),
    ]
    for copy in copies:
        copy.start()
    copies[0].wait()
    line, column = places(points_held[...], size, owners)
    half = size // 2
    lines = half * half // owners
    at_line = picks(line, lines).astype(jnp.bfloat16)
    at_column = picks(column, half)
    zero = jnp.zeros((), jnp.bfloat16)
    copies[1].wait()
    parts = [part for pair in zip(halves(psi_held[0]), halves(psi_held[1])) for part in pair]
    values = jnp.concatenate([jnp.where(at_column, part, zero) for part in parts], axis=0)
    total = lax.dot_general(at_line, values, (((1,), (1,)), ((), ())), preferred_element_type=jnp.float32)
    total = total[:, :size] + total[:, size:]
    around = turned(total)
    planes = lines // half
    fields = [jnp.concatenate([x[t * half : (t + 1) * half] for x in (total, around)], axis=0) for t in range(planes)]
    copies[2].wait()
    rows = dot(along_held[...], halves(jnp.concatenate(fields, axis=1)))
    for t in range(planes):
        out_ref[pl.ds(t, size, stride=planes), :] = rows[:, t * size : (t + 1) * size]


def fan_kernel(rows_ref, psi_ref, out_ref):
    for i in range(out_ref.shape[0]):
        out_ref[i, : rows_ref.shape[0]] = rows_ref[...]
        out_ref[i, rows_ref.shape[0] :] = psi_ref[...]


def apply_kernel(field_ref, potential_ref, z_ref, x_ref, back_x_ref, back_z_ref, mine_ref, out_ref, sums_ref, wide_ref, *, size, owners):
    per, own = size // (2 * owners), size // owners
    group = per * own
    wide = dot(halves(field_ref[...]), z_ref[...])
    for part in range(2):
        wide_ref[part] = wide[:, part * size : (part + 1) * size]

    def planes(y, part):
        return [wide_ref[part, pl.ds(y * per + t, owners, stride=group), :] for t in range(per)]

    columns = [jnp.concatenate(planes(y, 0) + planes(y, 1), axis=0) for y in range(own)]
    wave = dot(x_ref[...], halves(jnp.concatenate(columns, axis=1)))
    scale = jnp.concatenate([potential_ref[:, y, :] for y in range(own)], axis=1)
    product = jnp.concatenate([wave[:size] * scale, wave[size:] * scale], axis=0)
    back = dot(back_x_ref[...], halves(product))
    for y in range(own):
        for t in range(per):
            for part in range(2):
                first = (part * per + t) * owners
                wide_ref[part, pl.ds(y * per + t, owners, stride=group), :] = back[first : first + owners, y * size : (y + 1) * size]
    product = dot(halves(jnp.concatenate([wide_ref[0], wide_ref[1]], axis=1)), back_z_ref[...])
    out_ref[...] = product
    sums_ref[...] = overlaps(mine_ref, product, owners)


def overlaps(fields_ref, product, owners):
    half = product.shape[1] // 2
    crossed = jnp.concatenate([product[:, half:], -product[:, :half]], axis=1)
    fields = [fields_ref[m, :owners].reshape(product.shape) for m in range(fields_ref.shape[0])]
    return jnp.concatenate([jnp.sum(f * other, axis=0, keepdims=True) for other in (product, crossed) for f in fields], axis=0)


def pair_kernel(theirs_ref, product_ref, sums_ref, out_ref, *, owners):
    lanes = product_ref.shape[1]
    group = product_ref.shape[0] // owners
    sums = jnp.concatenate([sums_ref[...], overlaps(theirs_ref, product_ref[...], owners)], axis=0)
    sums = jnp.dot(sums, jnp.ones((lanes, lanes), jnp.float32), precision=highest, preferred_element_type=jnp.float32)
    on_diagonal = lax.broadcasted_iota(jnp.int32, sums.shape, 0) == lax.broadcasted_iota(jnp.int32, sums.shape, 1)
    row = jnp.sum(jnp.where(on_diagonal, sums, 0.0), axis=0, keepdims=True)
    for r in range(group):
        out_ref[pl.ds(r, owners, stride=group + 1), :] = product_ref[pl.ds(r, owners, stride=group), :]
    out_ref[pl.ds(group, owners, stride=group + 1), :] = jnp.broadcast_to(row, (owners, lanes))


def project_kernel(
    owner_ref, core_ref, occupied_ref, rows_ref, points_ref, along_ref, mine_ref, theirs_ref, out_ref, held_ref, sem, *, size, owners, coefs
):
    copy = own_points(owner_ref, points_ref, held_ref, sem)
    copy.start()
    chips = mine_ref.shape[0]
    bands = 2 * chips
    half = size // 2
    group = rows_ref.shape[0] // owners
    planes = half // owners
    sums = jnp.sum(rows_ref[pl.ds(group - 1, owners, stride=group), :], axis=0, keepdims=True)
    fields = []
    for t in range(planes):
        rows = [rows_ref[pl.ds(r, owners, stride=group), :] for r in range(t, group - 1, planes)]
        rows = jnp.concatenate(rows, axis=0)
        fields.append(jnp.concatenate([rows, turned(rows)], axis=0))
    lines = dot(along_ref[...], halves(jnp.concatenate(fields, axis=1)))
    lines = jnp.concatenate([lines[:, t * size : (t + 1) * size].T for t in range(planes)], axis=1)
    copy.wait()
    line, column = places(held_ref[...], size, owners)
    at_line = picks(line, lines.shape[1]).astype(jnp.bfloat16)
    at_column = picks(column, half)
    found = jnp.dot(jnp.concatenate(halves(lines), axis=1), jnp.concatenate([at_line, at_line], axis=0), preferred_element_type=jnp.float32)
    applied = [jnp.sum(jnp.where(at_column, found[p * half : (p + 1) * half], 0.0), axis=0, keepdims=True) for p in range(2)]
    tall, lanes = out_ref.shape[1:]
    taken = [jnp.zeros((tall, lanes), jnp.float32) for _ in range(2)]
    core = core_ref[0]
    for m in range(bands):
        held, first, source, from_core = (mine_ref, 0, m, core) if m < chips else (theirs_ref, 2 * chips, m - chips, 1 - core)
        share = occupied_ref[2 * source + from_core].astype(jnp.float32) * (1.0 / coefs)
        weight_real = sums[:, first + source : first + source + 1] * share
        weight_imag = sums[:, first + chips + source : first + chips + source + 1] * share
        basis = held[source, owners:].reshape(2, tall, lanes)
        taken[0] = taken[0] + weight_real * basis[0] - weight_imag * basis[1]
        taken[1] = taken[1] + weight_imag * basis[0] + weight_real * basis[1]
    for p in range(2):
        for r in range(tall):
            out_ref[p, r : r + 1, :] = applied[p][:, r * lanes : (r + 1) * lanes] - taken[p][r : r + 1]


SCALARS = pl.BlockSpec(memory_space=pltpu.SMEM)
FAR = pl.BlockSpec(memory_space=pl.ANY)
WHOLE = pl.BlockSpec(memory_space=pltpu.VMEM)


def spread(owner, core, psi, points, table, size, owners):
    return pl.pallas_call(
        functools.partial(spread_kernel, size=size, owners=owners),
        out_shape=made((size * (size // (2 * owners)), size)),
        in_specs=[SCALARS, SCALARS, FAR, FAR, FAR],
        scratch_shapes=[
            pltpu.VMEM(psi.shape, psi.dtype),
            pltpu.VMEM(points.shape[1:], points.dtype),
            pltpu.VMEM(table.shape, table.dtype),
            pltpu.SemaphoreType.DMA((3,)),
        ],
        interpret=INTERPRET,
        name="spread",
    )(owner, core, psi, points, table)


def fan(rows, psi, copies):
    shape = (copies, rows.shape[0] + psi.shape[0], *rows.shape[1:])
    return pl.pallas_call(fan_kernel, out_shape=made(shape), interpret=INTERPRET, name="fan")(near(rows), near(psi))


def apply(field, potential, along_z, along_x, back_x, back_z, mine, size, owners):
    return pl.pallas_call(
        functools.partial(apply_kernel, size=size, owners=owners),
        out_shape=(made(field.shape), made((2 * mine.shape[0], size))),
        scratch_shapes=[pltpu.VMEM((2, *field.shape), jnp.float32)],
        interpret=INTERPRET,
        name="apply",
    )(*map(near, (field, potential, along_z, along_x, back_x, back_z, mine)))


def pair(theirs, product, sums, owners):
    return pl.pallas_call(
        functools.partial(pair_kernel, owners=owners),
        out_shape=made((product.shape[0] + owners, product.shape[1])),
        interpret=INTERPRET,
        name="pair",
    )(*map(near, (theirs, product, sums)))


def project(owner, core, occupied, rows, points, table, mine, theirs, size, owners, coefs):
    block = points.shape[2]
    return pl.pallas_call(
        functools.partial(project_kernel, size=size, owners=owners, coefs=coefs),
        out_shape=jax.ShapeDtypeStruct((2, block // size, size), jnp.float32),
        in_specs=[SCALARS, SCALARS, SCALARS, WHOLE, FAR, WHOLE, WHOLE, WHOLE],
        scratch_shapes=[pltpu.VMEM(points.shape[1:], points.dtype), pltpu.SemaphoreType.DMA],
        interpret=INTERPRET,
        name="project",
    )(owner, core, occupied, near(rows), points, near(table), near(mine), near(theirs))


def along_ring(x, axis, step):
    count = lax.axis_size(axis)
    return lax.ppermute(x, axis, [(i, (i + step) % count) for i in range(count)])


def shards(psi, potential, miller, occupied):
    size = potential.shape[0]
    owners, chips = lax.axis_size("ga"), lax.axis_size("chip")
    block = psi.shape[2]
    along_y, along_z, along_x, back_x, back_z, back_y = tables(size, owners)
    owner, core = (lax.axis_index(axis).reshape(1) for axis in ("ga", "core"))
    points = miller.reshape(-1, 1, block)
    rows = spread(owner, core, psi, points, along_y, size, owners)
    group = rows.shape[0] // owners
    rows = lax.all_to_all(rows.reshape(owners, group, size), "ga", split_axis=0, concat_axis=0, tiled=True)
    sent = fan(rows, psi.reshape(-1, group, size), chips)
    mine = lax.all_to_all(sent, "chip", split_axis=0, concat_axis=0, tiled=True)
    theirs = along_ring(mine, "core", 1)
    product, sums = apply(rows.reshape(-1, size), potential, along_z, along_x, back_x, back_z, mine, size, owners)
    sent = pair(theirs, product, sums, owners)
    rows = lax.all_to_all(sent.reshape(owners, 1, -1), "ga", split_axis=0, concat_axis=0, tiled=True).reshape(sent.shape)
    out = project(owner, core, occupied, rows, points, back_y, mine, theirs, size, owners, miller.shape[0])
    return out.reshape(2, 1, block)


def solution(mesh):
    groups, owners, bands = (mesh.shape[axis] for axis in ("pert", "ga", "band"))
    mesh = Mesh(mesh.devices.reshape(groups, owners, bands // 2, 2), ("pert", "ga", "chip", "core"))
    in_specs = (P(None, ("chip", "core"), "ga"), P("pert", "ga", None), P(), P())
    out_specs = P(None, ("pert", "chip", "core"), "ga")
    return jax.shard_map(shards, mesh=mesh, in_specs=in_specs, out_specs=out_specs, check_vma=False)
```

time: 137 us -> 137 us (level)
  blocking collectives: 89.1 us -> 127 us
  waiting for transfers between devices: 20.9 us -> 0.52 us
  starting transfers between devices: 18.1 us -> 1.94 us
    all_to_all x1 -> x2, blocking collectives: 12.6 us -> 50.6 us  [the longest x1 37.3 us: shards(): lax.all_to_all(sent.reshape(owners, 1, -1), 'ga', split_axis=0, concat_ax...]
    all_to_all x1 -> x0, waiting for transfers between devices: 17.1 us -> none  [shards(): lax.all_to_all(sent.reshape(owners, 1, -1), 'ga', split_axis=0, concat_ax...]
    ppermute x5 -> x1, starting transfers between devices: 13.2 us -> 1.94 us  [along_ring(): lax.ppermute(x, axis, [(i, (i + step) % count) for i in range(count)])]
    all_to_all x1 -> x0, starting transfers between devices: 4.91 us -> none  [shards(): lax.all_to_all(sent.reshape(owners, 1, -1), 'ga', split_axis=0, concat_ax...]
    ppermute x5 -> x1, waiting for transfers between devices: 3.77 us -> 0.52 us  [along_ring(): lax.ppermute(x, axis, [(i, (i + step) % count) for i in range(count)])]
  transfers between devices with their start and end apart: 6 -> 1, of which waited for: 5 -> 1; matrix products, arithmetic and copies ran while one was open for 0% -> 0% of each run, Pallas kernels for 2% -> 1%
where the time goes in v4:
time: 137 us
  blocking collectives  127 us (93%)
  Pallas kernels  6.99 us (5%)
  starting transfers between devices  1.94 us (1%)
    all_to_all x1, blocking collectives, shards(): lax.all_to_all(rows.reshape(owners, group, size), 'ga', split_axis=0, con...  76.5 us
    all_to_all x1, blocking collectives, shards(): lax.all_to_all(sent.reshape(owners, 1, -1), 'ga', split_axis=0, concat_ax...  37.3 us
    all_to_all x1, blocking collectives, shards(): mine = lax.all_to_all(sent, 'chip', split_axis=0, concat_axis=0, tiled=True)  13.3 us
    pallas_call x1, Pallas kernels, project(): pl.pallas_call(functools.partial(project_kernel, size=size, owners=owners...  2.81 us
  transfers between devices with their start and end apart: 1, of which 1 were waited for; matrix products, arithmetic and copies ran while one was open for 0% of the time, Pallas kernels for 1%

profile of v4, /device:TPU:40, one launch (start us, length us, event | category | flops | bytes accessed | tf_op | source)
XLA Modules:
  0.0 136.6 jit_solution(1819811737947422467)
XLA Ops:
  0.0 2.3 %spread.1 = f32[256,128]{1,0:T(8,128)S(1)} custom-call(s32[1]{0:T(128)} %bitcast.owner_ref, s32[1]{0:T(128)} %bitcast.1.core_ref, f32[2,1,4096]{2,1,0:T(1,128)} %psi_ref.1, s32[32,1,4096]{2,1,0:T(1,128)} %bitcast.14, bf16[2,128,128]{2,1,0:T(8,128)(2,1)} %constant.20.clone.along_ref), custom_call_target="tpu_custom_call" | custom-call | tf_op jit(solution)/shard_map/spread/pallas_call | solution.py:199
  2.3 0.0 copy-start.4
  2.4 76.5 %all_to_all.15.rows_ref = f32[32,8,128]{2,1,0:T(8,128)S(1)} all-to-all(f32[32,8,128]{2,1,0:T(8,128)S(1)} %bitcast.12), channel_id=1, replica_groups=mesh['pert'=2,'ga'=32,'chip'=4,'core'=2] {'ga'}, dimensions={0} | all-to-all | bytes 262144 | tf_op jit(solution)/shard_map/all_to_all | solution.py:264
  78.8 0.0 copy-done.4
  78.9 0.0 copy-start
  78.9 0.0 copy-start.1
  78.9 0.0 copy-start.2
  78.9 0.0 copy-start.3
  78.9 13.3 %all_to_all.16.mine_ref = f32[4,40,8,128]{3,2,1,0:T(8,128)S(1)} all-to-all(f32[4,40,8,128]{3,2,1,0:T(8,128)S(1)} %fan.1), channel_id=1, replica_groups=mesh['pert'=2,'ga'=32,'chip'=4,'core'=2] {'chip'}, dimensions={0} | all-to-all | bytes 1310720 | tf_op jit(solution)/shard_map/all_to_all | solution.py:266
  92.2 1.9 %collective-permute-start = (f32[4,40,8,128]{3,2,1,0:T(8,128)S(1)}, f32[4,40,8,128]{3,2,1,0:T(8,128)S(1)}, u32[]{:S(2)}, u32[]{:S(2)}) collective-permute-start(f32[4,40,8,128]{3,2,1,0:T(8,128)S(1)} %all_to_all.16.mine_ref), channel_id=1, source_target_pairs={{0,1},{1,0},{2,3},{3,2},{4,5},{5,4},{6,7},{7,6},{8,9},{9,8},{10,11... | collective-permute-start | bytes 1966088 | tf_op jit(solution)/shard_map/ppermute | solution.py:252
  94.2 0.0 copy-done
  94.2 0.0 copy-done.1
  94.2 0.0 copy-done.2
  94.2 0.0 copy-done.3
  94.2 1.5 %apply.1 = (f32[256,128]{1,0:T(8,128)S(1)}, f32[8,128]{1,0:T(8,128)S(1)}) custom-call(f32[256,128]{1,0:T(8,128)S(1)} %bitcast.9, f32[128,4,128]{2,1,0:T(4,128)S(1)} %copy-done.1, bf16[2,128,256]{2,1,0:T(8,128)(2,1)S(1)} %copy-done, bf16[2,256,128]{2,1,0:T(8,128)(2,1)S(1)} %copy-done.3, bf16[2,128,256]{2,1,0:T(8,128)(2,1)S(1)} %copy-done, ...), custom_call_target="tpu_custom_call" | custom-call | tf_op jit(solution)/shard_map/apply/pallas_call | solution.py:220
  95.7 0.5 collective-permute-done.theirs_ref
  96.2 0.3 pair.1
  96.5 0.0 copy-start.5
  96.5 37.3 %all_to_all.17 = f32[32,1,1152]{2,1,0:T(1,128)S(1)} all-to-all(f32[32,1,1152]{2,1,0:T(1,128)S(1)} %bitcast.11), channel_id=1, replica_groups=mesh['pert'=2,'ga'=32,'chip'=4,'core'=2] {'ga'}, dimensions={0} | all-to-all | bytes 294912 | tf_op jit(solution)/shard_map/all_to_all | solution.py:270
  133.8 0.0 copy-done.5
  133.8 2.8 %project.1 = f32[2,32,128]{2,1,0:T(8,128)} custom-call(s32[1]{0:T(128)} %bitcast.owner_ref, s32[1]{0:T(128)} %bitcast.1.core_ref, s32[8]{0:T(128)} %occupied_ref.1, f32[288,128]{1,0:T(8,128)S(1)} %bitcast.10, s32[32,1,4096]{2,1,0:T(1,128)} %bitcast.15, bf16[2,64,256]{2,1,0:T(8,128)(2,1)S(1)} %copy-done.5, f32[4,40,8,128]{3,2,1,0:T(8,128)S(1)} %all_to_all.16.mine_ref, ...), custom_call_target="tpu_custom_call" | custom-call | tf_op jit(solution)/shard_map/project/pallas_call | solution.py:240
  (1 shorter events, 0.0 us)
Async XLA Ops:
  2.3 76.5 %copy-start.4 = (f32[2,1,4096]{2,1,0:T(1,128)S(1)}, f32[2,1,4096]{2,1,0:T(1,128)}, u32[]{:S(2)}) copy-start(f32[2,1,4096]{2,1,0:T(1,128)} %psi_ref.1) | copy-start | bytes 98308
  78.9 15.3 %copy-start = (bf16[2,128,256]{2,1,0:T(8,128)(2,1)S(1)}, bf16[2,128,256]{2,1,0:T(8,128)(2,1)}, u32[]{:S(2)}) copy-start(bf16[2,128,256]{2,1,0:T(8,128)(2,1)} %constant.21.clone.z_ref.back_x_ref) | copy-start | bytes 393220
  78.9 15.3 %copy-start.1 = (f32[128,4,128]{2,1,0:T(4,128)S(1)}, f32[128,4,128]{2,1,0:T(4,128)}, u32[]{:S(2)}) copy-start(f32[128,4,128]{2,1,0:T(4,128)} %potential_ref.1) | copy-start | bytes 786436
  78.9 15.3 %copy-start.2 = (bf16[2,256,128]{2,1,0:T(8,128)(2,1)S(1)}, bf16[2,256,128]{2,1,0:T(8,128)(2,1)}, u32[]{:S(2)}) copy-start(bf16[2,256,128]{2,1,0:T(8,128)(2,1)} %constant.23.clone.back_z_ref) | copy-start | bytes 393220
  78.9 15.3 %copy-start.3 = (bf16[2,256,128]{2,1,0:T(8,128)(2,1)S(1)}, bf16[2,256,128]{2,1,0:T(8,128)(2,1)}, u32[]{:S(2)}) copy-start(bf16[2,256,128]{2,1,0:T(8,128)(2,1)} %constant.22.clone.x_ref) | copy-start | bytes 393220
  92.2 4.0 %collective-permute-start = (f32[4,40,8,128]{3,2,1,0:T(8,128)S(1)}, f32[4,40,8,128]{3,2,1,0:T(8,128)S(1)}, u32[]{:S(2)}, u32[]{:S(2)}) collective-permute-start(f32[4,40,8,128]{3,2,1,0:T(8,128)S(1)} %all_to_all.16.mine_ref), channel_id=1, source_target_pairs={{0,1},{1,0},{2,3},{3,2},{4,5},{5,4},{6,7},{7,6},{8,9},{9,8},{10,11... | collective-permute-start | bytes 1966088 | tf_op jit(solution)/shard_map/ppermute | solution.py:252
  96.5 37.3 %copy-start.5 = (bf16[2,64,256]{2,1,0:T(8,128)(2,1)S(1)}, bf16[2,64,256]{2,1,0:T(8,128)(2,1)}, u32[]{:S(2)}) copy-start(bf16[2,64,256]{2,1,0:T(8,128)(2,1)} %constant.24.clone.along_ref) | copy-start | bytes 196612

commit v5 on v4

--- a/solution.py
+++ b/solution.py
@@ -62,15 +62,22 @@
     return plane // owners * (size // 2) + row, column
 
 
-def picks(index, count):
-    return lax.broadcasted_iota(jnp.int32, (count, index.shape[1]), 0) == index
-
-
 def own_points(owner_ref, points_ref, held_ref, sem):
     return pltpu.make_async_copy(points_ref.at[owner_ref[0]], held_ref, sem)
 
 
-def spread_kernel(owner_ref, core_ref, psi_ref, points_ref, along_ref, out_ref, psi_held, points_held, along_held, sems, *, size, owners):
+def numbered(count, lanes):
+    return lax.broadcasted_iota(jnp.int32, (count, lanes), 0).astype(jnp.float32).astype(jnp.bfloat16)
+
+
+def copied_down(row, count):
+    some = jnp.broadcast_to(row, (16, row.shape[1])).astype(jnp.bfloat16)
+    return jnp.concatenate([some] * (count // 16), axis=0)
+
+
+def spread_kernel(
+    owner_ref, core_ref, psi_ref, points_ref, along_ref, out_ref, psi_held, points_held, along_held, flat_ref, sems, *, size, owners
+):
     del core_ref
     copies = [
         own_points(owner_ref, points_ref, points_held, sems.at[0]),
@@ -79,16 +86,25 @@
     ]
     for copy in copies:
         copy.start()
+    half = size // 2
+    lines = half * half // owners
     copies[0].wait()
     line, column = places(points_held[...], size, owners)
-    half = size // 2
-    lines = half * half // owners
-    at_line = picks(line, lines).astype(jnp.bfloat16)
-    at_column = picks(column, half)
-    zero = jnp.zeros((), jnp.bfloat16)
+    flat_ref[0], flat_ref[1] = line.astype(jnp.float32), column.astype(jnp.float32)
     copies[1].wait()
-    parts = [part for pair in zip(halves(psi_held[0]), halves(psi_held[1])) for part in pair]
-    values = jnp.concatenate([jnp.where(at_column, part, zero) for part in parts], axis=0)
+    for part in range(2):
+        for which, x in enumerate(halves(psi_held[part])):
+            flat_ref[2 + 2 * which + part] = x.astype(jnp.float32)
+    tall, lanes = points_held.shape
+    every_line, every_column = numbered(lines, lanes), numbered(half, lanes)
+    one, zero = jnp.ones((), jnp.bfloat16), jnp.zeros((), jnp.bfloat16)
+    at_line, values = [], []
+    for r in range(tall):
+        at_line.append(jnp.where(every_line == copied_down(flat_ref[0, r : r + 1, :], lines), one, zero))
+        at_column = every_column == copied_down(flat_ref[1, r : r + 1, :], half)
+        parts = [jnp.where(at_column, copied_down(flat_ref[i, r : r + 1, :], half), zero) for i in range(2, 6)]
+        values.append(jnp.concatenate(parts, axis=0))
+    at_line, values = jnp.concatenate(at_line, axis=1), jnp.concatenate(values, axis=1)
     total = lax.dot_general(at_line, values, (((1,), (1,)), ((), ())), preferred_element_type=jnp.float32)
     total = total[:, :size] + total[:, size:]
     around = turned(total)
@@ -151,7 +167,7 @@
 
 
 def project_kernel(
-    owner_ref, core_ref, occupied_ref, rows_ref, points_ref, along_ref, mine_ref, theirs_ref, out_ref, held_ref, sem, *, size, owners, coefs
+    owner_ref, core_ref, occupied_ref, rows_ref, points_ref, along_ref, mine_ref, theirs_ref, out_ref, held_ref, flat_ref, sem, *, size, owners, coefs
 ):
     copy = own_points(owner_ref, points_ref, held_ref, sem)
     copy.start()
@@ -168,12 +184,10 @@
         fields.append(jnp.concatenate([rows, turned(rows)], axis=0))
     lines = dot(along_ref[...], halves(jnp.concatenate(fields, axis=1)))
     lines = jnp.concatenate([lines[:, t * size : (t + 1) * size].T for t in range(planes)], axis=1)
+    lines = jnp.concatenate(halves(lines), axis=1)
     copy.wait()
     line, column = places(held_ref[...], size, owners)
-    at_line = picks(line, lines.shape[1]).astype(jnp.bfloat16)
-    at_column = picks(column, half)
-    found = jnp.dot(jnp.concatenate(halves(lines), axis=1), jnp.concatenate([at_line, at_line], axis=0), preferred_element_type=jnp.float32)
-    applied = [jnp.sum(jnp.where(at_column, found[p * half : (p + 1) * half], 0.0), axis=0, keepdims=True) for p in range(2)]
+    flat_ref[0], flat_ref[1] = line.astype(jnp.float32), column.astype(jnp.float32)
     tall, lanes = out_ref.shape[1:]
     taken = [jnp.zeros((tall, lanes), jnp.float32) for _ in range(2)]
     core = core_ref[0]
@@ -185,9 +199,18 @@
         basis = held[source, owners:].reshape(2, tall, lanes)
         taken[0] = taken[0] + weight_real * basis[0] - weight_imag * basis[1]
         taken[1] = taken[1] + weight_imag * basis[0] + weight_real * basis[1]
-    for p in range(2):
-        for r in range(tall):
-            out_ref[p, r : r + 1, :] = applied[p][:, r * lanes : (r + 1) * lanes] - taken[p][r : r + 1]
+    every_line = numbered(planes * half, lanes)
+    every_column = lax.broadcasted_iota(jnp.int32, (half, lanes), 0).astype(jnp.float32)
+    one, zero = jnp.ones((), jnp.bfloat16), jnp.zeros((), jnp.bfloat16)
+    for r in range(0, tall, 2):
+        at_line = [jnp.where(every_line == copied_down(flat_ref[0, i : i + 1, :], planes * half), one, zero) for i in (r, r + 1)]
+        at_line = jnp.concatenate(at_line, axis=1)
+        found = jnp.dot(lines, jnp.concatenate([at_line, at_line], axis=0), preferred_element_type=jnp.float32)
+        for i in range(2):
+            at_column = every_column == flat_ref[1, r + i : r + i + 1, :]
+            for p in range(2):
+                applied = jnp.where(at_column, found[p * half : (p + 1) * half, i * lanes : (i + 1) * lanes], 0.0)
+                out_ref[p, r + i : r + i + 1, :] = jnp.sum(applied, axis=0, keepdims=True) - taken[p][r + i : r + i + 1]
 
 
 SCALARS = pl.BlockSpec(memory_space=pltpu.SMEM)
@@ -204,6 +227,7 @@
             pltpu.VMEM(psi.shape, psi.dtype),
             pltpu.VMEM(points.shape[1:], points.dtype),
             pltpu.VMEM(table.shape, table.dtype),
+            pltpu.VMEM((6, *points.shape[1:]), jnp.float32),
             pltpu.SemaphoreType.DMA((3,)),
         ],
         interpret=INTERPRET,
@@ -236,12 +260,12 @@
 
 
 def project(owner, core, occupied, rows, points, table, mine, theirs, size, owners, coefs):
-    block = points.shape[2]
+    tall, lanes = points.shape[1:]
     return pl.pallas_call(
         functools.partial(project_kernel, size=size, owners=owners, coefs=coefs),
-        out_shape=jax.ShapeDtypeStruct((2, block // size, size), jnp.float32),
+        out_shape=jax.ShapeDtypeStruct((2, tall, lanes), jnp.float32),
         in_specs=[SCALARS, SCALARS, SCALARS, WHOLE, FAR, WHOLE, WHOLE, WHOLE],
-        scratch_shapes=[pltpu.VMEM(points.shape[1:], points.dtype), pltpu.SemaphoreType.DMA],
+        scratch_shapes=[pltpu.VMEM((tall, lanes), points.dtype), pltpu.VMEM((2, tall, lanes), jnp.float32), pltpu.SemaphoreType.DMA],
         interpret=INTERPRET,
         name="project",
     )(owner, core, occupied, near(rows), points, near(table), near(mine), near(theirs))
@@ -258,8 +282,8 @@
     block = psi.shape[2]
     along_y, along_z, along_x, back_x, back_z, back_y = tables(size, owners)
     owner, core = (lax.axis_index(axis).reshape(1) for axis in ("ga", "core"))
-    points = miller.reshape(-1, 1, block)
-    rows = spread(owner, core, psi, points, along_y, size, owners)
+    points = miller.reshape(-1, block // size, size)
+    rows = spread(owner, core, psi.reshape(2, -1, size), points, along_y, size, owners)
     group = rows.shape[0] // owners
     rows = lax.all_to_all(rows.reshape(owners, group, size), "ga", split_axis=0, concat_axis=0, tiled=True)
     sent = fan(rows, psi.reshape(-1, group, size), chips)

time: 137 us -> 136 us (level)
  no operation moved by 1% of the time
where the time goes in v5:
time: 136 us
  blocking collectives  127 us (93%)
  Pallas kernels  6.4 us (5%)
  starting transfers between devices  1.94 us (1%)
    all_to_all x1, blocking collectives, shards(): lax.all_to_all(rows.reshape(owners, group, size), 'ga', split_axis=0, con...  76.5 us
    all_to_all x1, blocking collectives, shards(): lax.all_to_all(sent.reshape(owners, 1, -1), 'ga', split_axis=0, concat_ax...  37.3 us
    all_to_all x1, blocking collectives, shards(): mine = lax.all_to_all(sent, 'chip', split_axis=0, concat_axis=0, tiled=True)  13.3 us
  transfers between devices with their start and end apart: 1, of which 1 were waited for; matrix products, arithmetic and copies ran while one was open for 0% of the time, Pallas kernels for 1%

profile of v5, /device:TPU:40, one launch (start us, length us, event | category | flops | bytes accessed | tf_op | source)
XLA Modules:
  0.0 136.0 jit_solution(8336774408461323035)
XLA Ops:
  0.0 2.0 %spread.1 = f32[256,128]{1,0:T(8,128)S(1)} custom-call(s32[1]{0:T(128)} %bitcast.owner_ref, s32[1]{0:T(128)} %bitcast.1.core_ref, f32[2,32,128]{2,1,0:T(8,128)} %bitcast.14, s32[32,32,128]{2,1,0:T(8,128)} %bitcast.16, bf16[2,128,128]{2,1,0:T(8,128)(2,1)} %constant.20.clone.along_ref), custom_call_target="tpu_custom_call" | custom-call | tf_op jit(solution)/shard_map/spread/pallas_call | solution.py:222
  2.0 0.0 copy-start.4
  2.0 76.5 %all_to_all.15.rows_ref = f32[32,8,128]{2,1,0:T(8,128)S(1)} all-to-all(f32[32,8,128]{2,1,0:T(8,128)S(1)} %bitcast.13), channel_id=1, replica_groups=mesh['pert'=2,'ga'=32,'chip'=4,'core'=2] {'ga'}, dimensions={0} | all-to-all | bytes 262144 | tf_op jit(solution)/shard_map/all_to_all | solution.py:288
  78.5 0.0 copy-done.4
  78.5 0.0 copy-start
  78.6 0.0 copy-start.1
  78.6 0.0 copy-start.2
  78.6 0.0 copy-start.3
  78.6 13.3 %all_to_all.16.mine_ref = f32[4,40,8,128]{3,2,1,0:T(8,128)S(1)} all-to-all(f32[4,40,8,128]{3,2,1,0:T(8,128)S(1)} %fan.1), channel_id=1, replica_groups=mesh['pert'=2,'ga'=32,'chip'=4,'core'=2] {'chip'}, dimensions={0} | all-to-all | bytes 1310720 | tf_op jit(solution)/shard_map/all_to_all | solution.py:290
  91.9 1.9 %collective-permute-start = (f32[4,40,8,128]{3,2,1,0:T(8,128)S(1)}, f32[4,40,8,128]{3,2,1,0:T(8,128)S(1)}, u32[]{:S(2)}, u32[]{:S(2)}) collective-permute-start(f32[4,40,8,128]{3,2,1,0:T(8,128)S(1)} %all_to_all.16.mine_ref), channel_id=1, source_target_pairs={{0,1},{1,0},{2,3},{3,2},{4,5},{5,4},{6,7},{7,6},{8,9},{9,8},{10,11... | collective-permute-start | bytes 1966088 | tf_op jit(solution)/shard_map/ppermute | solution.py:276
  93.8 0.0 copy-done
  93.8 0.0 copy-done.1
  93.9 0.0 copy-done.2
  93.9 0.0 copy-done.3
  93.9 1.5 %apply.1 = (f32[256,128]{1,0:T(8,128)S(1)}, f32[8,128]{1,0:T(8,128)S(1)}) custom-call(f32[256,128]{1,0:T(8,128)S(1)} %bitcast.10, f32[128,4,128]{2,1,0:T(4,128)S(1)} %copy-done.1, bf16[2,128,256]{2,1,0:T(8,128)(2,1)S(1)} %copy-done, bf16[2,256,128]{2,1,0:T(8,128)(2,1)S(1)} %copy-done.3, bf16[2,128,256]{2,1,0:T(8,128)(2,1)S(1)} %copy-done, ...), custom_call_target="tpu_custom_call" | custom-call | tf_op jit(solution)/shard_map/apply/pallas_call | solution.py:244
  95.4 0.5 collective-permute-done.theirs_ref
  95.9 0.3 pair.1
  96.2 0.0 copy-start.5
  96.2 37.3 %all_to_all.17 = f32[32,1,1152]{2,1,0:T(1,128)S(1)} all-to-all(f32[32,1,1152]{2,1,0:T(1,128)S(1)} %bitcast.12), channel_id=1, replica_groups=mesh['pert'=2,'ga'=32,'chip'=4,'core'=2] {'ga'}, dimensions={0} | all-to-all | bytes 294912 | tf_op jit(solution)/shard_map/all_to_all | solution.py:294
  133.5 0.0 copy-done.5
  133.5 2.6 %project.1 = f32[2,32,128]{2,1,0:T(8,128)} custom-call(s32[1]{0:T(128)} %bitcast.owner_ref, s32[1]{0:T(128)} %bitcast.1.core_ref, s32[8]{0:T(128)} %occupied_ref.1, f32[288,128]{1,0:T(8,128)S(1)} %bitcast.11, s32[32,32,128]{2,1,0:T(8,128)} %bitcast.17, bf16[2,64,256]{2,1,0:T(8,128)(2,1)S(1)} %copy-done.5, f32[4,40,8,128]{3,2,1,0:T(8,128)S(1)} %all_to_all.16.mine_ref, ...), custom_call_target="tpu_custom_call" | custom-call | tf_op jit(solution)/shard_map/project/pallas_call | solution.py:264
  (1 shorter events, 0.0 us)
Async XLA Ops:
  2.0 76.5 %copy-start.4 = (f32[2,1,4096]{2,1,0:T(1,128)S(1)}, f32[2,1,4096]{2,1,0:T(1,128)}, u32[]{:S(2)}) copy-start(f32[2,1,4096]{2,1,0:T(1,128)} %param.10) | copy-start | bytes 98308
  78.5 15.3 %copy-start = (bf16[2,128,256]{2,1,0:T(8,128)(2,1)S(1)}, bf16[2,128,256]{2,1,0:T(8,128)(2,1)}, u32[]{:S(2)}) copy-start(bf16[2,128,256]{2,1,0:T(8,128)(2,1)} %constant.21.clone.z_ref.back_x_ref) | copy-start | bytes 393220
  78.6 15.3 %copy-start.1 = (f32[128,4,128]{2,1,0:T(4,128)S(1)}, f32[128,4,128]{2,1,0:T(4,128)}, u32[]{:S(2)}) copy-start(f32[128,4,128]{2,1,0:T(4,128)} %potential_ref.1) | copy-start | bytes 786436
  78.6 15.3 %copy-start.2 = (bf16[2,256,128]{2,1,0:T(8,128)(2,1)S(1)}, bf16[2,256,128]{2,1,0:T(8,128)(2,1)}, u32[]{:S(2)}) copy-start(bf16[2,256,128]{2,1,0:T(8,128)(2,1)} %constant.23.clone.back_z_ref) | copy-start | bytes 393220
  78.6 15.3 %copy-start.3 = (bf16[2,256,128]{2,1,0:T(8,128)(2,1)S(1)}, bf16[2,256,128]{2,1,0:T(8,128)(2,1)}, u32[]{:S(2)}) copy-start(bf16[2,256,128]{2,1,0:T(8,128)(2,1)} %constant.22.clone.x_ref) | copy-start | bytes 393220
  91.9 4.0 %collective-permute-start = (f32[4,40,8,128]{3,2,1,0:T(8,128)S(1)}, f32[4,40,8,128]{3,2,1,0:T(8,128)S(1)}, u32[]{:S(2)}, u32[]{:S(2)}) collective-permute-start(f32[4,40,8,128]{3,2,1,0:T(8,128)S(1)} %all_to_all.16.mine_ref), channel_id=1, source_target_pairs={{0,1},{1,0},{2,3},{3,2},{4,5},{5,4},{6,7},{7,6},{8,9},{9,8},{10,11... | collective-permute-start | bytes 1966088 | tf_op jit(solution)/shard_map/ppermute | solution.py:276
  96.2 37.3 %copy-start.5 = (bf16[2,64,256]{2,1,0:T(8,128)(2,1)S(1)}, bf16[2,64,256]{2,1,0:T(8,128)(2,1)}, u32[]{:S(2)}) copy-start(bf16[2,64,256]{2,1,0:T(8,128)(2,1)} %constant.24.clone.along_ref) | copy-start | bytes 196612

commit v6 on v5

--- a/solution.py
+++ b/solution.py
@@ -76,9 +76,8 @@
 
 
 def spread_kernel(
-    owner_ref, core_ref, psi_ref, points_ref, along_ref, out_ref, psi_held, points_held, along_held, flat_ref, sems, *, size, owners
+    owner_ref, psi_ref, points_ref, along_ref, out_ref, psi_held, points_held, along_held, flat_ref, sems, *, size, owners
 ):
-    del core_ref
     copies = [
         own_points(owner_ref, points_ref, points_held, sems.at[0]),
         pltpu.make_async_copy(psi_ref, psi_held, sems.at[1]),
@@ -116,10 +115,19 @@
         out_ref[pl.ds(t, size, stride=planes), :] = rows[:, t * size : (t + 1) * size]
 
 
-def fan_kernel(rows_ref, psi_ref, out_ref):
+def fan_kernel(rows_ref, out_ref):
     for i in range(out_ref.shape[0]):
-        out_ref[i, : rows_ref.shape[0]] = rows_ref[...]
-        out_ref[i, rows_ref.shape[0] :] = psi_ref[...]
+        out_ref[i] = rows_ref[...]
+
+
+def carry_kernel(x_ref, after_ref, out_ref):
+    del after_ref
+    out_ref[...] = x_ref[...]
+
+
+def join_kernel(*refs):
+    for i, ref in enumerate(refs[:-1]):
+        refs[-1][i] = ref[...]
 
 
 def apply_kernel(field_ref, potential_ref, z_ref, x_ref, back_x_ref, back_z_ref, mine_ref, out_ref, sums_ref, wide_ref, *, size, owners):
@@ -144,20 +152,20 @@
                 wide_ref[part, pl.ds(y * per + t, owners, stride=group), :] = back[first : first + owners, y * size : (y + 1) * size]
     product = dot(halves(jnp.concatenate([wide_ref[0], wide_ref[1]], axis=1)), back_z_ref[...])
     out_ref[...] = product
-    sums_ref[...] = overlaps(mine_ref, product, owners)
-
-
-def overlaps(fields_ref, product, owners):
+    sums_ref[...] = overlaps(mine_ref, product)
+
+
+def overlaps(fields_ref, product):
     half = product.shape[1] // 2
     crossed = jnp.concatenate([product[:, half:], -product[:, :half]], axis=1)
-    fields = [fields_ref[m, :owners].reshape(product.shape) for m in range(fields_ref.shape[0])]
+    fields = [fields_ref[m].reshape(product.shape) for m in range(fields_ref.shape[0])]
     return jnp.concatenate([jnp.sum(f * other, axis=0, keepdims=True) for other in (product, crossed) for f in fields], axis=0)
 
 
 def pair_kernel(theirs_ref, product_ref, sums_ref, out_ref, *, owners):
     lanes = product_ref.shape[1]
     group = product_ref.shape[0] // owners
-    sums = jnp.concatenate([sums_ref[...], overlaps(theirs_ref, product_ref[...], owners)], axis=0)
+    sums = jnp.concatenate([sums_ref[...], overlaps(theirs_ref, product_ref[...])], axis=0)
     sums = jnp.dot(sums, jnp.ones((lanes, lanes), jnp.float32), precision=highest, preferred_element_type=jnp.float32)
     on_diagonal = lax.broadcasted_iota(jnp.int32, sums.shape, 0) == lax.broadcasted_iota(jnp.int32, sums.shape, 1)
     row = jnp.sum(jnp.where(on_diagonal, sums, 0.0), axis=0, keepdims=True)
@@ -166,11 +174,24 @@
     out_ref[pl.ds(group, owners, stride=group + 1), :] = jnp.broadcast_to(row, (owners, lanes))
 
 
-def project_kernel(
-    owner_ref, core_ref, occupied_ref, rows_ref, points_ref, along_ref, mine_ref, theirs_ref, out_ref, held_ref, flat_ref, sem, *, size, owners, coefs
-):
+def sift_kernel(owner_ref, points_ref, after_ref, line_ref, column_ref, held_ref, flat_ref, sem, *, size, owners):
+    del after_ref
     copy = own_points(owner_ref, points_ref, held_ref, sem)
     copy.start()
+    copy.wait()
+    line, column = places(held_ref[...], size, owners)
+    flat_ref[...], column_ref[...] = line.astype(jnp.float32), column.astype(jnp.float32)
+    tall, lanes = held_ref.shape
+    lines = line_ref.shape[0]
+    every_line = numbered(lines, lanes)
+    one, zero = jnp.ones((), jnp.bfloat16), jnp.zeros((), jnp.bfloat16)
+    for r in range(tall):
+        line_ref[:, r * lanes : (r + 1) * lanes] = jnp.where(every_line == copied_down(flat_ref[r : r + 1, :], lines), one, zero)
+
+
+def project_kernel(
+    chip_ref, core_ref, occupied_ref, rows_ref, line_ref, column_ref, along_ref, mine_ref, theirs_ref, out_ref, *, size, owners, coefs
+):
     chips = mine_ref.shape[0]
     bands = 2 * chips
     half = size // 2
@@ -185,29 +206,23 @@
     lines = dot(along_ref[...], halves(jnp.concatenate(fields, axis=1)))
     lines = jnp.concatenate([lines[:, t * size : (t + 1) * size].T for t in range(planes)], axis=1)
     lines = jnp.concatenate(halves(lines), axis=1)
-    copy.wait()
-    line, column = places(held_ref[...], size, owners)
-    flat_ref[0], flat_ref[1] = line.astype(jnp.float32), column.astype(jnp.float32)
     tall, lanes = out_ref.shape[1:]
     taken = [jnp.zeros((tall, lanes), jnp.float32) for _ in range(2)]
-    core = core_ref[0]
+    chip, core = chip_ref[0], core_ref[0]
     for m in range(bands):
         held, first, source, from_core = (mine_ref, 0, m, core) if m < chips else (theirs_ref, 2 * chips, m - chips, 1 - core)
         share = occupied_ref[2 * source + from_core].astype(jnp.float32) * (1.0 / coefs)
         weight_real = sums[:, first + source : first + source + 1] * share
         weight_imag = sums[:, first + chips + source : first + chips + source + 1] * share
-        basis = held[source, owners:].reshape(2, tall, lanes)
+        basis = held[lax.rem(chip + chips - source, chips)].reshape(2, tall, lanes)
         taken[0] = taken[0] + weight_real * basis[0] - weight_imag * basis[1]
         taken[1] = taken[1] + weight_imag * basis[0] + weight_real * basis[1]
-    every_line = numbered(planes * half, lanes)
     every_column = lax.broadcasted_iota(jnp.int32, (half, lanes), 0).astype(jnp.float32)
-    one, zero = jnp.ones((), jnp.bfloat16), jnp.zeros((), jnp.bfloat16)
     for r in range(0, tall, 2):
-        at_line = [jnp.where(every_line == copied_down(flat_ref[0, i : i + 1, :], planes * half), one, zero) for i in (r, r + 1)]
-        at_line = jnp.concatenate(at_line, axis=1)
+        at_line = line_ref[:, r * lanes : (r + 2) * lanes]
         found = jnp.dot(lines, jnp.concatenate([at_line, at_line], axis=0), preferred_element_type=jnp.float32)
         for i in range(2):
-            at_column = every_column == flat_ref[1, r + i : r + i + 1, :]
+            at_column = every_column == column_ref[r + i : r + i + 1, :]
             for p in range(2):
                 applied = jnp.where(at_column, found[p * half : (p + 1) * half, i * lanes : (i + 1) * lanes], 0.0)
                 out_ref[p, r + i : r + i + 1, :] = jnp.sum(applied, axis=0, keepdims=True) - taken[p][r + i : r + i + 1]
@@ -218,11 +233,11 @@
 WHOLE = pl.BlockSpec(memory_space=pltpu.VMEM)
 
 
-def spread(owner, core, psi, points, table, size, owners):
+def spread(owner, psi, points, table, size, owners):
     return pl.pallas_call(
         functools.partial(spread_kernel, size=size, owners=owners),
         out_shape=made((size * (size // (2 * owners)), size)),
-        in_specs=[SCALARS, SCALARS, FAR, FAR, FAR],
+        in_specs=[SCALARS, FAR, FAR, FAR],
         scratch_shapes=[
             pltpu.VMEM(psi.shape, psi.dtype),
             pltpu.VMEM(points.shape[1:], points.dtype),
@@ -232,12 +247,31 @@
         ],
         interpret=INTERPRET,
         name="spread",
-    )(owner, core, psi, points, table)
-
-
-def fan(rows, psi, copies):
-    shape = (copies, rows.shape[0] + psi.shape[0], *rows.shape[1:])
-    return pl.pallas_call(fan_kernel, out_shape=made(shape), interpret=INTERPRET, name="fan")(near(rows), near(psi))
+    )(owner, psi, points, table)
+
+
+def fan(rows, copies):
+    return pl.pallas_call(fan_kernel, out_shape=made((copies, *rows.shape)), interpret=INTERPRET, name="fan")(near(rows))
+
+
+def carry(x, after):
+    return pl.pallas_call(carry_kernel, out_shape=made(x.shape), in_specs=[WHOLE, FAR], interpret=INTERPRET, name="carry")(near(x), after)
+
+
+def join(parts):
+    return pl.pallas_call(join_kernel, out_shape=made((len(parts), *parts[0].shape)), interpret=INTERPRET, name="join")(*map(near, parts))
+
+
+def sift(owner, points, after, size, owners):
+    tall, lanes = points.shape[1:]
+    return pl.pallas_call(
+        functools.partial(sift_kernel, size=size, owners=owners),
+        out_shape=(made((size // 2 * (size // (2 * owners)), tall * lanes), jnp.bfloat16), made((tall, lanes))),
+        in_specs=[SCALARS, FAR, FAR],
+        scratch_shapes=[pltpu.VMEM((tall, lanes), points.dtype), pltpu.VMEM((tall, lanes), jnp.float32), pltpu.SemaphoreType.DMA],
+        interpret=INTERPRET,
+        name="sift",
+    )(owner, points, after)
 
 
 def apply(field, potential, along_z, along_x, back_x, back_z, mine, size, owners):
@@ -259,16 +293,14 @@
     )(*map(near, (theirs, product, sums)))
 
 
-def project(owner, core, occupied, rows, points, table, mine, theirs, size, owners, coefs):
-    tall, lanes = points.shape[1:]
+def project(place, occupied, rows, picked, table, mine, theirs, size, owners, coefs):
     return pl.pallas_call(
         functools.partial(project_kernel, size=size, owners=owners, coefs=coefs),
-        out_shape=jax.ShapeDtypeStruct((2, tall, lanes), jnp.float32),
-        in_specs=[SCALARS, SCALARS, SCALARS, WHOLE, FAR, WHOLE, WHOLE, WHOLE],
-        scratch_shapes=[pltpu.VMEM((tall, lanes), points.dtype), pltpu.VMEM((2, tall, lanes), jnp.float32), pltpu.SemaphoreType.DMA],
+        out_shape=jax.ShapeDtypeStruct((2, *picked[1].shape), jnp.float32),
+        in_specs=[SCALARS, SCALARS, SCALARS] + [WHOLE] * 6,
         interpret=INTERPRET,
         name="project",
-    )(owner, core, occupied, near(rows), points, near(table), near(mine), near(theirs))
+    )(*place, occupied, *map(near, (rows, *picked, table, mine, theirs)))
 
 
 def along_ring(x, axis, step):
@@ -281,18 +313,21 @@
     owners, chips = lax.axis_size("ga"), lax.axis_size("chip")
     block = psi.shape[2]
     along_y, along_z, along_x, back_x, back_z, back_y = tables(size, owners)
-    owner, core = (lax.axis_index(axis).reshape(1) for axis in ("ga", "core"))
+    owner, *place = (lax.axis_index(axis).reshape(1) for axis in ("ga", "chip", "core"))
     points = miller.reshape(-1, block // size, size)
-    rows = spread(owner, core, psi.reshape(2, -1, size), points, along_y, size, owners)
+    rows = spread(owner, psi.reshape(2, -1, size), points, along_y, size, owners)
     group = rows.shape[0] // owners
     rows = lax.all_to_all(rows.reshape(owners, group, size), "ga", split_axis=0, concat_axis=0, tiled=True)
-    sent = fan(rows, psi.reshape(-1, group, size), chips)
-    mine = lax.all_to_all(sent, "chip", split_axis=0, concat_axis=0, tiled=True)
+    mine = lax.all_to_all(fan(rows, chips), "chip", split_axis=0, concat_axis=0, tiled=True)
     theirs = along_ring(mine, "core", 1)
     product, sums = apply(rows.reshape(-1, size), potential, along_z, along_x, back_x, back_z, mine, size, owners)
     sent = pair(theirs, product, sums, owners)
     rows = lax.all_to_all(sent.reshape(owners, 1, -1), "ga", split_axis=0, concat_axis=0, tiled=True).reshape(sent.shape)
-    out = project(owner, core, occupied, rows, points, back_y, mine, theirs, size, owners, miller.shape[0])
+    own = carry(psi.reshape(-1, size), sent)
+    basis = join([own] + [along_ring(own, "chip", step) for step in range(1, chips)])
+    other_basis = along_ring(basis, "core", 1)
+    picked = sift(owner, points, sent, size, owners)
+    out = project(place, occupied, rows, picked, back_y, basis, other_basis, size, owners, miller.shape[0])
     return out.reshape(2, 1, block)
 
 

time: 136 us -> 137 us (level)
  blocking collectives: 127 us -> 89.1 us
  waiting for transfers between devices: 0.52 us -> 20.8 us
  starting transfers between devices: 1.94 us -> 18.1 us
  Pallas kernels: 6.4 us -> 7.84 us
    all_to_all x2 -> x1, blocking collectives: 50.6 us -> 12.6 us  [shards(): lax.all_to_all(fan(rows, chips), 'chip', split_axis=0, concat_axis=0, til...]
    all_to_all x0 -> x1, waiting for transfers between devices: none -> 17.1 us  [shards(): lax.all_to_all(sent.reshape(owners, 1, -1), 'ga', split_axis=0, concat_ax...]
    ppermute x1 -> x5, starting transfers between devices: 1.94 us -> 13.2 us  [along_ring(): lax.ppermute(x, axis, [(i, (i + step) % count) for i in range(count)])]
    all_to_all x0 -> x1, starting transfers between devices: none -> 4.91 us  [shards(): lax.all_to_all(sent.reshape(owners, 1, -1), 'ga', split_axis=0, concat_ax...]
    ppermute x1 -> x5, waiting for transfers between devices: 0.52 us -> 3.65 us  [along_ring(): lax.ppermute(x, axis, [(i, (i + step) % count) for i in range(count)])]
  transfers between devices with their start and end apart: 1 -> 6, of which waited for: 1 -> 5; matrix products, arithmetic and copies ran while one was open for 0% -> 0% of each run, Pallas kernels for 1% -> 2%
where the time goes in v6:
time: 137 us; the launch traced here: 136 us
  blocking collectives  89.1 us (65%)
  waiting for transfers between devices  20.8 us (15%)
  starting transfers between devices  18.1 us (13%)
  Pallas kernels  7.84 us (6%)
    all_to_all x1, blocking collectives, shards(): lax.all_to_all(rows.reshape(owners, group, size), 'ga', split_axis=0, con...  76.5 us
    all_to_all x1, waiting for transfers between devices, shards(): lax.all_to_all(sent.reshape(owners, 1, -1), 'ga', split_axis=0, concat_ax...  17.1 us
    ppermute x5, starting transfers between devices, along_ring(): lax.ppermute(x, axis, [(i, (i + step) % count) for i in range(count)])  13.2 us
    all_to_all x1, blocking collectives, shards(): lax.all_to_all(fan(rows, chips), 'chip', split_axis=0, concat_axis=0, til...  12.6 us
    all_to_all x1, starting transfers between devices, shards(): lax.all_to_all(sent.reshape(owners, 1, -1), 'ga', split_axis=0, concat_ax...  4.91 us
    ppermute x5, waiting for transfers between devices, along_ring(): lax.ppermute(x, axis, [(i, (i + step) % count) for i in range(count)])  3.65 us
  transfers between devices with their start and end apart: 6, of which 5 were waited for; matrix products, arithmetic and copies ran while one was open for 0% of the time, Pallas kernels for 2%

profile of v6, /device:TPU:40, one launch (start us, length us, event | category | flops | bytes accessed | tf_op | source)
XLA Modules:
  0.0 136.0 jit_solution(13062995729915102337)
XLA Ops:
  0.0 2.0 %spread.1 = f32[256,128]{1,0:T(8,128)S(1)} custom-call(s32[1]{0:T(128)} %bitcast.2.owner_ref, f32[2,32,128]{2,1,0:T(8,128)} %bitcast.14, s32[32,32,128]{2,1,0:T(8,128)} %bitcast.16, bf16[2,128,128]{2,1,0:T(8,128)(2,1)} %constant.23.clone.along_ref), custom_call_target="tpu_custom_call" | custom-call | tf_op jit(solution)/shard_map/spread/pallas_call | solution.py:237
  2.0 76.5 %all_to_all.15.rows_ref = f32[32,8,128]{2,1,0:T(8,128)S(1)} all-to-all(f32[32,8,128]{2,1,0:T(8,128)S(1)} %bitcast.13), channel_id=1, replica_groups=mesh['pert'=2,'ga'=32,'chip'=4,'core'=2] {'ga'}, dimensions={0} | all-to-all | bytes 262144 | tf_op jit(solution)/shard_map/all_to_all | solution.py:320
  78.5 0.0 copy-start
  78.5 0.0 copy-start.1
  78.5 0.0 copy-start.3
  78.6 0.0 copy-start.4
  78.6 12.6 %all_to_all.16.mine_ref = f32[4,32,8,128]{3,2,1,0:T(8,128)S(1)} all-to-all(f32[4,32,8,128]{3,2,1,0:T(8,128)S(1)} %fan.1), channel_id=1, replica_groups=mesh['pert'=2,'ga'=32,'chip'=4,'core'=2] {'chip'}, dimensions={0} | all-to-all | bytes 1048576 | tf_op jit(solution)/shard_map/all_to_all | solution.py:321
  91.2 1.9 %collective-permute-start = (f32[4,32,8,128]{3,2,1,0:T(8,128)S(1)}, f32[4,32,8,128]{3,2,1,0:T(8,128)S(1)}, u32[]{:S(2)}, u32[]{:S(2)}) collective-permute-start(f32[4,32,8,128]{3,2,1,0:T(8,128)S(1)} %all_to_all.16.mine_ref), channel_id=1, source_target_pairs={{0,1},{1,0},{2,3},{3,2},{4,5},{5,4},{6,7},{7,6},{8,9},{9,8},{10,11... | collective-permute-start | bytes 1572872 | tf_op jit(solution)/shard_map/ppermute | solution.py:308
  93.1 0.0 copy-done
  93.1 0.0 copy-done.1
  93.1 0.0 copy-done.3
  93.1 0.0 copy-done.4
  93.1 1.5 %apply.1 = (f32[256,128]{1,0:T(8,128)S(1)}, f32[8,128]{1,0:T(8,128)S(1)}) custom-call(f32[256,128]{1,0:T(8,128)S(1)} %bitcast.11, f32[128,4,128]{2,1,0:T(4,128)S(1)} %copy-done.1, bf16[2,128,256]{2,1,0:T(8,128)(2,1)S(1)} %copy-done, bf16[2,256,128]{2,1,0:T(8,128)(2,1)S(1)} %copy-done.3, bf16[2,128,256]{2,1,0:T(8,128)(2,1)S(1)} %copy-done, ...), custom_call_target="tpu_custom_call" | custom-call | tf_op jit(solution)/shard_map/apply/pallas_call | solution.py:278
  94.6 0.3 collective-permute-done.theirs_ref
  95.0 1.0 pair.1.after_ref
  95.9 0.0 copy-start.2
  95.9 4.9 %all-to-all-start.2 = ((f32[32,1,1152]{2,1,0:T(1,128)}), f32[32,1,1152]{2,1,0:T(1,128)S(1)}, u32[]{:S(2)}, u32[]{:S(2)}) async-start(f32[32,1,1152]{2,1,0:T(1,128)} %bitcast.7), calls=%async_computation.2 | async-start | bytes 294912 | tf_op jit(solution)/shard_map/all_to_all | solution.py:325
  100.9 0.0 copy-done.2
  100.9 2.5 %collective-permute-start.1 = (f32[64,128]{1,0:T(8,128)S(1)}, f32[64,128]{1,0:T(8,128)S(1)}, u32[]{:S(2)}, u32[]{:S(2)}) collective-permute-start(f32[64,128]{1,0:T(8,128)S(1)} %carry.1.refs_0_), channel_id=1, source_target_pairs={{0,2},{2,4},{4,6},{6,0},{1,3},{3,5},{5,7},{7,1},{8,10},{10,12},{12... | collective-permute-start | bytes 98312 | tf_op jit(solution)/shard_map/ppermute | solution.py:308
  103.4 4.0 %collective-permute-start.2 = (f32[64,128]{1,0:T(8,128)S(1)}, f32[64,128]{1,0:T(8,128)S(1)}, u32[]{:S(2)}, u32[]{:S(2)}) collective-permute-start(f32[64,128]{1,0:T(8,128)S(1)} %carry.1.refs_0_), channel_id=1, source_target_pairs={{0,4},{2,6},{4,0},{6,2},{1,5},{3,7},{5,1},{7,3},{8,12},{10,14},{12... | collective-permute-start | bytes 98312 | tf_op jit(solution)/shard_map/ppermute | solution.py:308
  107.4 2.8 %collective-permute-start.3 = (f32[64,128]{1,0:T(8,128)S(1)}, f32[64,128]{1,0:T(8,128)S(1)}, u32[]{:S(2)}, u32[]{:S(2)}) collective-permute-start(f32[64,128]{1,0:T(8,128)S(1)} %carry.1.refs_0_), channel_id=1, source_target_pairs={{0,6},{2,0},{4,2},{6,4},{1,7},{3,1},{5,3},{7,5},{8,14},{10,8},{12,... | collective-permute-start | bytes 98312 | tf_op jit(solution)/shard_map/ppermute | solution.py:308
  110.2 0.0 collective-permute-done.1.refs_1_
  110.2 0.6 collective-permute-done.2.refs_2_
  110.7 2.5 %collective-permute-done.3.refs_3_ = f32[64,128]{1,0:T(8,128)S(1)} collective-permute-done((f32[64,128]{1,0:T(8,128)S(1)}, f32[64,128]{1,0:T(8,128)S(1)}, u32[]{:S(2)}, u32[]{:S(2)}) %collective-permute-start.3) | collective-permute-done | bytes 32800 | tf_op jit(solution)/shard_map/ppermute | solution.py:308
  113.3 2.0 %collective-permute-start.4 = (f32[4,64,128]{2,1,0:T(8,128)S(1)}, f32[4,64,128]{2,1,0:T(8,128)S(1)}, u32[]{:S(2)}, u32[]{:S(2)}) collective-permute-start(f32[4,64,128]{2,1,0:T(8,128)S(1)} %join.1.mine_ref), channel_id=1, source_target_pairs={{0,1},{1,0},{2,3},{3,2},{4,5},{5,4},{6,7},{7,6},{8,9},{9,8},{10,11... | collective-permute-start | bytes 393224 | tf_op jit(solution)/shard_map/ppermute | solution.py:308
  115.2 0.0 copy-start.5
  115.2 1.0 sift.1
  116.3 0.3 collective-permute-done.4.theirs_ref
  116.5 17.1 %all-to-all-done.2 = f32[32,1,1152]{2,1,0:T(1,128)S(1)} async-done(((f32[32,1,1152]{2,1,0:T(1,128)}), f32[32,1,1152]{2,1,0:T(1,128)S(1)}, u32[]{:S(2)}, u32[]{:S(2)}) %all-to-all-start.2) | async-done | bytes 147488 | tf_op jit(solution)/shard_map/all_to_all | solution.py:325
  133.7 0.0 copy-done.5
  133.7 2.3 %project.1 = f32[2,32,128]{2,1,0:T(8,128)} custom-call(s32[1]{0:T(128)} %bitcast.chip_ref, s32[1]{0:T(128)} %bitcast.1.core_ref, s32[8]{0:T(128)} %occupied_ref.1, f32[288,128]{1,0:T(8,128)S(1)} %bitcast.12, bf16[128,4096]{1,0:T(8,128)(2,1)S(1)} %get-tuple-element.11.line_ref, f32[32,128]{1,0:T(8,128)S(1)} %get-tuple-element.12.column_ref, ...), custom_call_target="tpu_custom_call" | custom-call | tf_op jit(solution)/shard_map/project/pallas_call | solution.py:297
  (3 shorter events, 0.0 us)
Async XLA Ops:
  78.5 14.6 %copy-start = (bf16[2,128,256]{2,1,0:T(8,128)(2,1)S(1)}, bf16[2,128,256]{2,1,0:T(8,128)(2,1)}, u32[]{:S(2)}) copy-start(bf16[2,128,256]{2,1,0:T(8,128)(2,1)} %constant.24.clone.z_ref.back_x_ref) | copy-start | bytes 393220
  78.5 14.6 %copy-start.1 = (f32[128,4,128]{2,1,0:T(4,128)S(1)}, f32[128,4,128]{2,1,0:T(4,128)}, u32[]{:S(2)}) copy-start(f32[128,4,128]{2,1,0:T(4,128)} %potential_ref.1) | copy-start | bytes 786436
  78.5 14.6 %copy-start.3 = (bf16[2,256,128]{2,1,0:T(8,128)(2,1)S(1)}, bf16[2,256,128]{2,1,0:T(8,128)(2,1)}, u32[]{:S(2)}) copy-start(bf16[2,256,128]{2,1,0:T(8,128)(2,1)} %constant.25.clone.x_ref) | copy-start | bytes 393220
  78.6 14.6 %copy-start.4 = (bf16[2,256,128]{2,1,0:T(8,128)(2,1)S(1)}, bf16[2,256,128]{2,1,0:T(8,128)(2,1)}, u32[]{:S(2)}) copy-start(bf16[2,256,128]{2,1,0:T(8,128)(2,1)} %constant.26.clone.back_z_ref) | copy-start | bytes 393220
  91.2 3.8 %collective-permute-start = (f32[4,32,8,128]{3,2,1,0:T(8,128)S(1)}, f32[4,32,8,128]{3,2,1,0:T(8,128)S(1)}, u32[]{:S(2)}, u32[]{:S(2)}) collective-permute-start(f32[4,32,8,128]{3,2,1,0:T(8,128)S(1)} %all_to_all.16.mine_ref), channel_id=1, source_target_pairs={{0,1},{1,0},{2,3},{3,2},{4,5},{5,4},{6,7},{7,6},{8,9},{9,8},{10,11... | collective-permute-start | bytes 1572872 | tf_op jit(solution)/shard_map/ppermute | solution.py:308
  95.9 4.9 %copy-start.2 = (f32[2,1,4096]{2,1,0:T(1,128)S(1)}, f32[2,1,4096]{2,1,0:T(1,128)}, u32[]{:S(2)}) copy-start(f32[2,1,4096]{2,1,0:T(1,128)} %param.10) | copy-start | bytes 98308
  95.9 37.7 %all-to-all-start.2 = ((f32[32,1,1152]{2,1,0:T(1,128)}), f32[32,1,1152]{2,1,0:T(1,128)S(1)}, u32[]{:S(2)}, u32[]{:S(2)}) async-start(f32[32,1,1152]{2,1,0:T(1,128)} %bitcast.7), calls=%async_computation.2 | async-start | bytes 294912 | tf_op jit(solution)/shard_map/all_to_all | solution.py:325
  100.9 9.3 %collective-permute-start.1 = (f32[64,128]{1,0:T(8,128)S(1)}, f32[64,128]{1,0:T(8,128)S(1)}, u32[]{:S(2)}, u32[]{:S(2)}) collective-permute-start(f32[64,128]{1,0:T(8,128)S(1)} %carry.1.refs_0_), channel_id=1, source_target_pairs={{0,2},{2,4},{4,6},{6,0},{1,3},{3,5},{5,7},{7,1},{8,10},{10,12},{12... | collective-permute-start | bytes 98312 | tf_op jit(solution)/shard_map/ppermute | solution.py:308
  103.4 7.3 %collective-permute-start.2 = (f32[64,128]{1,0:T(8,128)S(1)}, f32[64,128]{1,0:T(8,128)S(1)}, u32[]{:S(2)}, u32[]{:S(2)}) collective-permute-start(f32[64,128]{1,0:T(8,128)S(1)} %carry.1.refs_0_), channel_id=1, source_target_pairs={{0,4},{2,6},{4,0},{6,2},{1,5},{3,7},{5,1},{7,3},{8,12},{10,14},{12... | collective-permute-start | bytes 98312 | tf_op jit(solution)/shard_map/ppermute | solution.py:308
  107.4 5.8 %collective-permute-start.3 = (f32[64,128]{1,0:T(8,128)S(1)}, f32[64,128]{1,0:T(8,128)S(1)}, u32[]{:S(2)}, u32[]{:S(2)}) collective-permute-start(f32[64,128]{1,0:T(8,128)S(1)} %carry.1.refs_0_), channel_id=1, source_target_pairs={{0,6},{2,0},{4,2},{6,4},{1,7},{3,1},{5,3},{7,5},{8,14},{10,8},{12,... | collective-permute-start | bytes 98312 | tf_op jit(solution)/shard_map/ppermute | solution.py:308
  113.3 3.3 %collective-permute-start.4 = (f32[4,64,128]{2,1,0:T(8,128)S(1)}, f32[4,64,128]{2,1,0:T(8,128)S(1)}, u32[]{:S(2)}, u32[]{:S(2)}) collective-permute-start(f32[4,64,128]{2,1,0:T(8,128)S(1)} %join.1.mine_ref), channel_id=1, source_target_pairs={{0,1},{1,0},{2,3},{3,2},{4,5},{5,4},{6,7},{7,6},{8,9},{9,8},{10,11... | collective-permute-start | bytes 393224 | tf_op jit(solution)/shard_map/ppermute | solution.py:308
  115.2 18.4 %copy-start.5 = (bf16[2,64,256]{2,1,0:T(8,128)(2,1)S(1)}, bf16[2,64,256]{2,1,0:T(8,128)(2,1)}, u32[]{:S(2)}) copy-start(bf16[2,64,256]{2,1,0:T(8,128)(2,1)} %constant.27.clone.along_ref) | copy-start | bytes 196612

commit v7 on v5

--- a/solution.py
+++ b/solution.py
@@ -36,15 +36,22 @@
     return jnp.concatenate([-x[:, half:], x[:, :half]], axis=1)
 
 
+def ring(owners):
+    return [(i + owners // 2) % owners for i in range(owners)]
+
+
 def tables(size, owners):
+    order = np.asarray(ring(owners))
     signed = np.arange(size // 2) - size // 4
     angle = 2.0 * np.pi / size * (np.arange(size)[:, None] * signed[None, :] % size)
     cosine, sine = np.cos(angle), np.sin(angle)
-    along_y = np.concatenate([cosine, sine], axis=1)
+    by_owner = [part.reshape(owners, size // owners, -1)[order] for part in (cosine, sine)]
+    along_y = np.concatenate([part.reshape(size, -1) for part in by_owner], axis=1)
     along_z = np.block([[cosine.T, sine.T], [-sine.T, cosine.T]])
-    along_x = np.block([[cosine, -sine], [sine, cosine]])
-    back = [part.reshape(owners, size // owners, -1).transpose(2, 1, 0).reshape(size // 2, size) for part in (cosine, -sine)]
-    back_y = np.concatenate(back, axis=1)
+    planes = [part.reshape(size, -1, owners)[:, :, order].reshape(size, -1) for part in (cosine, sine)]
+    along_x = np.block([[planes[0], -planes[1]], [planes[1], planes[0]]])
+    back = [part.transpose(2, 1, 0).reshape(size // 2, size) for part in by_owner]
+    back_y = np.concatenate([back[0], -back[1]], axis=1)
 
     def both(table):
         table = np.asarray(table, np.float32)
@@ -271,6 +278,11 @@
     )(owner, core, occupied, near(rows), points, near(table), near(mine), near(theirs))
 
 
+def exchanged(x, axis):
+    groups = [ring(lax.axis_size(axis))]
+    return lax.all_to_all(x, axis, split_axis=0, concat_axis=0, axis_index_groups=groups, tiled=True)
+
+
 def along_ring(x, axis, step):
     count = lax.axis_size(axis)
     return lax.ppermute(x, axis, [(i, (i + step) % count) for i in range(count)])
@@ -285,13 +297,13 @@
     points = miller.reshape(-1, block // size, size)
     rows = spread(owner, core, psi.reshape(2, -1, size), points, along_y, size, owners)
     group = rows.shape[0] // owners
-    rows = lax.all_to_all(rows.reshape(owners, group, size), "ga", split_axis=0, concat_axis=0, tiled=True)
+    rows = exchanged(rows.reshape(owners, group, size), "ga")
     sent = fan(rows, psi.reshape(-1, group, size), chips)
     mine = lax.all_to_all(sent, "chip", split_axis=0, concat_axis=0, tiled=True)
     theirs = along_ring(mine, "core", 1)
     product, sums = apply(rows.reshape(-1, size), potential, along_z, along_x, back_x, back_z, mine, size, owners)
     sent = pair(theirs, product, sums, owners)
-    rows = lax.all_to_all(sent.reshape(owners, 1, -1), "ga", split_axis=0, concat_axis=0, tiled=True).reshape(sent.shape)
+    rows = exchanged(sent.reshape(owners, 1, -1), "ga").reshape(sent.shape)
     out = project(owner, core, occupied, rows, points, back_y, mine, theirs, size, owners, miller.shape[0])
     return out.reshape(2, 1, block)
 

time: 136 us -> 134 us (0.985)
  blocking collectives: 127 us -> 125 us
    all_to_all x2, blocking collectives: 114 us -> 110 us  [exchanged(): lax.all_to_all(x, axis, split_axis=0, concat_axis=0, axis_index_groups=gr...]
    all_to_all x1, blocking collectives: 13.3 us -> 15.1 us  [shards(): mine = lax.all_to_all(sent, 'chip', split_axis=0, concat_axis=0, tiled=True)]
where the time goes in v7:
time: 134 us
  blocking collectives  125 us (93%)
  Pallas kernels  6.4 us (5%)
  starting transfers between devices  1.94 us (1%)
    all_to_all x2, blocking collectives, exchanged(): lax.all_to_all(x, axis, split_axis=0, concat_axis=0, axis_index_groups=gr...  110 us
    all_to_all x1, blocking collectives, shards(): mine = lax.all_to_all(sent, 'chip', split_axis=0, concat_axis=0, tiled=True)  15.1 us
  transfers between devices with their start and end apart: 1, of which 1 were waited for; matrix products, arithmetic and copies ran while one was open for 0% of the time, Pallas kernels for 1%

profile of v7, /device:TPU:40, one launch (start us, length us, event | category | flops | bytes accessed | tf_op | source)
XLA Modules:
  0.0 133.9 jit_solution(3086741179038212709)
XLA Ops:
  0.0 2.0 %spread.1 = f32[256,128]{1,0:T(8,128)S(1)} custom-call(s32[1]{0:T(128)} %bitcast.owner_ref, s32[1]{0:T(128)} %bitcast.1.core_ref, f32[2,32,128]{2,1,0:T(8,128)} %bitcast.14, s32[32,32,128]{2,1,0:T(8,128)} %bitcast.16, bf16[2,128,128]{2,1,0:T(8,128)(2,1)} %constant.22.clone.along_ref), custom_call_target="tpu_custom_call" | custom-call | tf_op jit(solution)/shard_map/spread/pallas_call | solution.py:229
  2.0 0.0 copy-start.5
  2.0 74.4 %all_to_all.15.rows_ref = f32[32,8,128]{2,1,0:T(8,128)S(1)} all-to-all(f32[32,8,128]{2,1,0:T(8,128)S(1)} %bitcast.13), channel_id=1, replica_groups={{128,136,144,152,160,168,176,184,192,200,208,216,224,232,240,248,0,8,16..., dimensions={0} | all-to-all | bytes 262144 | tf_op jit(solution)/shard_map/all_to_all | solution.py:283
  76.4 0.0 copy-done.5
  76.4 0.0 copy-start
  76.4 0.0 copy-start.1
  76.5 0.0 copy-start.2
  76.5 0.0 copy-start.3
  76.5 0.0 copy-start.4
  76.5 15.1 %all_to_all.16.mine_ref = f32[4,40,8,128]{3,2,1,0:T(8,128)S(1)} all-to-all(f32[4,40,8,128]{3,2,1,0:T(8,128)S(1)} %fan.1), channel_id=1, replica_groups=mesh['pert'=2,'ga'=32,'chip'=4,'core'=2] {'chip'}, dimensions={0} | all-to-all | bytes 1310720 | tf_op jit(solution)/shard_map/all_to_all | solution.py:302
  91.6 1.9 %collective-permute-start = (f32[4,40,8,128]{3,2,1,0:T(8,128)S(1)}, f32[4,40,8,128]{3,2,1,0:T(8,128)S(1)}, u32[]{:S(2)}, u32[]{:S(2)}) collective-permute-start(f32[4,40,8,128]{3,2,1,0:T(8,128)S(1)} %all_to_all.16.mine_ref), channel_id=1, source_target_pairs={{0,1},{1,0},{2,3},{3,2},{4,5},{5,4},{6,7},{7,6},{8,9},{9,8},{10,11... | collective-permute-start | bytes 1966088 | tf_op jit(solution)/shard_map/ppermute | solution.py:288
  93.5 0.0 copy-done
  93.5 0.0 copy-done.1
  93.5 0.0 copy-done.2
  93.5 0.0 copy-done.3
  93.5 0.0 copy-done.4
  93.6 1.5 %apply.1 = (f32[256,128]{1,0:T(8,128)S(1)}, f32[8,128]{1,0:T(8,128)S(1)}) custom-call(f32[256,128]{1,0:T(8,128)S(1)} %bitcast.10, f32[128,4,128]{2,1,0:T(4,128)S(1)} %copy-done, bf16[2,128,256]{2,1,0:T(8,128)(2,1)S(1)} %copy-done.4, bf16[2,256,128]{2,1,0:T(8,128)(2,1)S(1)} %copy-done.3, bf16[2,128,256]{2,1,0:T(8,128)(2,1)S(1)} %copy-done.2, ...), custom_call_target="tpu_custom_call" | custom-call | tf_op jit(solution)/shard_map/apply/pallas_call | solution.py:251
  95.1 0.5 collective-permute-done.theirs_ref
  95.6 0.3 pair.1
  95.9 0.0 copy-start.6
  95.9 35.5 %all_to_all.17 = f32[32,1,1152]{2,1,0:T(1,128)S(1)} all-to-all(f32[32,1,1152]{2,1,0:T(1,128)S(1)} %bitcast.12), channel_id=1, replica_groups={{128,136,144,152,160,168,176,184,192,200,208,216,224,232,240,248,0,8,16..., dimensions={0} | all-to-all | bytes 294912 | tf_op jit(solution)/shard_map/all_to_all | solution.py:283
  131.4 0.0 copy-done.6
  131.4 2.6 %project.1 = f32[2,32,128]{2,1,0:T(8,128)} custom-call(s32[1]{0:T(128)} %bitcast.owner_ref, s32[1]{0:T(128)} %bitcast.1.core_ref, s32[8]{0:T(128)} %occupied_ref.1, f32[288,128]{1,0:T(8,128)S(1)} %bitcast.11, s32[32,32,128]{2,1,0:T(8,128)} %bitcast.17, bf16[2,64,256]{2,1,0:T(8,128)(2,1)S(1)} %copy-done.6, f32[4,40,8,128]{3,2,1,0:T(8,128)S(1)} %all_to_all.16.mine_ref, ...), custom_call_target="tpu_custom_call" | custom-call | tf_op jit(solution)/shard_map/project/pallas_call | solution.py:271
  (1 shorter events, 0.0 us)
Async XLA Ops:
  2.0 74.4 %copy-start.5 = (f32[2,1,4096]{2,1,0:T(1,128)S(1)}, f32[2,1,4096]{2,1,0:T(1,128)}, u32[]{:S(2)}) copy-start(f32[2,1,4096]{2,1,0:T(1,128)} %param.10) | copy-start | bytes 98308
  76.4 17.1 %copy-start = (f32[128,4,128]{2,1,0:T(4,128)S(1)}, f32[128,4,128]{2,1,0:T(4,128)}, u32[]{:S(2)}) copy-start(f32[128,4,128]{2,1,0:T(4,128)} %potential_ref.1) | copy-start | bytes 786436
  76.4 17.1 %copy-start.1 = (bf16[2,256,128]{2,1,0:T(8,128)(2,1)S(1)}, bf16[2,256,128]{2,1,0:T(8,128)(2,1)}, u32[]{:S(2)}) copy-start(bf16[2,256,128]{2,1,0:T(8,128)(2,1)} %constant.26.clone.back_z_ref) | copy-start | bytes 393220
  76.5 17.1 %copy-start.2 = (bf16[2,128,256]{2,1,0:T(8,128)(2,1)S(1)}, bf16[2,128,256]{2,1,0:T(8,128)(2,1)}, u32[]{:S(2)}) copy-start(bf16[2,128,256]{2,1,0:T(8,128)(2,1)} %constant.25.clone.back_x_ref) | copy-start | bytes 393220
  76.5 17.1 %copy-start.3 = (bf16[2,256,128]{2,1,0:T(8,128)(2,1)S(1)}, bf16[2,256,128]{2,1,0:T(8,128)(2,1)}, u32[]{:S(2)}) copy-start(bf16[2,256,128]{2,1,0:T(8,128)(2,1)} %constant.24.clone.x_ref) | copy-start | bytes 393220
  76.5 17.1 %copy-start.4 = (bf16[2,128,256]{2,1,0:T(8,128)(2,1)S(1)}, bf16[2,128,256]{2,1,0:T(8,128)(2,1)}, u32[]{:S(2)}) copy-start(bf16[2,128,256]{2,1,0:T(8,128)(2,1)} %constant.23.clone.z_ref) | copy-start | bytes 393220
  91.6 4.0 %collective-permute-start = (f32[4,40,8,128]{3,2,1,0:T(8,128)S(1)}, f32[4,40,8,128]{3,2,1,0:T(8,128)S(1)}, u32[]{:S(2)}, u32[]{:S(2)}) collective-permute-start(f32[4,40,8,128]{3,2,1,0:T(8,128)S(1)} %all_to_all.16.mine_ref), channel_id=1, source_target_pairs={{0,1},{1,0},{2,3},{3,2},{4,5},{5,4},{6,7},{7,6},{8,9},{9,8},{10,11... | collective-permute-start | bytes 1966088 | tf_op jit(solution)/shard_map/ppermute | solution.py:288
  95.9 35.5 %copy-start.6 = (bf16[2,64,256]{2,1,0:T(8,128)(2,1)S(1)}, bf16[2,64,256]{2,1,0:T(8,128)(2,1)}, u32[]{:S(2)}) copy-start(bf16[2,64,256]{2,1,0:T(8,128)(2,1)} %constant.27.clone.along_ref) | copy-start | bytes 196612

commit v8 on v7

--- a/solution.py
+++ b/solution.py
@@ -36,8 +36,16 @@
     return jnp.concatenate([-x[:, half:], x[:, :half]], axis=1)
 
 
+def listed(count, first):
+    return [(first + i) % count for i in range(count)]
+
+
 def ring(owners):
-    return [(i + owners // 2) % owners for i in range(owners)]
+    return listed(owners, owners - 1)
+
+
+def row(chips):
+    return listed(chips, chips // 2)
 
 
 def tables(size, owners):
@@ -200,7 +208,7 @@
     core = core_ref[0]
     for m in range(bands):
         held, first, source, from_core = (mine_ref, 0, m, core) if m < chips else (theirs_ref, 2 * chips, m - chips, 1 - core)
-        share = occupied_ref[2 * source + from_core].astype(jnp.float32) * (1.0 / coefs)
+        share = occupied_ref[2 * row(chips)[source] + from_core].astype(jnp.float32) * (1.0 / coefs)
         weight_real = sums[:, first + source : first + source + 1] * share
         weight_imag = sums[:, first + chips + source : first + chips + source + 1] * share
         basis = held[source, owners:].reshape(2, tall, lanes)
@@ -278,9 +286,8 @@
     )(owner, core, occupied, near(rows), points, near(table), near(mine), near(theirs))
 
 
-def exchanged(x, axis):
-    groups = [ring(lax.axis_size(axis))]
-    return lax.all_to_all(x, axis, split_axis=0, concat_axis=0, axis_index_groups=groups, tiled=True)
+def exchanged(x, axis, order):
+    return lax.all_to_all(x, axis, split_axis=0, concat_axis=0, axis_index_groups=[order], tiled=True)
 
 
 def along_ring(x, axis, step):
@@ -297,13 +304,13 @@
     points = miller.reshape(-1, block // size, size)
     rows = spread(owner, core, psi.reshape(2, -1, size), points, along_y, size, owners)
     group = rows.shape[0] // owners
-    rows = exchanged(rows.reshape(owners, group, size), "ga")
+    rows = exchanged(rows.reshape(owners, group, size), "ga", ring(owners))
     sent = fan(rows, psi.reshape(-1, group, size), chips)
-    mine = lax.all_to_all(sent, "chip", split_axis=0, concat_axis=0, tiled=True)
+    mine = exchanged(sent, "chip", row(chips))
     theirs = along_ring(mine, "core", 1)
     product, sums = apply(rows.reshape(-1, size), potential, along_z, along_x, back_x, back_z, mine, size, owners)
     sent = pair(theirs, product, sums, owners)
-    rows = exchanged(sent.reshape(owners, 1, -1), "ga").reshape(sent.shape)
+    rows = exchanged(sent.reshape(owners, 1, -1), "ga", ring(owners)).reshape(sent.shape)
     out = project(owner, core, occupied, rows, points, back_y, mine, theirs, size, owners, miller.shape[0])
     return out.reshape(2, 1, block)
 

time: 134 us -> 132 us (0.985)
  the two profiles are of different devices: /device:TPU:40 before, /device:TPU:96 now
where the time goes in v8:
time: 132 us; the launch traced here: 131 us
  blocking collectives  122 us (92%)
  Pallas kernels  6.39 us (5%)
  starting transfers between devices  1.94 us (1%)
    all_to_all x3, blocking collectives, exchanged(): lax.all_to_all(x, axis, split_axis=0, concat_axis=0, axis_index_groups=[o...  122 us
  transfers between devices with their start and end apart: 1, of which 1 were waited for; matrix products, arithmetic and copies ran while one was open for 0% of the time, Pallas kernels for 1%

profile of v8, /device:TPU:96, one launch (start us, length us, event | category | flops | bytes accessed | tf_op | source)
XLA Modules:
  0.0 131.3 jit_solution(3282214751762209178)
XLA Ops:
  0.0 2.0 %spread.1 = f32[256,128]{1,0:T(8,128)S(1)} custom-call(s32[1]{0:T(128)} %bitcast.owner_ref, s32[1]{0:T(128)} %bitcast.1.core_ref, f32[2,32,128]{2,1,0:T(8,128)} %bitcast.14, s32[32,32,128]{2,1,0:T(8,128)} %bitcast.16, bf16[2,128,128]{2,1,0:T(8,128)(2,1)} %constant.22.clone.along_ref), custom_call_target="tpu_custom_call" | custom-call | tf_op jit(solution)/shard_map/spread/pallas_call | solution.py:237
  2.0 0.0 copy-start.5
  2.0 73.3 %all_to_all.15.rows_ref = f32[32,8,128]{2,1,0:T(8,128)S(1)} all-to-all(f32[32,8,128]{2,1,0:T(8,128)S(1)} %bitcast.13), channel_id=1, replica_groups={{248,0,8,16,24,32,40,48,56,64,72,80,88,96,104,112,120,128,136,144,152,1..., dimensions={0} | all-to-all | bytes 262144 | tf_op jit(solution)/shard_map/all_to_all | solution.py:290
  75.3 0.0 copy-done.5
  75.4 0.0 copy-start
  75.4 0.0 copy-start.1
  75.4 0.0 copy-start.2
  75.4 0.0 copy-start.3
  75.4 0.0 copy-start.4
  75.4 12.6 %all_to_all.16.mine_ref = f32[4,40,8,128]{3,2,1,0:T(8,128)S(1)} all-to-all(f32[4,40,8,128]{3,2,1,0:T(8,128)S(1)} %fan.1), channel_id=1, replica_groups={{4,6,0,2},{5,7,1,3},{12,14,8,10},{13,15,9,11},{20,22,16,18},{21,23,17,1..., dimensions={0} | all-to-all | bytes 1310720 | tf_op jit(solution)/shard_map/all_to_all | solution.py:290
  88.0 1.9 %collective-permute-start = (f32[4,40,8,128]{3,2,1,0:T(8,128)S(1)}, f32[4,40,8,128]{3,2,1,0:T(8,128)S(1)}, u32[]{:S(2)}, u32[]{:S(2)}) collective-permute-start(f32[4,40,8,128]{3,2,1,0:T(8,128)S(1)} %all_to_all.16.mine_ref), channel_id=1, source_target_pairs={{0,1},{1,0},{2,3},{3,2},{4,5},{5,4},{6,7},{7,6},{8,9},{9,8},{10,11... | collective-permute-start | bytes 1966088 | tf_op jit(solution)/shard_map/ppermute | solution.py:295
  90.0 0.0 copy-done
  90.0 0.0 copy-done.1
  90.0 0.0 copy-done.2
  90.0 0.0 copy-done.3
  90.0 0.0 copy-done.4
  90.0 1.5 %apply.1 = (f32[256,128]{1,0:T(8,128)S(1)}, f32[8,128]{1,0:T(8,128)S(1)}) custom-call(f32[256,128]{1,0:T(8,128)S(1)} %bitcast.10, f32[128,4,128]{2,1,0:T(4,128)S(1)} %copy-done, bf16[2,128,256]{2,1,0:T(8,128)(2,1)S(1)} %copy-done.4, bf16[2,256,128]{2,1,0:T(8,128)(2,1)S(1)} %copy-done.3, bf16[2,128,256]{2,1,0:T(8,128)(2,1)S(1)} %copy-done.2, ...), custom_call_target="tpu_custom_call" | custom-call | tf_op jit(solution)/shard_map/apply/pallas_call | solution.py:259
  91.5 0.5 collective-permute-done.theirs_ref
  92.0 0.3 pair.1
  92.3 0.0 copy-start.6
  92.4 36.3 %all_to_all.17 = f32[32,1,1152]{2,1,0:T(1,128)S(1)} all-to-all(f32[32,1,1152]{2,1,0:T(1,128)S(1)} %bitcast.12), channel_id=1, replica_groups={{248,0,8,16,24,32,40,48,56,64,72,80,88,96,104,112,120,128,136,144,152,1..., dimensions={0} | all-to-all | bytes 294912 | tf_op jit(solution)/shard_map/all_to_all | solution.py:290
  128.7 0.0 copy-done.6
  128.7 2.6 %project.1 = f32[2,32,128]{2,1,0:T(8,128)} custom-call(s32[1]{0:T(128)} %bitcast.owner_ref, s32[1]{0:T(128)} %bitcast.1.core_ref, s32[8]{0:T(128)} %occupied_ref.1, f32[288,128]{1,0:T(8,128)S(1)} %bitcast.11, s32[32,32,128]{2,1,0:T(8,128)} %bitcast.17, bf16[2,64,256]{2,1,0:T(8,128)(2,1)S(1)} %copy-done.6, f32[4,40,8,128]{3,2,1,0:T(8,128)S(1)} %all_to_all.16.mine_ref, ...), custom_call_target="tpu_custom_call" | custom-call | tf_op jit(solution)/shard_map/project/pallas_call | solution.py:279
  (1 shorter events, 0.0 us)
Async XLA Ops:
  2.0 73.3 %copy-start.5 = (f32[2,1,4096]{2,1,0:T(1,128)S(1)}, f32[2,1,4096]{2,1,0:T(1,128)}, u32[]{:S(2)}) copy-start(f32[2,1,4096]{2,1,0:T(1,128)} %param.10) | copy-start | bytes 98308
  75.4 14.6 %copy-start = (f32[128,4,128]{2,1,0:T(4,128)S(1)}, f32[128,4,128]{2,1,0:T(4,128)}, u32[]{:S(2)}) copy-start(f32[128,4,128]{2,1,0:T(4,128)} %potential_ref.1) | copy-start | bytes 786436
  75.4 14.6 %copy-start.1 = (bf16[2,256,128]{2,1,0:T(8,128)(2,1)S(1)}, bf16[2,256,128]{2,1,0:T(8,128)(2,1)}, u32[]{:S(2)}) copy-start(bf16[2,256,128]{2,1,0:T(8,128)(2,1)} %constant.26.clone.back_z_ref) | copy-start | bytes 393220
  75.4 14.6 %copy-start.2 = (bf16[2,128,256]{2,1,0:T(8,128)(2,1)S(1)}, bf16[2,128,256]{2,1,0:T(8,128)(2,1)}, u32[]{:S(2)}) copy-start(bf16[2,128,256]{2,1,0:T(8,128)(2,1)} %constant.25.clone.back_x_ref) | copy-start | bytes 393220
  75.4 14.6 %copy-start.3 = (bf16[2,256,128]{2,1,0:T(8,128)(2,1)S(1)}, bf16[2,256,128]{2,1,0:T(8,128)(2,1)}, u32[]{:S(2)}) copy-start(bf16[2,256,128]{2,1,0:T(8,128)(2,1)} %constant.24.clone.x_ref) | copy-start | bytes 393220
  75.4 14.6 %copy-start.4 = (bf16[2,128,256]{2,1,0:T(8,128)(2,1)S(1)}, bf16[2,128,256]{2,1,0:T(8,128)(2,1)}, u32[]{:S(2)}) copy-start(bf16[2,128,256]{2,1,0:T(8,128)(2,1)} %constant.23.clone.z_ref) | copy-start | bytes 393220
  88.0 4.0 %collective-permute-start = (f32[4,40,8,128]{3,2,1,0:T(8,128)S(1)}, f32[4,40,8,128]{3,2,1,0:T(8,128)S(1)}, u32[]{:S(2)}, u32[]{:S(2)}) collective-permute-start(f32[4,40,8,128]{3,2,1,0:T(8,128)S(1)} %all_to_all.16.mine_ref), channel_id=1, source_target_pairs={{0,1},{1,0},{2,3},{3,2},{4,5},{5,4},{6,7},{7,6},{8,9},{9,8},{10,11... | collective-permute-start | bytes 1966088 | tf_op jit(solution)/shard_map/ppermute | solution.py:295
  92.3 36.4 %copy-start.6 = (bf16[2,64,256]{2,1,0:T(8,128)(2,1)S(1)}, bf16[2,64,256]{2,1,0:T(8,128)(2,1)}, u32[]{:S(2)}) copy-start(bf16[2,64,256]{2,1,0:T(8,128)(2,1)} %constant.27.clone.along_ref) | copy-start | bytes 196612

commit v9 on v8

--- a/solution.py
+++ b/solution.py
@@ -59,7 +59,7 @@
     planes = [part.reshape(size, -1, owners)[:, :, order].reshape(size, -1) for part in (cosine, sine)]
     along_x = np.block([[planes[0], -planes[1]], [planes[1], planes[0]]])
     back = [part.transpose(2, 1, 0).reshape(size // 2, size) for part in by_owner]
-    back_y = np.concatenate([back[0], -back[1]], axis=1)
+    back_y = np.concatenate(back, axis=0)
 
     def both(table):
         table = np.asarray(table, np.float32)
@@ -91,7 +91,7 @@
 
 
 def spread_kernel(
-    owner_ref, core_ref, psi_ref, points_ref, along_ref, out_ref, psi_held, points_held, along_held, flat_ref, sems, *, size, owners
+    owner_ref, core_ref, psi_ref, points_ref, along_ref, out_ref, at_ref, psi_held, points_held, along_held, flat_ref, sems, *, size, owners
 ):
     del core_ref
     copies = [
@@ -104,20 +104,20 @@
     half = size // 2
     lines = half * half // owners
     copies[0].wait()
-    line, column = places(points_held[...], size, owners)
-    flat_ref[0], flat_ref[1] = line.astype(jnp.float32), column.astype(jnp.float32)
+    for i, x in enumerate(places(points_held[...], size, owners)):
+        at_ref[i] = x.astype(jnp.float32)
     copies[1].wait()
     for part in range(2):
         for which, x in enumerate(halves(psi_held[part])):
-            flat_ref[2 + 2 * which + part] = x.astype(jnp.float32)
+            flat_ref[2 * which + part] = x.astype(jnp.float32)
     tall, lanes = points_held.shape
     every_line, every_column = numbered(lines, lanes), numbered(half, lanes)
     one, zero = jnp.ones((), jnp.bfloat16), jnp.zeros((), jnp.bfloat16)
     at_line, values = [], []
     for r in range(tall):
-        at_line.append(jnp.where(every_line == copied_down(flat_ref[0, r : r + 1, :], lines), one, zero))
-        at_column = every_column == copied_down(flat_ref[1, r : r + 1, :], half)
-        parts = [jnp.where(at_column, copied_down(flat_ref[i, r : r + 1, :], half), zero) for i in range(2, 6)]
+        at_line.append(jnp.where(every_line == copied_down(at_ref[0, r : r + 1, :], lines), one, zero))
+        at_column = every_column == copied_down(at_ref[1, r : r + 1, :], half)
+        parts = [jnp.where(at_column, copied_down(flat_ref[i, r : r + 1, :], half), zero) for i in range(4)]
         values.append(jnp.concatenate(parts, axis=0))
     at_line, values = jnp.concatenate(at_line, axis=1), jnp.concatenate(values, axis=1)
     total = lax.dot_general(at_line, values, (((1,), (1,)), ((), ())), preferred_element_type=jnp.float32)
@@ -181,11 +181,7 @@
     out_ref[pl.ds(group, owners, stride=group + 1), :] = jnp.broadcast_to(row, (owners, lanes))
 
 
-def project_kernel(
-    owner_ref, core_ref, occupied_ref, rows_ref, points_ref, along_ref, mine_ref, theirs_ref, out_ref, held_ref, flat_ref, sem, *, size, owners, coefs
-):
-    copy = own_points(owner_ref, points_ref, held_ref, sem)
-    copy.start()
+def project_kernel(core_ref, occupied_ref, rows_ref, at_ref, along_ref, mine_ref, theirs_ref, out_ref, *, size, owners, coefs):
     chips = mine_ref.shape[0]
     bands = 2 * chips
     half = size // 2
@@ -195,14 +191,13 @@
     fields = []
     for t in range(planes):
         rows = [rows_ref[pl.ds(r, owners, stride=group), :] for r in range(t, group - 1, planes)]
-        rows = jnp.concatenate(rows, axis=0)
-        fields.append(jnp.concatenate([rows, turned(rows)], axis=0))
-    lines = dot(along_ref[...], halves(jnp.concatenate(fields, axis=1)))
-    lines = jnp.concatenate([lines[:, t * size : (t + 1) * size].T for t in range(planes)], axis=1)
+        fields.append(jnp.concatenate(rows, axis=0))
+    both = dot(along_ref[...], halves(jnp.concatenate(fields, axis=1)))
+    by_cosine, by_sine = (
+        jnp.concatenate([x[:, t * size : (t + 1) * size] for t in range(planes)], axis=0).T for x in (both[:half], both[half:])
+    )
+    lines = jnp.concatenate([by_cosine[:half] + by_sine[half:], by_cosine[half:] - by_sine[:half]], axis=0)
     lines = jnp.concatenate(halves(lines), axis=1)
-    copy.wait()
-    line, column = places(held_ref[...], size, owners)
-    flat_ref[0], flat_ref[1] = line.astype(jnp.float32), column.astype(jnp.float32)
     tall, lanes = out_ref.shape[1:]
     taken = [jnp.zeros((tall, lanes), jnp.float32) for _ in range(2)]
     core = core_ref[0]
@@ -218,11 +213,11 @@
     every_column = lax.broadcasted_iota(jnp.int32, (half, lanes), 0).astype(jnp.float32)
     one, zero = jnp.ones((), jnp.bfloat16), jnp.zeros((), jnp.bfloat16)
     for r in range(0, tall, 2):
-        at_line = [jnp.where(every_line == copied_down(flat_ref[0, i : i + 1, :], planes * half), one, zero) for i in (r, r + 1)]
+        at_line = [jnp.where(every_line == copied_down(at_ref[0, i : i + 1, :], planes * half), one, zero) for i in (r, r + 1)]
         at_line = jnp.concatenate(at_line, axis=1)
         found = jnp.dot(lines, jnp.concatenate([at_line, at_line], axis=0), preferred_element_type=jnp.float32)
         for i in range(2):
-            at_column = every_column == flat_ref[1, r + i : r + i + 1, :]
+            at_column = every_column == at_ref[1, r + i : r + i + 1, :]
             for p in range(2):
                 applied = jnp.where(at_column, found[p * half : (p + 1) * half, i * lanes : (i + 1) * lanes], 0.0)
                 out_ref[p, r + i : r + i + 1, :] = jnp.sum(applied, axis=0, keepdims=True) - taken[p][r + i : r + i + 1]
@@ -236,13 +231,13 @@
 def spread(owner, core, psi, points, table, size, owners):
     return pl.pallas_call(
         functools.partial(spread_kernel, size=size, owners=owners),
-        out_shape=made((size * (size // (2 * owners)), size)),
+        out_shape=(made((size * (size // (2 * owners)), size)), made((2, *points.shape[1:]))),
         in_specs=[SCALARS, SCALARS, FAR, FAR, FAR],
         scratch_shapes=[
             pltpu.VMEM(psi.shape, psi.dtype),
             pltpu.VMEM(points.shape[1:], points.dtype),
             pltpu.VMEM(table.shape, table.dtype),
-            pltpu.VMEM((6, *points.shape[1:]), jnp.float32),
+            pltpu.VMEM((4, *points.shape[1:]), jnp.float32),
             pltpu.SemaphoreType.DMA((3,)),
         ],
         interpret=INTERPRET,
@@ -274,16 +269,14 @@
     )(*map(near, (theirs, product, sums)))
 
 
-def project(owner, core, occupied, rows, points, table, mine, theirs, size, owners, coefs):
-    tall, lanes = points.shape[1:]
+def project(core, occupied, rows, at, table, mine, theirs, size, owners, coefs):
     return pl.pallas_call(
         functools.partial(project_kernel, size=size, owners=owners, coefs=coefs),
-        out_shape=jax.ShapeDtypeStruct((2, tall, lanes), jnp.float32),
-        in_specs=[SCALARS, SCALARS, SCALARS, WHOLE, FAR, WHOLE, WHOLE, WHOLE],
-        scratch_shapes=[pltpu.VMEM((tall, lanes), points.dtype), pltpu.VMEM((2, tall, lanes), jnp.float32), pltpu.SemaphoreType.DMA],
+        out_shape=jax.ShapeDtypeStruct(at.shape, jnp.float32),
+        in_specs=[SCALARS, SCALARS] + [WHOLE] * 5,
         interpret=INTERPRET,
         name="project",
-    )(owner, core, occupied, near(rows), points, near(table), near(mine), near(theirs))
+    )(core, occupied, *map(near, (rows, at, table, mine, theirs)))
 
 
 def exchanged(x, axis, order):
@@ -302,7 +295,7 @@
     along_y, along_z, along_x, back_x, back_z, back_y = tables(size, owners)
     owner, core = (lax.axis_index(axis).reshape(1) for axis in ("ga", "core"))
     points = miller.reshape(-1, block // size, size)
-    rows = spread(owner, core, psi.reshape(2, -1, size), points, along_y, size, owners)
+    rows, at = spread(owner, core, psi.reshape(2, -1, size), points, along_y, size, owners)
     group = rows.shape[0] // owners
     rows = exchanged(rows.reshape(owners, group, size), "ga", ring(owners))
     sent = fan(rows, psi.reshape(-1, group, size), chips)
@@ -311,7 +304,7 @@
     product, sums = apply(rows.reshape(-1, size), potential, along_z, along_x, back_x, back_z, mine, size, owners)
     sent = pair(theirs, product, sums, owners)
     rows = exchanged(sent.reshape(owners, 1, -1), "ga", ring(owners)).reshape(sent.shape)
-    out = project(owner, core, occupied, rows, points, back_y, mine, theirs, size, owners, miller.shape[0])
+    out = project(core, occupied, rows, at, back_y, mine, theirs, size, owners, miller.shape[0])
     return out.reshape(2, 1, block)
 
 

time: 132 us -> 131 us (level)
  no operation moved by 1% of the time
where the time goes in v9:
time: 131 us
  blocking collectives  122 us (93%)
  Pallas kernels  5.9 us (5%)
  starting transfers between devices  1.94 us (1%)
    all_to_all x3, blocking collectives, exchanged(): lax.all_to_all(x, axis, split_axis=0, concat_axis=0, axis_index_groups=[o...  122 us
  transfers between devices with their start and end apart: 1, of which 1 were waited for; matrix products, arithmetic and copies ran while one was open for 0% of the time, Pallas kernels for 1%

profile of v9, /device:TPU:96, one launch (start us, length us, event | category | flops | bytes accessed | tf_op | source)
XLA Modules:
  0.0 130.8 jit_solution(16969323375039451360)
XLA Ops:
  0.0 2.0 %spread.1 = (f32[256,128]{1,0:T(8,128)S(1)}, f32[2,32,128]{2,1,0:T(8,128)S(1)}) custom-call(s32[1]{0:T(128)} %bitcast.1.owner_ref, s32[1]{0:T(128)} %bitcast.core_ref, f32[2,32,128]{2,1,0:T(8,128)} %bitcast.13, s32[32,32,128]{2,1,0:T(8,128)} %bitcast.16, bf16[2,128,128]{2,1,0:T(8,128)(2,1)} %constant.22.clone.along_ref), custom_call_target="tpu_custom_call" | custom-call | tf_op jit(solution)/shard_map/spread/pallas_call | solution.py:232
  2.0 0.0 copy-start.5
  2.0 73.3 %all_to_all.15.rows_ref = f32[32,8,128]{2,1,0:T(8,128)S(1)} all-to-all(f32[32,8,128]{2,1,0:T(8,128)S(1)} %bitcast.15), channel_id=1, replica_groups={{248,0,8,16,24,32,40,48,56,64,72,80,88,96,104,112,120,128,136,144,152,1..., dimensions={0} | all-to-all | bytes 262144 | tf_op jit(solution)/shard_map/all_to_all | solution.py:283
  75.3 0.0 copy-done.5
  75.3 0.0 copy-start
  75.4 0.0 copy-start.1
  75.4 0.0 copy-start.2
  75.4 0.0 copy-start.3
  75.4 0.0 copy-start.4
  75.4 12.6 %all_to_all.16.mine_ref = f32[4,40,8,128]{3,2,1,0:T(8,128)S(1)} all-to-all(f32[4,40,8,128]{3,2,1,0:T(8,128)S(1)} %fan.1), channel_id=1, replica_groups={{4,6,0,2},{5,7,1,3},{12,14,8,10},{13,15,9,11},{20,22,16,18},{21,23,17,1..., dimensions={0} | all-to-all | bytes 1310720 | tf_op jit(solution)/shard_map/all_to_all | solution.py:283
  88.0 1.9 %collective-permute-start = (f32[4,40,8,128]{3,2,1,0:T(8,128)S(1)}, f32[4,40,8,128]{3,2,1,0:T(8,128)S(1)}, u32[]{:S(2)}, u32[]{:S(2)}) collective-permute-start(f32[4,40,8,128]{3,2,1,0:T(8,128)S(1)} %all_to_all.16.mine_ref), channel_id=1, source_target_pairs={{0,1},{1,0},{2,3},{3,2},{4,5},{5,4},{6,7},{7,6},{8,9},{9,8},{10,11... | collective-permute-start | bytes 1966088 | tf_op jit(solution)/shard_map/ppermute | solution.py:288
  90.0 0.0 copy-done
  90.0 0.0 copy-done.1
  90.0 0.0 copy-done.2
  90.0 0.0 copy-done.3
  90.0 0.0 copy-done.4
  90.0 1.5 %apply.1 = (f32[256,128]{1,0:T(8,128)S(1)}, f32[8,128]{1,0:T(8,128)S(1)}) custom-call(f32[256,128]{1,0:T(8,128)S(1)} %bitcast.10, f32[128,4,128]{2,1,0:T(4,128)S(1)} %copy-done, bf16[2,128,256]{2,1,0:T(8,128)(2,1)S(1)} %copy-done.4, bf16[2,256,128]{2,1,0:T(8,128)(2,1)S(1)} %copy-done.3, bf16[2,128,256]{2,1,0:T(8,128)(2,1)S(1)} %copy-done.2, ...), custom_call_target="tpu_custom_call" | custom-call | tf_op jit(solution)/shard_map/apply/pallas_call | solution.py:254
  91.5 0.5 collective-permute-done.theirs_ref
  92.0 0.3 pair.1
  92.3 0.0 copy-start.6
  92.3 36.3 %all_to_all.17 = f32[32,1,1152]{2,1,0:T(1,128)S(1)} all-to-all(f32[32,1,1152]{2,1,0:T(1,128)S(1)} %bitcast.11), channel_id=1, replica_groups={{248,0,8,16,24,32,40,48,56,64,72,80,88,96,104,112,120,128,136,144,152,1..., dimensions={0} | all-to-all | bytes 294912 | tf_op jit(solution)/shard_map/all_to_all | solution.py:283
  128.7 0.0 copy-done.6
  128.7 2.1 %project.1 = f32[2,32,128]{2,1,0:T(8,128)} custom-call(s32[1]{0:T(128)} %bitcast.core_ref, s32[8]{0:T(128)} %occupied_ref.1, f32[288,128]{1,0:T(8,128)S(1)} %bitcast.12, f32[2,32,128]{2,1,0:T(8,128)S(1)} %get-tuple-element.12.at_ref, bf16[2,128,128]{2,1,0:T(8,128)(2,1)S(1)} %copy-done.6, f32[4,40,8,128]{3,2,1,0:T(8,128)S(1)} %all_to_all.16.mine_ref, ...), custom_call_target="tpu_custom_call" | custom-call | tf_op jit(solution)/shard_map/project/pallas_call | solution.py:273
  (1 shorter events, 0.0 us)
Async XLA Ops:
  2.0 73.3 %copy-start.5 = (f32[2,1,4096]{2,1,0:T(1,128)S(1)}, f32[2,1,4096]{2,1,0:T(1,128)}, u32[]{:S(2)}) copy-start(f32[2,1,4096]{2,1,0:T(1,128)} %param.10) | copy-start | bytes 98308
  75.3 14.6 %copy-start = (f32[128,4,128]{2,1,0:T(4,128)S(1)}, f32[128,4,128]{2,1,0:T(4,128)}, u32[]{:S(2)}) copy-start(f32[128,4,128]{2,1,0:T(4,128)} %potential_ref.1) | copy-start | bytes 786436
  75.4 14.6 %copy-start.1 = (bf16[2,256,128]{2,1,0:T(8,128)(2,1)S(1)}, bf16[2,256,128]{2,1,0:T(8,128)(2,1)}, u32[]{:S(2)}) copy-start(bf16[2,256,128]{2,1,0:T(8,128)(2,1)} %constant.26.clone.back_z_ref) | copy-start | bytes 393220
  75.4 14.6 %copy-start.2 = (bf16[2,128,256]{2,1,0:T(8,128)(2,1)S(1)}, bf16[2,128,256]{2,1,0:T(8,128)(2,1)}, u32[]{:S(2)}) copy-start(bf16[2,128,256]{2,1,0:T(8,128)(2,1)} %constant.25.clone.back_x_ref) | copy-start | bytes 393220
  75.4 14.6 %copy-start.3 = (bf16[2,256,128]{2,1,0:T(8,128)(2,1)S(1)}, bf16[2,256,128]{2,1,0:T(8,128)(2,1)}, u32[]{:S(2)}) copy-start(bf16[2,256,128]{2,1,0:T(8,128)(2,1)} %constant.24.clone.x_ref) | copy-start | bytes 393220
  75.4 14.6 %copy-start.4 = (bf16[2,128,256]{2,1,0:T(8,128)(2,1)S(1)}, bf16[2,128,256]{2,1,0:T(8,128)(2,1)}, u32[]{:S(2)}) copy-start(bf16[2,128,256]{2,1,0:T(8,128)(2,1)} %constant.23.clone.z_ref) | copy-start | bytes 393220
  88.0 4.0 %collective-permute-start = (f32[4,40,8,128]{3,2,1,0:T(8,128)S(1)}, f32[4,40,8,128]{3,2,1,0:T(8,128)S(1)}, u32[]{:S(2)}, u32[]{:S(2)}) collective-permute-start(f32[4,40,8,128]{3,2,1,0:T(8,128)S(1)} %all_to_all.16.mine_ref), channel_id=1, source_target_pairs={{0,1},{1,0},{2,3},{3,2},{4,5},{5,4},{6,7},{7,6},{8,9},{9,8},{10,11... | collective-permute-start | bytes 1966088 | tf_op jit(solution)/shard_map/ppermute | solution.py:288
  92.3 36.4 %copy-start.6 = (bf16[2,128,128]{2,1,0:T(8,128)(2,1)S(1)}, bf16[2,128,128]{2,1,0:T(8,128)(2,1)}, u32[]{:S(2)}) copy-start(bf16[2,128,128]{2,1,0:T(8,128)(2,1)} %constant.27.clone.along_ref) | copy-start | bytes 196612

commit v10 on v9

--- a/solution.py
+++ b/solution.py
@@ -41,7 +41,7 @@
 
 
 def ring(owners):
-    return listed(owners, owners - 1)
+    return listed(owners, owners * 7 // 8)
 
 
 def row(chips):

time: 131 us -> 131 us (level)
  the two profiles are of different devices: /device:TPU:96 before, /device:TPU:40 now
where the time goes in v10:
time: 131 us
  blocking collectives  122 us (93%)
  Pallas kernels  5.91 us (5%)
  starting transfers between devices  1.94 us (1%)
    all_to_all x3, blocking collectives, exchanged(): lax.all_to_all(x, axis, split_axis=0, concat_axis=0, axis_index_groups=[o...  122 us
  transfers between devices with their start and end apart: 1, of which 1 were waited for; matrix products, arithmetic and copies ran while one was open for 0% of the time, Pallas kernels for 1%

profile of v10, /device:TPU:40, one launch (start us, length us, event | category | flops | bytes accessed | tf_op | source)
XLA Modules:
  0.0 130.8 jit_solution(564427040348457642)
XLA Ops:
  0.0 2.0 %spread.1 = (f32[256,128]{1,0:T(8,128)S(1)}, f32[2,32,128]{2,1,0:T(8,128)S(1)}) custom-call(s32[1]{0:T(128)} %bitcast.1.owner_ref, s32[1]{0:T(128)} %bitcast.core_ref, f32[2,32,128]{2,1,0:T(8,128)} %bitcast.13, s32[32,32,128]{2,1,0:T(8,128)} %bitcast.16, bf16[2,128,128]{2,1,0:T(8,128)(2,1)} %constant.22.clone.along_ref), custom_call_target="tpu_custom_call" | custom-call | tf_op jit(solution)/shard_map/spread/pallas_call | solution.py:232
  2.0 0.0 copy-start.5
  2.0 73.1 %all_to_all.15.rows_ref = f32[32,8,128]{2,1,0:T(8,128)S(1)} all-to-all(f32[32,8,128]{2,1,0:T(8,128)S(1)} %bitcast.15), channel_id=1, replica_groups={{224,232,240,248,0,8,16,24,32,40,48,56,64,72,80,88,96,104,112,120,128,1..., dimensions={0} | all-to-all | bytes 262144 | tf_op jit(solution)/shard_map/all_to_all | solution.py:283
  75.1 0.0 copy-done.5
  75.2 0.0 copy-start
  75.2 0.0 copy-start.1
  75.2 0.0 copy-start.2
  75.2 0.0 copy-start.3
  75.2 0.0 copy-start.4
  75.2 11.5 %all_to_all.16.mine_ref = f32[4,40,8,128]{3,2,1,0:T(8,128)S(1)} all-to-all(f32[4,40,8,128]{3,2,1,0:T(8,128)S(1)} %fan.1), channel_id=1, replica_groups={{4,6,0,2},{5,7,1,3},{12,14,8,10},{13,15,9,11},{20,22,16,18},{21,23,17,1..., dimensions={0} | all-to-all | bytes 1310720 | tf_op jit(solution)/shard_map/all_to_all | solution.py:283
  86.7 1.9 %collective-permute-start = (f32[4,40,8,128]{3,2,1,0:T(8,128)S(1)}, f32[4,40,8,128]{3,2,1,0:T(8,128)S(1)}, u32[]{:S(2)}, u32[]{:S(2)}) collective-permute-start(f32[4,40,8,128]{3,2,1,0:T(8,128)S(1)} %all_to_all.16.mine_ref), channel_id=1, source_target_pairs={{0,1},{1,0},{2,3},{3,2},{4,5},{5,4},{6,7},{7,6},{8,9},{9,8},{10,11... | collective-permute-start | bytes 1966088 | tf_op jit(solution)/shard_map/ppermute | solution.py:288
  88.7 0.0 copy-done
  88.7 0.0 copy-done.1
  88.7 0.0 copy-done.2
  88.7 0.0 copy-done.3
  88.7 0.0 copy-done.4
  88.7 1.5 %apply.1 = (f32[256,128]{1,0:T(8,128)S(1)}, f32[8,128]{1,0:T(8,128)S(1)}) custom-call(f32[256,128]{1,0:T(8,128)S(1)} %bitcast.10, f32[128,4,128]{2,1,0:T(4,128)S(1)} %copy-done, bf16[2,128,256]{2,1,0:T(8,128)(2,1)S(1)} %copy-done.4, bf16[2,256,128]{2,1,0:T(8,128)(2,1)S(1)} %copy-done.3, bf16[2,128,256]{2,1,0:T(8,128)(2,1)S(1)} %copy-done.2, ...), custom_call_target="tpu_custom_call" | custom-call | tf_op jit(solution)/shard_map/apply/pallas_call | solution.py:254
  90.2 0.5 collective-permute-done.theirs_ref
  90.7 0.3 pair.1
  91.0 0.0 copy-start.6
  91.0 37.7 %all_to_all.17 = f32[32,1,1152]{2,1,0:T(1,128)S(1)} all-to-all(f32[32,1,1152]{2,1,0:T(1,128)S(1)} %bitcast.11), channel_id=1, replica_groups={{224,232,240,248,0,8,16,24,32,40,48,56,64,72,80,88,96,104,112,120,128,1..., dimensions={0} | all-to-all | bytes 294912 | tf_op jit(solution)/shard_map/all_to_all | solution.py:283
  128.7 0.0 copy-done.6
  128.7 2.1 %project.1 = f32[2,32,128]{2,1,0:T(8,128)} custom-call(s32[1]{0:T(128)} %bitcast.core_ref, s32[8]{0:T(128)} %occupied_ref.1, f32[288,128]{1,0:T(8,128)S(1)} %bitcast.12, f32[2,32,128]{2,1,0:T(8,128)S(1)} %get-tuple-element.12.at_ref, bf16[2,128,128]{2,1,0:T(8,128)(2,1)S(1)} %copy-done.6, f32[4,40,8,128]{3,2,1,0:T(8,128)S(1)} %all_to_all.16.mine_ref, ...), custom_call_target="tpu_custom_call" | custom-call | tf_op jit(solution)/shard_map/project/pallas_call | solution.py:273
  (1 shorter events, 0.0 us)
Async XLA Ops:
  2.0 73.1 %copy-start.5 = (f32[2,1,4096]{2,1,0:T(1,128)S(1)}, f32[2,1,4096]{2,1,0:T(1,128)}, u32[]{:S(2)}) copy-start(f32[2,1,4096]{2,1,0:T(1,128)} %param.10) | copy-start | bytes 98308
  75.2 13.5 %copy-start = (f32[128,4,128]{2,1,0:T(4,128)S(1)}, f32[128,4,128]{2,1,0:T(4,128)}, u32[]{:S(2)}) copy-start(f32[128,4,128]{2,1,0:T(4,128)} %potential_ref.1) | copy-start | bytes 786436
  75.2 13.5 %copy-start.1 = (bf16[2,256,128]{2,1,0:T(8,128)(2,1)S(1)}, bf16[2,256,128]{2,1,0:T(8,128)(2,1)}, u32[]{:S(2)}) copy-start(bf16[2,256,128]{2,1,0:T(8,128)(2,1)} %constant.26.clone.back_z_ref) | copy-start | bytes 393220
  75.2 13.5 %copy-start.2 = (bf16[2,128,256]{2,1,0:T(8,128)(2,1)S(1)}, bf16[2,128,256]{2,1,0:T(8,128)(2,1)}, u32[]{:S(2)}) copy-start(bf16[2,128,256]{2,1,0:T(8,128)(2,1)} %constant.25.clone.back_x_ref) | copy-start | bytes 393220
  75.2 13.5 %copy-start.3 = (bf16[2,256,128]{2,1,0:T(8,128)(2,1)S(1)}, bf16[2,256,128]{2,1,0:T(8,128)(2,1)}, u32[]{:S(2)}) copy-start(bf16[2,256,128]{2,1,0:T(8,128)(2,1)} %constant.24.clone.x_ref) | copy-start | bytes 393220
  75.2 13.5 %copy-start.4 = (bf16[2,128,256]{2,1,0:T(8,128)(2,1)S(1)}, bf16[2,128,256]{2,1,0:T(8,128)(2,1)}, u32[]{:S(2)}) copy-start(bf16[2,128,256]{2,1,0:T(8,128)(2,1)} %constant.23.clone.z_ref) | copy-start | bytes 393220
  86.7 4.0 %collective-permute-start = (f32[4,40,8,128]{3,2,1,0:T(8,128)S(1)}, f32[4,40,8,128]{3,2,1,0:T(8,128)S(1)}, u32[]{:S(2)}, u32[]{:S(2)}) collective-permute-start(f32[4,40,8,128]{3,2,1,0:T(8,128)S(1)} %all_to_all.16.mine_ref), channel_id=1, source_target_pairs={{0,1},{1,0},{2,3},{3,2},{4,5},{5,4},{6,7},{7,6},{8,9},{9,8},{10,11... | collective-permute-start | bytes 1966088 | tf_op jit(solution)/shard_map/ppermute | solution.py:288
  91.0 37.7 %copy-start.6 = (bf16[2,128,128]{2,1,0:T(8,128)(2,1)S(1)}, bf16[2,128,128]{2,1,0:T(8,128)(2,1)}, u32[]{:S(2)}) copy-start(bf16[2,128,128]{2,1,0:T(8,128)(2,1)} %constant.27.clone.along_ref) | copy-start | bytes 196612
